TPU v7x, 512 devices: a whole 4x8x8 slice. The times are simulated.
512 devices in a mesh: grp: 2 (over core), gx: 16 (over x, z_lo), gy: 16 (over z_hi, y).
Axes of the slice: x: 4, y: 8, z: 8 (z_hi: 2, z_lo: 4; z = z_hi * 4 + z_lo), core: 2. Of those that a mesh axis runs over, the one named last changes fastest.
Arguments:
- coarse_density: float32 [512, 512, 512], P('gx', ('grp', 'gy')), may hold values from -3 to 3
- fine_density: float32 [128, 512, 256], P('gx', 'gy', 'grp'), may hold values from -96 to 96
- fine_start: float32 [128, 512, 256], P('gx', 'gy', 'grp'), may hold values from -6 to 6
- anchor: int32 [3], replicated, may hold values from 1 to 383
Outputs:
- coarse_potential: float32 [512, 512, 512], P('gx', ('grp', 'gy'))
- fine_potential: float32 [128, 512, 256], P('gx', 'gy', 'grp')
Inputs may be any that keep to these rules, and one draw needn't show every extreme that they name: Along every dimension d the coarse cells anchor[d] - 1 up to anchor[d] + (fine cells along d) / 4 lie inside the coarse grid.
All inputs are finite; a program needn't handle non-finite values.
Results may differ from a plain program's by a relative error of at most 0.00015.
Values sent between devices are 32-bit elements; how exact they have to be, the bound alone decides.
A program may use at most 64 MiB of HBM per device.

v0:
```python
import math

import jax
import jax.numpy as jnp
from jax import lax
from jax.sharding import PartitionSpec as P

RATIO = 4
SWEEPS = 8


highest = lax.Precision.HIGHEST


def with_halo(block, sides, width):
    for axis, dim in sides:
        count = lax.axis_size(axis)
        forward = [(i, i + 1) for i in range(count - 1)]
        backward = [(target, source) for source, target in forward]
        low = lax.ppermute(
            lax.slice_in_dim(block, block.shape[dim] - width, None, axis=dim), axis, forward
        )
        high = lax.ppermute(lax.slice_in_dim(block, 0, width, axis=dim), axis, backward)
        block = jnp.concatenate([low, block, high], axis=dim)
    return block


def sine_table(amount):
    indices = jnp.arange(amount, dtype=jnp.int32) + 1
    product = indices[:, None] * indices[None, :] % (2 * (amount + 1))
    angles = product.astype(jnp.float32) * (math.pi / (amount + 1))
    return math.sqrt(2.0 / (amount + 1)) * jnp.sin(angles)


def eigen_values(indices, amount):
    angles = (indices + 1).astype(jnp.float32) * (math.pi / (2 * (amount + 1)))
    return -4.0 * jnp.square(jnp.sin(angles))


def interpolation(fine_index, cell_count):
    scaled = 2 * fine_index + 1 + RATIO
    bottom = scaled // (2 * RATIO)
    weight = (scaled % (2 * RATIO)).astype(jnp.float32) / (2.0 * RATIO)
    column = jnp.arange(cell_count, dtype=jnp.int32)
    first_part = jnp.where(column[None, :] == bottom[:, None], 1.0 - weight[:, None], 0.0)
    second_part = jnp.where(column[None, :] == bottom[:, None] + 1, weight[:, None], 0.0)
    return first_part + second_part


def ghost_values(face, left_matrix, right_matrix):
    partial_value = jnp.einsum("fbc,kc->fbk", face, right_matrix, precision=highest)
    return jnp.einsum("fbk,jb->fjk", partial_value, left_matrix, precision=highest)


def neighbours(padded):
    summed = padded[2:, 1:-1, 1:-1] + padded[:-2, 1:-1, 1:-1]
    summed = summed + padded[1:-1, 2:, 1:-1] + padded[1:-1, :-2, 1:-1]
    return summed + padded[1:-1, 1:-1, 2:] + padded[1:-1, 1:-1, :-2]


def selection(first_global, length, window_start, window_length):
    here = first_global + jnp.arange(length, dtype=jnp.int32)
    window = window_start + jnp.arange(window_length, dtype=jnp.int32)
    return (here[:, None] == window[None, :]).astype(jnp.float32)


def body(coarse_density, fine_density, fine_start, anchor):
    cell_count = coarse_density.shape[2]
    coarse_rows = coarse_density.shape[0]
    coarse_cols = coarse_density.shape[1]
    matrix = sine_table(cell_count)
    whole_index = jnp.arange(cell_count, dtype=jnp.int32)

    def along_first(block):
        return jnp.einsum("abc,ad->dbc", block, matrix, precision=highest)

    def along_second(block):
        return jnp.einsum("abc,bd->adc", block, matrix, precision=highest)

    def along_third(block):
        return jnp.einsum("abc,cd->abd", block, matrix, precision=highest)

    spectrum = along_third(coarse_density)
    spectrum = along_second(
        lax.all_to_all(spectrum, ("grp", "gy"), split_axis=2, concat_axis=1, tiled=True)
    )
    spectrum = along_first(lax.all_to_all(spectrum, "gx", split_axis=1, concat_axis=0, tiled=True))
    index_second = lax.axis_index("gx") * spectrum.shape[1] + jnp.arange(
        spectrum.shape[1], dtype=jnp.int32
    )
    index_third = lax.axis_index(("grp", "gy")) * spectrum.shape[2] + jnp.arange(
        spectrum.shape[2], dtype=jnp.int32
    )
    divisor = (
        eigen_values(whole_index, cell_count)[:, None, None]
        + eigen_values(index_second, cell_count)[None, :, None]
        + eigen_values(index_third, cell_count)[None, None, :]
    )
    spectrum = along_first(spectrum / divisor)
    spectrum = along_second(lax.all_to_all(spectrum, "gx", split_axis=0, concat_axis=1, tiled=True))
    potential = along_third(
        lax.all_to_all(spectrum, ("grp", "gy"), split_axis=1, concat_axis=2, tiled=True)
    )
    fine_rows, fine_cols, fine_depth = fine_start.shape
    total_x = fine_rows * lax.axis_size("gx")
    total_y = fine_cols * lax.axis_size("gy")
    total_z = fine_depth * lax.axis_size("grp")
    bound_x = total_x // RATIO + 2
    bound_y = total_y // RATIO + 2
    bound_z = total_z // RATIO + 2
    ends_x = interpolation(jnp.array([-1, total_x], dtype=jnp.int32), bound_x)
    ends_y = interpolation(jnp.array([-1, total_y], dtype=jnp.int32), bound_y)
    ends_z = interpolation(jnp.array([-1, total_z], dtype=jnp.int32), bound_z)
    coarse_x_start = lax.axis_index("gx") * coarse_rows
    coarse_y_start = lax.axis_index(("grp", "gy")) * coarse_cols
    pick_x = selection(coarse_x_start, coarse_rows, anchor[0] - 1, bound_x)
    pick_y = selection(coarse_y_start, coarse_cols, anchor[1] - 1, bound_y)
    pick_z = selection(0, cell_count, anchor[2] - 1, bound_z)
    weight_x = jnp.dot(ends_x, pick_x.T, precision=highest)
    weight_y = jnp.dot(ends_y, pick_y.T, precision=highest)
    weight_z = jnp.dot(ends_z, pick_z.T, precision=highest)
    partial_x = jnp.einsum("fx,xyz->fyz", weight_x, potential, precision=highest)
    partial_x = jnp.einsum("fyz,yb->fbz", partial_x, pick_y, precision=highest)
    partial_y = jnp.einsum("fy,xyz->fxz", weight_y, potential, precision=highest)
    partial_y = jnp.einsum("fxz,xa->faz", partial_y, pick_x, precision=highest)
    partial_z = jnp.einsum("fz,xyz->fxy", weight_z, potential, precision=highest)
    partial_z = jnp.einsum("fxy,xa->fay", partial_z, pick_x, precision=highest)
    place_y = selection(coarse_y_start, coarse_cols, 0, cell_count)
    partial_z = jnp.einsum("fay,yg->fag", partial_z, place_y, precision=highest)
    planes = lax.psum((partial_x, partial_y, partial_z), ("grp", "gx", "gy"))
    face_x = lax.dynamic_slice_in_dim(planes[0], anchor[2] - 1, bound_z, 2)
    face_y = lax.dynamic_slice_in_dim(planes[1], anchor[2] - 1, bound_z, 2)
    face_z = lax.dynamic_slice_in_dim(planes[2], anchor[1] - 1, bound_y, 2)
    start_x = lax.axis_index("gx") * fine_rows
    start_y = lax.axis_index("gy") * fine_cols
    start_z = lax.axis_index("grp") * fine_depth
    values = fine_start
    density_wide = with_halo(fine_density, (("grp", 2), ("gx", 0), ("gy", 1)), 1)
    index_x = start_x - 1 + jnp.arange(fine_rows + 2 * 1, dtype=jnp.int32)
    index_y = start_y - 1 + jnp.arange(fine_cols + 2 * 1, dtype=jnp.int32)
    index_z = start_z - 1 + jnp.arange(fine_depth + 2 * 1, dtype=jnp.int32)
    inner_x = interpolation(index_x, bound_x)
    inner_y = interpolation(index_y, bound_y)
    inner_z = interpolation(index_z, bound_z)
    ghost_x = ghost_values(face_x, inner_y, inner_z)
    ghost_y = ghost_values(face_y, inner_x, inner_z)
    ghost_z = ghost_values(face_z, inner_x, inner_y)
    boundary = jnp.where((index_x == 0)[:, None, None], ghost_x[0][None], 0.0)
    boundary = boundary + jnp.where((index_x == total_x - 1)[:, None, None], ghost_x[1][None], 0.0)
    boundary = boundary + jnp.where((index_y == 0)[None, :, None], ghost_y[0][:, None, :], 0.0)
    boundary = boundary + jnp.where(
        (index_y == total_y - 1)[None, :, None], ghost_y[1][:, None, :], 0.0
    )
    boundary = boundary + jnp.where((index_z == 0)[None, None, :], ghost_z[0][:, :, None], 0.0)
    boundary = boundary + jnp.where(
        (index_z == total_z - 1)[None, None, :], ghost_z[1][:, :, None], 0.0
    )
    inside_x = (index_x >= 0) & (index_x < total_x)
    inside_y = (index_y >= 0) & (index_y < total_y)
    inside_z = (index_z >= 0) & (index_z < total_z)
    inside = inside_x[:, None, None] & inside_y[None, :, None] & inside_z[None, None, :]
    boundary_wide, inside = (boundary, inside)
    source_wide = boundary_wide - density_wide / (RATIO * RATIO)
    source_core = source_wide[1:-1, 1:-1, 1:-1]
    for sweep in range(SWEEPS // 2):
        margin_values = with_halo(values, (("grp", 2), ("gx", 0), ("gy", 1)), 2)
        first_pass = jnp.where(inside, (neighbours(margin_values) + source_wide) / 6.0, 0.0)
        values = (neighbours(first_pass) + source_core) / 6.0
    return (potential, values)


def solution(mesh):
    return jax.shard_map(
        body,
        mesh=mesh,
        in_specs=(P("gx", ("grp", "gy"), None), P("gx", "gy", "grp"), P("gx", "gy", "grp"), P()),
        out_specs=(P("gx", ("grp", "gy"), None), P("gx", "gy", "grp")),
        check_vma=False,
    )
```

profile of v0, /device:TPU:58, one launch (start us, length us, event | category | flops | bytes accessed | tf_op | source)
XLA Modules:
  0.0 677.1 jit_solution(1906610364772339676)
XLA Ops:
  8.4 6.3 convolution_bitcast_fusion.1
  14.7 3.7 copy.23
  18.5 3.9 reshape.340
  22.3 43.8 %all_to_all.72 = f32[32,1,8192]{2,1,0:T(1,128)S(1)} all-to-all(f32[32,1,8192]{2,1,0:T(1,128)S(1)} %reshape.340), channel_id=1, replica_groups=mesh['grp'=2,'gx'=16,'gy'=16] {'grp','gy'}, dimensions={0} | all-to-all | bytes 2097152 | tf_op jit(solution)/shard_map/all_to_all | solution.py:85
  66.7 3.2 reduce
  69.9 2.8 reshape.341
  72.6 3.9 copy.25
  76.6 11.7 %fusion.2 = f32[32,512,16]{1,0,2:T(8,128)S(1)} fusion(f32[32,512,16]{0,2,1:T(8,128)S(1)} %bitcast.123, s32[512]{0:T(512)S(1)} %iota_add_fusion), kind=kOutput, calls=%fused_computation.5 | convolution fusion | flops 1613234176 | bytes 2099200 | tf_op jit(solution)/shard_map/abc,bd->adc/dot_general | solution.py:78
  88.3 3.7 copy.27
  92.0 4.9 reshape.342
  96.9 7.3 %all-to-all-start.1 = ((f32[16,1,16384]{2,1,0:T(1,128)}), f32[16,1,16384]{2,1,0:T(1,128)S(1)}, u32[]{:S(2)}, u32[]{:S(2)}) async-start(f32[16,1,16384]{2,1,0:T(1,128)} %reshape.342), calls=%async_computation.1 | async-start | bytes 2097152 | tf_op jit(solution)/shard_map/all_to_all | solution.py:87
  104.4 26.3 %all-to-all-done.1 = f32[16,1,16384]{2,1,0:T(1,128)S(1)} async-done(((f32[16,1,16384]{2,1,0:T(1,128)}), f32[16,1,16384]{2,1,0:T(1,128)S(1)}, u32[]{:S(2)}, u32[]{:S(2)}) %all-to-all-start.1) | async-done | bytes 1048608 | tf_op jit(solution)/shard_map/all_to_all | solution.py:87
  130.6 3.1 reduce.1
  133.8 2.8 reshape.343
  136.6 6.6 copy.57
  143.2 3.9 all_to_all.59
  147.1 6.3 convolution_divide_fusion
  153.5 6.2 fusion.18
  159.7 3.7 copy.30
  163.5 4.8 reshape.344
  168.2 6.2 all-to-all-start.2
  177.5 3.0 collective-permute-start.6
  184.5 15.5 %all-to-all-done.2 = f32[16,1,16384]{2,1,0:T(1,128)S(1)} async-done(((f32[16,1,16384]{2,1,0:T(1,128)}), f32[16,1,16384]{2,1,0:T(1,128)S(1)}, u32[]{:S(2)}, u32[]{:S(2)}) %all-to-all-start.2) | async-done | bytes 1048608 | tf_op jit(solution)/shard_map/all_to_all | solution.py:100
  200.0 3.1 reduce.2
  205.9 6.6 copy.56
  212.6 3.5 all_to_all.63
  216.1 6.0 convolution_bitcast_fusion
  222.1 3.7 copy.32
  225.8 4.8 reshape.346
  230.6 7.1 %all-to-all-start.3 = ((f32[32,1,8192]{2,1,0:T(1,128)}), f32[32,1,8192]{2,1,0:T(1,128)S(1)}, u32[]{:S(2)}, u32[]{:S(2)}) async-start(f32[32,1,8192]{2,1,0:T(1,128)} %reshape.346), calls=%async_computation.3 | async-start | bytes 2097152 | tf_op jit(solution)/shard_map/all_to_all | solution.py:102
  242.1 6.6 collective-permute-start.3
  248.7 16.8 %all-to-all-done.3 = f32[32,1,8192]{2,1,0:T(1,128)S(1)} async-done(((f32[32,1,8192]{2,1,0:T(1,128)}), f32[32,1,8192]{2,1,0:T(1,128)S(1)}, u32[]{:S(2)}, u32[]{:S(2)}) %all-to-all-start.3) | async-done | bytes 1048608 | tf_op jit(solution)/shard_map/all_to_all | solution.py:102
  265.5 3.2 reduce.3
  274.1 11.1 %fusion.15 = f32[32,16,512]{2,0,1:T(8,128)S(1)} fusion(f32[32,16,512]{0,2,1:T(8,128)S(1)} %bitcast.134, s32[512]{0:T(512)S(1)} %iota_add_fusion), kind=kOutput, calls=%fused_computation.28 | convolution fusion | flops 1613234176 | bytes 2099200 | tf_op jit(solution)/shard_map/abc,cd->abd/dot_general | solution.py:81
  295.2 6.3 collective-permute-start.9
  301.7 6.7 collective-permute-start.4
  310.5 9.9 %collective-permute-start.10 = (f32[10,1,130]{2,1,0:T(1,128)S(1)}, f32[10,1,130]{2,1,0:T(1,128)S(1)}, u32[]{:S(2)}, u32[]{:S(2)}) collective-permute-start(f32[10,1,130]{2,1,0:T(1,128)S(1)} %get-tuple-element.17), channel_id=1, source_target_pairs={{0,1},{1,2},{2,3},{3,4},{4,5},{5,6},{6,7},{7,8},{8,9},{9,10},{10,1... | collective-permute-start | bytes 15608 | tf_op jit(solution)/shard_map/ppermute | solution.py:20
  322.6 245.4 %all-reduce.3.cloned.1.call-done = (f32[2,34,512]{2,1,0:T(8,128)}, f32[2,34,512]{2,1,0:T(8,128)}, f32[2,130,512]{2,1,0:T(8,128)}) async-done(((f32[2,34,512]{2,1,0:T(8,128)}, f32[2,34,512]{2,1,0:T(8,128)}, f32[2,130,512]{2,1,0:T(8,128)}), (f32[2,34,512]{2,1,0:T(8,128)}, f32[2,34,512]{2,1,0:T(8,128)}, f32[2,130,512]{2,1,0:T(8,128)})) %all-reduce.3.cloned.1.call-update) | async-done | bytes 811024 | tf_op jit(solution)/shard_map/psum | solution.py:130
  580.8 6.6 collective-permute-start.15
  589.5 5.4 collective-permute-start.16
  596.8 9.8 %collective-permute-done.17 = f32[12,2,132]{2,1,0:T(2,128)S(1)} collective-permute-done((f32[12,2,132]{2,1,0:T(2,128)S(1)}, f32[12,2,132]{2,1,0:T(2,128)S(1)}, u32[]{:S(2)}, u32[]{:S(2)}) %collective-permute-start.17) | collective-permute-done | bytes 12704 | tf_op jit(solution)/shard_map/ppermute | solution.py:23
  615.0 6.6 collective-permute-start.21
  625.5 3.9 collective-permute-start.23
  629.5 7.9 %collective-permute-done.23 = f32[12,2,132]{2,1,0:T(2,128)S(1)} collective-permute-done((f32[12,2,132]{2,1,0:T(2,128)S(1)}, f32[12,2,132]{2,1,0:T(2,128)S(1)}, u32[]{:S(2)}, u32[]{:S(2)}) %collective-permute-start.23) | collective-permute-done | bytes 12704 | tf_op jit(solution)/shard_map/ppermute | solution.py:23
  643.5 3.3 collective-permute-start.26
  646.8 5.6 collective-permute-start.27
  656.3 3.9 collective-permute-start.29
  660.3 7.8 %collective-permute-done.29 = f32[12,2,132]{2,1,0:T(2,128)S(1)} collective-permute-done((f32[12,2,132]{2,1,0:T(2,128)S(1)}, f32[12,2,132]{2,1,0:T(2,128)S(1)}, u32[]{:S(2)}, u32[]{:S(2)}) %collective-permute-start.29) | collective-permute-done | bytes 12704 | tf_op jit(solution)/shard_map/ppermute | solution.py:23
  (148 shorter events, 73.3 us)
Async XLA Ops:
  7.2 1.2 copy-start
  96.9 33.8 %all-to-all-start.1 = ((f32[16,1,16384]{2,1,0:T(1,128)}), f32[16,1,16384]{2,1,0:T(1,128)S(1)}, u32[]{:S(2)}, u32[]{:S(2)}) async-start(f32[16,1,16384]{2,1,0:T(1,128)} %reshape.342), calls=%async_computation.1 | async-start | bytes 2097152 | tf_op jit(solution)/shard_map/all_to_all | solution.py:87
  163.5 10.9 %copy-start.2 = (f32[8,32,128]{2,1,0:T(8,128)S(1)}, f32[8,32,128]{2,1,0:T(8,128)}, u32[]{:S(2)}) copy-start(f32[8,32,128]{2,1,0:T(8,128)} %param.9) | copy-start | bytes 393220
  163.5 14.0 %copy-start.4 = (f32[8,32,128]{2,1,0:T(8,128)S(1)}, f32[8,32,128]{2,1,0:T(8,128)}, u32[]{:S(2)}) copy-start(f32[8,32,128]{2,1,0:T(8,128)} %param.8) | copy-start | bytes 393220
  163.5 18.4 %copy-start.5 = (s32[3]{0:T(128)S(1)}, s32[3]{0:T(128)}, u32[]{:S(2)}) copy-start(s32[3]{0:T(128)} %param.10) | copy-start | bytes 40
  168.2 31.8 %all-to-all-start.2 = ((f32[16,1,16384]{2,1,0:T(1,128)}), f32[16,1,16384]{2,1,0:T(1,128)S(1)}, u32[]{:S(2)}, u32[]{:S(2)}) async-start(f32[16,1,16384]{2,1,0:T(1,128)} %reshape.344), calls=%async_computation.2 | async-start | bytes 2097152 | tf_op jit(solution)/shard_map/all_to_all | solution.py:100
  174.5 65.5 %collective-permute-start = (f32[8,32,2]{2,1,0:T(8,128)S(1)}, f32[8,32,2]{2,1,0:T(8,128)S(1)}, u32[]{:S(2)}, u32[]{:S(2)}) collective-permute-start(f32[8,32,2]{2,1,0:T(8,128)S(1)} %get-tuple-element.37), channel_id=1, source_target_pairs={{0,256},{1,257},{2,258},{3,259},{4,260},{5,261},{6,262},{7,263},{8... | collective-permute-start | bytes 6152 | tf_op jit(solution)/shard_map/ppermute | solution.py:20
  176.1 63.9 %collective-permute-start.1 = (f32[8,32,2]{2,1,0:T(8,128)S(1)}, f32[8,32,2]{2,1,0:T(8,128)S(1)}, u32[]{:S(2)}, u32[]{:S(2)}) collective-permute-start(f32[8,32,2]{2,1,0:T(8,128)S(1)} %get-tuple-element.38), channel_id=1, source_target_pairs={{256,0},{257,1},{258,2},{259,3},{260,4},{261,5},{262,6},{263,7},{2... | collective-permute-start | bytes 6152 | tf_op jit(solution)/shard_map/ppermute | solution.py:23
  177.5 115.4 %collective-permute-start.6 = (f32[8,32,1]{2,1,0:T(8,128)S(1)}, f32[8,32,1]{2,1,0:T(8,128)S(1)}, u32[]{:S(2)}, u32[]{:S(2)}) collective-permute-start(f32[8,32,1]{2,1,0:T(8,128)S(1)} %get-tuple-element.35), channel_id=1, source_target_pairs={{0,256},{1,257},{2,258},{3,259},{4,260},{5,261},{6,262},{7,263},{8... | collective-permute-start | bytes 3080 | tf_op jit(solution)/shard_map/ppermute | solution.py:20
  180.6 112.3 %collective-permute-start.7 = (f32[8,32,1]{2,1,0:T(8,128)S(1)}, f32[8,32,1]{2,1,0:T(8,128)S(1)}, u32[]{:S(2)}, u32[]{:S(2)}) collective-permute-start(f32[8,32,1]{2,1,0:T(8,128)S(1)} %get-tuple-element.36), channel_id=1, source_target_pairs={{256,0},{257,1},{258,2},{259,3},{260,4},{261,5},{262,6},{263,7},{2... | collective-permute-start | bytes 3080 | tf_op jit(solution)/shard_map/ppermute | solution.py:23
  225.8 12.2 %copy-start.6 = (f32[2]{0:T(128)S(1)}, f32[2]{0:T(128)}, u32[]{:S(2)}) copy-start(f32[2]{0:T(128)} %constant.270) | copy-start | bytes 28
  225.8 12.2 %copy-start.7 = (f32[2]{0:T(128)S(1)}, f32[2]{0:T(128)}, u32[]{:S(2)}) copy-start(f32[2]{0:T(128)} %constant.271) | copy-start | bytes 28
  225.8 12.2 %copy-start.10 = (s32[2]{0:T(128)S(1)}, s32[2]{0:T(128)}, u32[]{:S(2)}) copy-start(s32[2]{0:T(128)} %constant.322) | copy-start | bytes 28
  225.8 12.4 %copy-start.9 = (s32[2]{0:T(128)S(1)}, s32[2]{0:T(128)}, u32[]{:S(2)}) copy-start(s32[2]{0:T(128)} %constant.272) | copy-start | bytes 28
  225.8 12.6 %copy-start.8 = (s32[2]{0:T(128)S(1)}, s32[2]{0:T(128)}, u32[]{:S(2)}) copy-start(s32[2]{0:T(128)} %constant.297) | copy-start | bytes 28
  230.6 34.9 %all-to-all-start.3 = ((f32[32,1,8192]{2,1,0:T(1,128)}), f32[32,1,8192]{2,1,0:T(1,128)S(1)}, u32[]{:S(2)}, u32[]{:S(2)}) async-start(f32[32,1,8192]{2,1,0:T(1,128)} %reshape.346), calls=%async_computation.3 | async-start | bytes 2097152 | tf_op jit(solution)/shard_map/all_to_all | solution.py:102
  237.7 330.2 %all-reduce.3.cloned.1.call-start = ((), (), s32[]{:S(2)}) async-start(), calls=%async_computation.4 | async-start | bytes 1769472 | tf_op jit(solution)/shard_map/psum | solution.py:130
  240.2 61.4 %collective-permute-start.2 = (f32[2,32,132]{2,1,0:T(8,128)S(1)}, f32[2,32,132]{2,1,0:T(8,128)S(1)}, u32[]{:S(2)}, u32[]{:S(2)}) collective-permute-start(f32[2,32,132]{2,1,0:T(8,128)S(1)} %get-tuple-element.27), channel_id=1, source_target_pairs={{0,16},{16,32},{32,48},{48,64},{64,80},{80,96},{96,112},{112,128},... | collective-permute-start | bytes 101384 | tf_op jit(solution)/shard_map/ppermute | solution.py:20
  242.1 59.5 %collective-permute-start.3 = (f32[2,32,132]{2,1,0:T(8,128)S(1)}, f32[2,32,132]{2,1,0:T(8,128)S(1)}, u32[]{:S(2)}, u32[]{:S(2)}) collective-permute-start(f32[2,32,132]{2,1,0:T(8,128)S(1)} %get-tuple-element.28), channel_id=1, source_target_pairs={{16,0},{32,16},{48,32},{64,48},{80,64},{96,80},{112,96},{128,112},... | collective-permute-start | bytes 101384 | tf_op jit(solution)/shard_map/ppermute | solution.py:23
  285.8 283.6 %copy-start.3 = (f32[32,16,512]{2,1,0:T(8,128)}, f32[32,16,512]{2,1,0:T(8,128)S(1)}, u32[]{:S(2)}) copy-start(f32[32,16,512]{2,1,0:T(8,128)S(1)} %copy.39) | copy-start | bytes 3145732
  293.0 17.3 %collective-permute-start.8 = (f32[1,32,130]{2,1,0:T(8,128)S(1)}, f32[1,32,130]{2,1,0:T(8,128)S(1)}, u32[]{:S(2)}, u32[]{:S(2)}) collective-permute-start(f32[1,32,130]{2,1,0:T(8,128)S(1)} %get-tuple-element.25), channel_id=1, source_target_pairs={{0,16},{16,32},{32,48},{48,64},{64,80},{80,96},{96,112},{112,128},... | collective-permute-start | bytes 49928 | tf_op jit(solution)/shard_map/ppermute | solution.py:20
  295.2 15.1 %collective-permute-start.9 = (f32[1,32,130]{2,1,0:T(8,128)S(1)}, f32[1,32,130]{2,1,0:T(8,128)S(1)}, u32[]{:S(2)}, u32[]{:S(2)}) collective-permute-start(f32[1,32,130]{2,1,0:T(8,128)S(1)} %get-tuple-element.26), channel_id=1, source_target_pairs={{16,0},{32,16},{48,32},{64,48},{80,64},{96,80},{112,96},{128,112},... | collective-permute-start | bytes 49928 | tf_op jit(solution)/shard_map/ppermute | solution.py:23
  301.7 20.6 %collective-permute-start.4 = (f32[12,2,132]{2,1,0:T(2,128)S(1)}, f32[12,2,132]{2,1,0:T(2,128)S(1)}, u32[]{:S(2)}, u32[]{:S(2)}) collective-permute-start(f32[12,2,132]{2,1,0:T(2,128)S(1)} %get-tuple-element.15), channel_id=1, source_target_pairs={{0,1},{1,2},{2,3},{3,4},{4,5},{5,6},{6,7},{7,8},{8,9},{9,10},{10,1... | collective-permute-start | bytes 38024 | tf_op jit(solution)/shard_map/ppermute | solution.py:20
  308.4 14.0 %collective-permute-start.5 = (f32[12,2,132]{2,1,0:T(2,128)S(1)}, f32[12,2,132]{2,1,0:T(2,128)S(1)}, u32[]{:S(2)}, u32[]{:S(2)}) collective-permute-start(f32[12,2,132]{2,1,0:T(2,128)S(1)} %get-tuple-element.16), channel_id=1, source_target_pairs={{1,0},{2,1},{3,2},{4,3},{5,4},{6,5},{7,6},{8,7},{9,8},{10,9},{11,1... | collective-permute-start | bytes 38024 | tf_op jit(solution)/shard_map/ppermute | solution.py:23
  310.5 262.2 %collective-permute-start.10 = (f32[10,1,130]{2,1,0:T(1,128)S(1)}, f32[10,1,130]{2,1,0:T(1,128)S(1)}, u32[]{:S(2)}, u32[]{:S(2)}) collective-permute-start(f32[10,1,130]{2,1,0:T(1,128)S(1)} %get-tuple-element.17), channel_id=1, source_target_pairs={{0,1},{1,2},{2,3},{3,4},{4,5},{5,6},{6,7},{7,8},{8,9},{9,10},{10,1... | collective-permute-start | bytes 15608 | tf_op jit(solution)/shard_map/ppermute | solution.py:20
  320.4 252.3 %collective-permute-start.11 = (f32[10,1,130]{2,1,0:T(1,128)S(1)}, f32[10,1,130]{2,1,0:T(1,128)S(1)}, u32[]{:S(2)}, u32[]{:S(2)}) collective-permute-start(f32[10,1,130]{2,1,0:T(1,128)S(1)} %get-tuple-element.18), channel_id=1, source_target_pairs={{1,0},{2,1},{3,2},{4,3},{5,4},{6,5},{7,6},{8,7},{9,8},{10,9},{11,1... | collective-permute-start | bytes 15608 | tf_op jit(solution)/shard_map/ppermute | solution.py:23
  574.2 2.6 collective-permute-start.12
  575.5 3.2 collective-permute-start.13
  578.9 8.9 %collective-permute-start.14 = (f32[2,32,132]{2,1,0:T(8,128)S(1)}, f32[2,32,132]{2,1,0:T(8,128)S(1)}, u32[]{:S(2)}, u32[]{:S(2)}) collective-permute-start(f32[2,32,132]{2,1,0:T(8,128)S(1)} %get-tuple-element.23), channel_id=1, source_target_pairs={{0,16},{16,32},{32,48},{48,64},{64,80},{80,96},{96,112},{112,128},... | collective-permute-start | bytes 101384 | tf_op jit(solution)/shard_map/ppermute | solution.py:20
  580.8 8.5 %collective-permute-start.15 = (f32[2,32,132]{2,1,0:T(8,128)S(1)}, f32[2,32,132]{2,1,0:T(8,128)S(1)}, u32[]{:S(2)}, u32[]{:S(2)}) collective-permute-start(f32[2,32,132]{2,1,0:T(8,128)S(1)} %get-tuple-element.24), channel_id=1, source_target_pairs={{16,0},{32,16},{48,32},{64,48},{80,64},{96,80},{112,96},{128,112},... | collective-permute-start | bytes 101384 | tf_op jit(solution)/shard_map/ppermute | solution.py:23
  589.5 7.3 %collective-permute-start.16 = (f32[12,2,132]{2,1,0:T(2,128)S(1)}, f32[12,2,132]{2,1,0:T(2,128)S(1)}, u32[]{:S(2)}, u32[]{:S(2)}) collective-permute-start(f32[12,2,132]{2,1,0:T(2,128)S(1)} %get-tuple-element.13), channel_id=1, source_target_pairs={{0,1},{1,2},{2,3},{3,4},{4,5},{5,6},{6,7},{7,8},{8,9},{9,10},{10,1... | collective-permute-start | bytes 38024 | tf_op jit(solution)/shard_map/ppermute | solution.py:20
  594.9 11.7 %collective-permute-start.17 = (f32[12,2,132]{2,1,0:T(2,128)S(1)}, f32[12,2,132]{2,1,0:T(2,128)S(1)}, u32[]{:S(2)}, u32[]{:S(2)}) collective-permute-start(f32[12,2,132]{2,1,0:T(2,128)S(1)} %get-tuple-element.14), channel_id=1, source_target_pairs={{1,0},{2,1},{3,2},{4,3},{5,4},{6,5},{7,6},{8,7},{9,8},{10,9},{11,1... | collective-permute-start | bytes 38024 | tf_op jit(solution)/shard_map/ppermute | solution.py:23
  608.0 2.6 collective-permute-start.18
  609.3 3.2 collective-permute-start.19
  612.7 9.5 %collective-permute-start.20 = (f32[2,32,132]{2,1,0:T(8,128)S(1)}, f32[2,32,132]{2,1,0:T(8,128)S(1)}, u32[]{:S(2)}, u32[]{:S(2)}) collective-permute-start(f32[2,32,132]{2,1,0:T(8,128)S(1)} %get-tuple-element.21), channel_id=1, source_target_pairs={{0,16},{16,32},{32,48},{48,64},{64,80},{80,96},{96,112},{112,128},... | collective-permute-start | bytes 101384 | tf_op jit(solution)/shard_map/ppermute | solution.py:20
  615.0 8.5 %collective-permute-start.21 = (f32[2,32,132]{2,1,0:T(8,128)S(1)}, f32[2,32,132]{2,1,0:T(8,128)S(1)}, u32[]{:S(2)}, u32[]{:S(2)}) collective-permute-start(f32[2,32,132]{2,1,0:T(8,128)S(1)} %get-tuple-element.22), channel_id=1, source_target_pairs={{16,0},{32,16},{48,32},{64,48},{80,64},{96,80},{112,96},{128,112},... | collective-permute-start | bytes 101384 | tf_op jit(solution)/shard_map/ppermute | solution.py:23
  623.6 5.9 collective-permute-start.22
  625.5 11.8 %collective-permute-start.23 = (f32[12,2,132]{2,1,0:T(2,128)S(1)}, f32[12,2,132]{2,1,0:T(2,128)S(1)}, u32[]{:S(2)}, u32[]{:S(2)}) collective-permute-start(f32[12,2,132]{2,1,0:T(2,128)S(1)} %get-tuple-element.12), channel_id=1, source_target_pairs={{1,0},{2,1},{3,2},{4,3},{5,4},{6,5},{7,6},{8,7},{9,8},{10,9},{11,1... | collective-permute-start | bytes 38024 | tf_op jit(solution)/shard_map/ppermute | solution.py:23
  637.6 32.5 %copy-start.1 = (f32[32,16,512]{2,1,0:T(8,128)S(1)}, f32[32,16,512]{2,1,0:T(8,128)}, u32[]{:S(2)}) copy-start(f32[32,16,512]{2,1,0:T(8,128)} %param.7) | copy-start | bytes 3145732
  638.8 2.6 collective-permute-start.24
  640.1 3.2 collective-permute-start.25
  643.5 9.5 %collective-permute-start.26 = (f32[2,32,132]{2,1,0:T(8,128)S(1)}, f32[2,32,132]{2,1,0:T(8,128)S(1)}, u32[]{:S(2)}, u32[]{:S(2)}) collective-permute-start(f32[2,32,132]{2,1,0:T(8,128)S(1)} %get-tuple-element.19), channel_id=1, source_target_pairs={{0,16},{16,32},{32,48},{48,64},{64,80},{80,96},{96,112},{112,128},... | collective-permute-start | bytes 101384 | tf_op jit(solution)/shard_map/ppermute | solution.py:20
  646.8 7.5 %collective-permute-start.27 = (f32[2,32,132]{2,1,0:T(8,128)S(1)}, f32[2,32,132]{2,1,0:T(8,128)S(1)}, u32[]{:S(2)}, u32[]{:S(2)}) collective-permute-start(f32[2,32,132]{2,1,0:T(8,128)S(1)} %get-tuple-element.20), channel_id=1, source_target_pairs={{16,0},{32,16},{48,32},{64,48},{80,64},{96,80},{112,96},{128,112},... | collective-permute-start | bytes 101384 | tf_op jit(solution)/shard_map/ppermute | solution.py:23
  654.4 5.9 collective-permute-start.28
  656.3 11.7 %collective-permute-start.29 = (f32[12,2,132]{2,1,0:T(2,128)S(1)}, f32[12,2,132]{2,1,0:T(2,128)S(1)}, u32[]{:S(2)}, u32[]{:S(2)}) collective-permute-start(f32[12,2,132]{2,1,0:T(2,128)S(1)} %get-tuple-element.10), channel_id=1, source_target_pairs={{1,0},{2,1},{3,2},{4,3},{5,4},{6,5},{7,6},{8,7},{9,8},{10,9},{11,1... | collective-permute-start | bytes 38024 | tf_op jit(solution)/shard_map/ppermute | solution.py:23
Sparse Core Ops, SparseCore 0:
  293.0 274.8 all-reduce.2
where the time goes:
time: 685 us; the launch traced here: 677 us
  waiting for transfers between devices  341 us (50%)
  starting transfers between devices  118 us (17%)
  local copies, waits for them, and re-layouts  75.1 us (11%)
  matrix products  59.9 us (9%)
  blocking collectives  43.8 us (6%)
  other arithmetic  20.5 us (3%)
  between operations  18.4 us (3%)
    psum x1, waiting for transfers between devices, body(): planes = lax.psum((partial_x, partial_y, partial_z), ('grp', 'gx', 'gy'))  245 us
    ppermute x15, starting transfers between devices, with_halo(): lax.ppermute(lax.slice_in_dim(block, 0, width, axis=dim), axis, backward)  51.8 us
    ppermute x15, starting transfers between devices, with_halo(): lax.ppermute(lax.slice_in_dim(block, block.shape[dim] - width, None, axis...  46 us
    all_to_all x1, blocking collectives, body(): lax.all_to_all(spectrum, ('grp', 'gy'), split_axis=2, concat_axis=1, tile...  43.8 us
    ppermute x15, waiting for transfers between devices, with_halo(): lax.ppermute(lax.slice_in_dim(block, 0, width, axis=dim), axis, backward)  35.5 us
    unnamed x31, local copies, waits for them, and re-layouts  31.2 us
    all_to_all x1, waiting for transfers between devices, body(): lax.all_to_all(spectrum, 'gx', split_axis=1, concat_axis=0, tiled=True)  26.3 us
    dot_general x2, matrix products, along_second(): return jnp.einsum('abc,bd->adc', block, matrix, precision=highest)  17.6 us
  transfers between devices with their start and end apart: 34, of which 16 were waited for; matrix products, arithmetic and copies ran while one was open for 9% of the time, Pallas kernels for 0%

commit v1 on v0

--- a/solution.py
+++ b/solution.py
@@ -1,9 +1,310 @@
+import functools
 import math
 
 import jax
 import jax.numpy as jnp
+import numpy as np
 from jax import lax
+from jax.experimental import pallas as pl
+from jax.experimental.pallas import tpu as pltpu
 from jax.sharding import PartitionSpec as P
+
+MESH = pl.DeviceIdType.MESH
+NC = 512
+F32 = jnp.float32
+BF16 = jnp.bfloat16
+
+
+def tables():
+    index = np.arange(1, NC + 1, dtype=np.int64)
+    angle = (index[:, None] * index[None, :]) % (2 * (NC + 1))
+    sine = math.sqrt(2.0 / (NC + 1)) * np.sin(angle * (math.pi / (NC + 1)))
+    sine = sine.astype(np.float32)
+    high = sine.astype(jnp.bfloat16)
+    low = (sine - high.astype(np.float32)).astype(jnp.bfloat16)
+    lam = 4.0 * np.sin(index * (math.pi / (2 * (NC + 1)))) ** 2
+    return high, low, lam.astype(np.float32)
+
+
+def split(value):
+    high = value.astype(BF16)
+    low = (value - high.astype(F32)).astype(BF16)
+    return high, low
+
+
+def dot3(a, b, dims):
+    ah, al = a
+    bh, bl = b
+    dd = functools.partial(
+        lax.dot_general, dimension_numbers=(dims, ((), ())), preferred_element_type=F32
+    )
+    return dd(ah, bh) + (dd(al, bh) + dd(ah, bl))
+
+
+NN = ((1,), (0,))
+NT = ((1,), (1,))
+TN = ((0,), (0,))
+
+
+def swap_groups(source, target):
+    lane = lax.broadcasted_iota(jnp.int32, (8, 128), 1) // 16
+
+    def step(index, carry):
+        at = index // 8
+        bt = (index // 2) % 4
+        row = pl.multiple_of((index % 2) * 8, 8)
+        cols = pl.ds(pl.multiple_of(bt * 128, 128), 128)
+        outs = pl.ds(pl.multiple_of(at * 128, 128), 128)
+        v = [source[at * 8 + q, pl.ds(row, 8), cols] for q in range(8)]
+        for bit in (1, 2, 4):
+            upper = (lane & bit) != 0
+            for i in range(8):
+                if i & bit:
+                    continue
+                a, c = v[i], v[i | bit]
+                v[i] = jnp.where(upper, pltpu.roll(c, 16 * bit, 1), a)
+                v[i | bit] = jnp.where(upper, c, pltpu.roll(a, 128 - 16 * bit, 1))
+        for q in range(8):
+            target[bt * 8 + q, pl.ds(row, 8), outs] = v[q]
+        return carry
+
+    lax.fori_loop(0, 32, step, 0)
+
+
+def device(core, x, y, z):
+    return (core, x * 4 + z % 4, (z // 4) * 8 + y)
+
+
+ORDER = [
+    (dy, side, core) for dy in (4, 3, 5, 2, 6, 1, 7, 0) for side in (0, 1) for core in (0, 1)
+]
+
+
+def shuffled():
+    return list(ORDER[i] for i in np.random.RandomState(3).permutation(len(ORDER)))
+
+
+def coarse_kernel(
+    x_ref, sh_ref, sl_ref, lamr_ref, lamc_ref, lamq_ref, out_ref,
+    za, zb, dd, u, dtab, m1, r1, m2, r2, dint,
+    s1, q1, s2, q2, s3, q3, s4, q4,
+):
+    core = lax.axis_index("grp")
+    gx = lax.axis_index("gx")
+    gy = lax.axis_index("gy")
+    x, zl = gx // 4, gx % 4
+    y, zh = gy % 8, gy // 8
+    z = zh * 4 + zl
+    me = core * 16 + gy
+    zv = (z + 6) % 8
+    lv, hv = zv % 4, zv // 4
+    mid = core * 16 + hv * 8 + y
+    pv = x * 4 + lv
+
+    def to_mid(o):
+        dy, side, oc = o
+        ty = (y + dy) % 8
+        tc = (core + oc) % 2
+        return device(tc, x, ty, (zl + 4 * side + 2) % 8), tc * 16 + side * 8 + ty
+
+    def to_real(o):
+        dy, side, oc = o
+        ty = (y + dy) % 8
+        tc = (core + oc) % 2
+        return device(tc, x, ty, lv + 4 * side), tc * 16 + side * 8 + ty
+
+    def to_row(q):
+        return device(core, q // 4, y, (q % 4 + 4 * hv + 2) % 8)
+
+    barrier = pltpu.get_barrier_semaphore()
+    peers = shuffled()
+    for o in peers:
+        pl.semaphore_signal(barrier, inc=1, device_id=to_mid(o)[0], device_id_type=MESH)
+    for k in range(1, 16):
+        pl.semaphore_signal(barrier, inc=1, device_id=to_row((pv + k) % 16), device_id_type=MESH)
+
+    s_pair = (sh_ref[...], sl_ref[...])
+    value = x_ref[...].reshape(512, 512)
+    za[...] = dot3(split(value), s_pair, NN).reshape(32, 16, 512)
+    swap_groups(za, zb)
+
+    pl.semaphore_wait(barrier, 47)
+
+    t1 = []
+    for i, o in enumerate(peers):
+        target, block = to_mid(o)
+        copy = pltpu.make_async_remote_copy(
+            src_ref=zb.at[block], dst_ref=dd.at[me], send_sem=s1.at[i], recv_sem=q1.at[me],
+            device_id=target, device_id_type=MESH,
+        )
+        copy.start()
+        t1.append(copy)
+
+    mu = lamr_ref[...] + lamc_ref[pl.ds(pl.multiple_of(mid * 16, 16), 16), :]
+
+    def table(i, g):
+        d = 1.0 / (1.0 + (mu + g))
+        dtab[i] = d
+        return (mu + g) * d
+
+    lax.fori_loop(0, 31, table, jnp.ones((16, 512), F32))
+    muq = lamq_ref[...] + lamc_ref[pl.ds(mid * 16 + pv, 1), :]
+    c = 0.5 * muq
+    c1 = c
+    r32 = 2.0 * (1.0 + c)
+    for _ in range(4):
+        c = 2.0 * c * (c + 2.0)
+        r32 = r32 * (2.0 * (1.0 + c))
+    c = 2.0 * c * (c + 2.0)
+    g = jnp.ones((4, 128), F32)
+    for i in range(15):
+        d = 1.0 / (1.0 + (2.0 * c + g))
+        dint[i] = d
+        g = (2.0 * c + g) * d
+    dint[15] = 1.0 / (r32 * (1.0 + c1) + c + g)
+
+    for s in range(32):
+        pltpu.make_async_remote_copy(
+            src_ref=dd.at[s], dst_ref=dd.at[s], send_sem=s1.at[s], recv_sem=q1.at[s],
+            device_id=(core, gx, gy), device_id_type=MESH,
+        ).wait_recv()
+
+    value = dd[...].reshape(512, 512)
+    u[...] = dot3(split(value), s_pair, TN).reshape(32, 16, 512)
+
+    first = -u[0]
+    u[0] = first
+    q0 = dtab[30]
+
+    def forward(i, carry):
+        yv, q, e = carry
+        w = u[i]
+        yv = dtab[i - 1] * yv - w
+        u[i] = yv
+        q = q * dtab[30 - i]
+        return yv, q, e - q * w
+
+    yv, _, e = lax.fori_loop(1, 31, forward, (first, q0, q0 * first))
+    b = q0 * yv - u[31]
+    for j in range(4):
+        m1[pl.ds(j, 16, stride=8), :] = e[:, 128 * j : 128 * j + 128]
+        m1[pl.ds(4 + j, 16, stride=8), :] = b[:, 128 * j : 128 * j + 128]
+    t2 = []
+    for k in range(1, 16):
+        q = (pv + k) % 16
+        copy = pltpu.make_async_remote_copy(
+            src_ref=m1.at[pl.ds(pl.multiple_of(q * 8, 8), 8), :], dst_ref=r1.at[pv],
+            send_sem=s2.at[k], recv_sem=q2.at[pv], device_id=to_row(q), device_id_type=MESH,
+        )
+        copy.start()
+        t2.append(copy)
+    r1[pv] = m1[pl.ds(pl.multiple_of(pv * 8, 8), 8), :]
+    for k in range(1, 16):
+        q = (pv + k) % 16
+        pltpu.make_async_remote_copy(
+            src_ref=r1.at[q], dst_ref=r1.at[q], send_sem=s2.at[k], recv_sem=q2.at[q],
+            device_id=(core, gx, gy), device_id_type=MESH,
+        ).wait_recv()
+    ys = []
+    prev = None
+    for p in range(16):
+        h = r1[p, 4:8, :]
+        if p < 15:
+            h = h + r1[p + 1, 0:4, :]
+        h = r32 * h
+        prev = h if p == 0 else h + dint[p - 1] * prev
+        ys.append(prev)
+    sol = [None] * 16
+    sol[15] = dint[15] * ys[15]
+    for p in range(14, -1, -1):
+        sol[p] = dint[p] * (sol[p + 1] + ys[p])
+    for p in range(16):
+        m2[p, 0:4, :] = sol[p - 1] if p else jnp.zeros((4, 128), F32)
+        m2[p, 4:8, :] = sol[p]
+    t3 = []
+    for k in range(1, 16):
+        q = (pv + k) % 16
+        copy = pltpu.make_async_remote_copy(
+            src_ref=m2.at[q], dst_ref=r2.at[pl.ds(pl.multiple_of(pv * 8, 8), 8), :],
+            send_sem=s3.at[k], recv_sem=q3.at[pv], device_id=to_row(q), device_id_type=MESH,
+        )
+        copy.start()
+        t3.append(copy)
+    r2[pl.ds(pl.multiple_of(pv * 8, 8), 8), :] = m2[pv]
+    for k in range(1, 16):
+        q = (pv + k) % 16
+        view = r2.at[pl.ds(pl.multiple_of(q * 8, 8), 8), :]
+        pltpu.make_async_remote_copy(
+            src_ref=view, dst_ref=view, send_sem=s3.at[k], recv_sem=q3.at[q],
+            device_id=(core, gx, gy), device_id_type=MESH,
+        ).wait_recv()
+    left = jnp.concatenate([r2[pl.ds(j, 16, stride=8), :] for j in range(4)], axis=1)
+    right = jnp.concatenate([r2[pl.ds(4 + j, 16, stride=8), :] for j in range(4)], axis=1)
+
+    def spread(i, t):
+        u[i] = u[i] + t
+        return dtab[i] * t
+
+    lax.fori_loop(0, 31, spread, left)
+    u[31] = right
+
+    def backward(k, v):
+        i = 30 - k
+        v = dtab[i] * (v + u[i])
+        u[i] = v
+        return v
+
+    lax.fori_loop(0, 31, backward, right)
+
+    for copy in t1:
+        copy.wait_send()
+    value = u[...].reshape(512, 512)
+    zb[...] = dot3(s_pair, split(value), NT).reshape(32, 16, 512)
+    t4 = []
+    for i, o in enumerate(peers):
+        target, block = to_real(o)
+        copy = pltpu.make_async_remote_copy(
+            src_ref=zb.at[block], dst_ref=za.at[mid], send_sem=s4.at[i], recv_sem=q4.at[mid],
+            device_id=target, device_id_type=MESH,
+        )
+        copy.start()
+        t4.append(copy)
+    for s in range(32):
+        pltpu.make_async_remote_copy(
+            src_ref=za.at[s], dst_ref=za.at[s], send_sem=s4.at[s], recv_sem=q4.at[s],
+            device_id=(core, gx, gy), device_id_type=MESH,
+        ).wait_recv()
+    swap_groups(za, dd)
+    value = dd[...].reshape(512, 512)
+    out_ref[...] = dot3(split(value), s_pair, NN).reshape(32, 16, 512)
+    for copy in t2 + t3 + t4:
+        copy.wait_send()
+
+
+def coarse(density):
+    high, low, lam = tables()
+    vm = pl.BlockSpec(memory_space=pltpu.VMEM)
+    big = pltpu.VMEM((32, 16, 512), F32)
+    dma = pltpu.SemaphoreType.DMA
+    return pl.pallas_call(
+        coarse_kernel,
+        out_shape=jax.ShapeDtypeStruct((32, 16, 512), F32),
+        in_specs=[vm] * 6,
+        out_specs=vm,
+        scratch_shapes=[
+            big, big, big, big, pltpu.VMEM((31, 16, 512), F32),
+            pltpu.VMEM((128, 128), F32), pltpu.VMEM((16, 8, 128), F32),
+            pltpu.VMEM((16, 8, 128), F32), pltpu.VMEM((128, 128), F32),
+            pltpu.VMEM((16, 4, 128), F32),
+            dma((32,)), dma((32,)), dma((16,)), dma((16,)), dma((16,)), dma((16,)),
+            dma((32,)), dma((32,)),
+        ],
+        compiler_params=pltpu.CompilerParams(
+            collective_id=0, has_side_effects=True, vmem_limit_bytes=40 << 20
+        ),
+    )(density, jnp.asarray(high), jnp.asarray(low), jnp.asarray(lam.reshape(1, 512)),
+      jnp.asarray(lam.reshape(512, 1)), jnp.asarray(lam.reshape(4, 128)))
+
 
 RATIO = 4
 SWEEPS = 8
@@ -68,39 +369,7 @@
     cell_count = coarse_density.shape[2]
     coarse_rows = coarse_density.shape[0]
     coarse_cols = coarse_density.shape[1]
-    matrix = sine_table(cell_count)
-    whole_index = jnp.arange(cell_count, dtype=jnp.int32)
-
-    def along_first(block):
-        return jnp.einsum("abc,ad->dbc", block, matrix, precision=highest)
-
-    def along_second(block):
-        return jnp.einsum("abc,bd->adc", block, matrix, precision=highest)
-
-    def along_third(block):
-        return jnp.einsum("abc,cd->abd", block, matrix, precision=highest)
-
-    spectrum = along_third(coarse_density)
-    spectrum = along_second(
-        lax.all_to_all(spectrum, ("grp", "gy"), split_axis=2, concat_axis=1, tiled=True)
-    )
-    spectrum = along_first(lax.all_to_all(spectrum, "gx", split_axis=1, concat_axis=0, tiled=True))
-    index_second = lax.axis_index("gx") * spectrum.shape[1] + jnp.arange(
-        spectrum.shape[1], dtype=jnp.int32
-    )
-    index_third = lax.axis_index(("grp", "gy")) * spectrum.shape[2] + jnp.arange(
-        spectrum.shape[2], dtype=jnp.int32
-    )
-    divisor = (
-        eigen_values(whole_index, cell_count)[:, None, None]
-        + eigen_values(index_second, cell_count)[None, :, None]
-        + eigen_values(index_third, cell_count)[None, None, :]
-    )
-    spectrum = along_first(spectrum / divisor)
-    spectrum = along_second(lax.all_to_all(spectrum, "gx", split_axis=0, concat_axis=1, tiled=True))
-    potential = along_third(
-        lax.all_to_all(spectrum, ("grp", "gy"), split_axis=1, concat_axis=2, tiled=True)
-    )
+    potential = coarse(coarse_density)
     fine_rows, fine_cols, fine_depth = fine_start.shape
     total_x = fine_rows * lax.axis_size("gx")
     total_y = fine_cols * lax.axis_size("gy")

time: 685 us -> 511 us (0.75)
  the two profiles are of different devices: /device:TPU:58 before, /device:TPU:56 now
where the time goes in v1:
time: 511 us; the launch traced here: 510 us
  waiting for transfers between devices  291 us (57%)
  Pallas kernels  93.1 us (18%)
  starting transfers between devices  78.9 us (15%)
  between operations  18.1 us (4%)
  local copies, waits for them, and re-layouts  12.2 us (2%)
  matrix products  8.78 us (2%)
  other arithmetic  7.57 us (1%)
    psum x1, waiting for transfers between devices, body(): planes = lax.psum((partial_x, partial_y, partial_z), ('grp', 'gx', 'gy'))  241 us
    pallas_call x1, Pallas kernels, coarse(): pl.pallas_call(coarse_kernel, out_shape=jax.ShapeDtypeStruct((32, 16, 512...  93.1 us
    ppermute x15, starting transfers between devices, with_halo(): lax.ppermute(lax.slice_in_dim(block, block.shape[dim] - width, None, axis...  52.1 us
    ppermute x15, waiting for transfers between devices, with_halo(): lax.ppermute(lax.slice_in_dim(block, 0, width, axis=dim), axis, backward)  48.2 us
    ppermute x15, starting transfers between devices, with_halo(): lax.ppermute(lax.slice_in_dim(block, 0, width, axis=dim), axis, backward)  26.7 us
  transfers between devices with their start and end apart: 31, of which 13 were waited for; matrix products, arithmetic and copies ran while one was open for 3% of the time, Pallas kernels for 18%

profile of v1, /device:TPU:56, one launch (start us, length us, event | category | flops | bytes accessed | tf_op | source)
XLA Modules:
  0.0 509.5 jit_solution(15104868922365606143)
XLA Ops:
  7.2 1.1 fusion.150
  8.4 1.7 collective-permute-start
  10.1 1.3 collective-permute-start.1
  11.5 1.1 fusion.149
  12.6 3.2 collective-permute-start.6
  15.7 1.3 collective-permute-start.7
  21.9 93.1 %shard_map.131 = f32[32,16,512]{2,1,0:T(8,128)S(1)} custom-call(f32[32,16,512]{2,1,0:T(8,128)S(1)} %copy-done, bf16[512,512]{1,0:T(8,128)(2,1)S(1)} %copy-done.1, bf16[512,512]{1,0:T(8,128)(2,1)S(1)} %copy-done.2, f32[1,512]{1,0:T(1,128)S(1)} %copy-done.4, f32[512,1]{1,0:T(8,128)S(1)} %copy-done.3, f32[4,128]{1,0:T(4,128)S(1)} %copy-done.5), custom_call_target="tpu_custom_call" | custom-call | tf_op jit(solution)/shard_map/pallas_call | solution.py:289
  114.9 1.2 fusion.2
  116.6 1.2 copy.42
  121.2 2.5 fusion
  126.7 2.8 collective-permute-start.2
  129.4 1.3 collective-permute-start.3
  130.9 4.5 collective-permute-start.8
  135.4 1.3 collective-permute-start.9
  136.9 7.3 %collective-permute-start.4 = (f32[12,2,132]{2,1,0:T(2,128)S(1)}, f32[12,2,132]{2,1,0:T(2,128)S(1)}, u32[]{:S(2)}, u32[]{:S(2)}) collective-permute-start(f32[12,2,132]{2,1,0:T(2,128)S(1)} %get-tuple-element.13), channel_id=1, source_target_pairs={{0,1},{1,2},{2,3},{3,4},{4,5},{5,6},{6,7},{7,8},{8,9},{9,10},{10,1... | collective-permute-start | bytes 38024 | tf_op jit(solution)/shard_map/ppermute | solution.py:321
  144.2 1.9 collective-permute-start.5
  146.2 9.9 %collective-permute-start.10 = (f32[10,1,130]{2,1,0:T(1,128)S(1)}, f32[10,1,130]{2,1,0:T(1,128)S(1)}, u32[]{:S(2)}, u32[]{:S(2)}) collective-permute-start(f32[10,1,130]{2,1,0:T(1,128)S(1)} %get-tuple-element.15), channel_id=1, source_target_pairs={{0,1},{1,2},{2,3},{3,4},{4,5},{5,6},{6,7},{7,8},{8,9},{9,10},{10,1... | collective-permute-start | bytes 15608 | tf_op jit(solution)/shard_map/ppermute | solution.py:321
  156.2 2.1 collective-permute-start.11
  158.5 241.0 %all-reduce.3.cloned.1.call-done = (f32[2,34,512]{2,1,0:T(8,128)}, f32[2,34,512]{2,0,1:T(2,128)}, f32[2,130,512]{2,0,1:T(2,128)}) async-done(((f32[2,34,512]{2,1,0:T(8,128)}, f32[2,34,512]{2,0,1:T(2,128)}, f32[2,130,512]{2,0,1:T(2,128)}), (f32[2,34,512]{2,1,0:T(8,128)}, f32[2,34,512]{2,0,1:T(2,128)}, f32[2,130,512]{2,0,1:T(2,128)})) %all-reduce.3.cloned.1.call-update) | async-done | bytes 811024 | tf_op jit(solution)/shard_map/psum | solution.py:399
  399.5 1.2 constant_dynamic-slice_fusion.1
  404.3 1.1 and_select_fusion.3
  405.8 1.3 collective-permute-start.12
  407.1 1.3 collective-permute-start.13
  408.5 1.9 collective-permute-done.13
  410.5 1.6 collective-permute-start.14
  412.1 1.3 collective-permute-start.15
  414.0 5.7 %collective-permute-done.15 = f32[2,32,132]{2,1,0:T(8,128)S(1)} collective-permute-done((f32[2,32,132]{2,1,0:T(8,128)S(1)}, f32[2,32,132]{2,1,0:T(8,128)S(1)}, u32[]{:S(2)}, u32[]{:S(2)}) %collective-permute-start.15) | collective-permute-done | bytes 33824 | tf_op jit(solution)/shard_map/ppermute | solution.py:324
  419.8 5.9 %collective-permute-start.16 = (f32[12,2,132]{2,1,0:T(2,128)S(1)}, f32[12,2,132]{2,1,0:T(2,128)S(1)}, u32[]{:S(2)}, u32[]{:S(2)}) collective-permute-start(f32[12,2,132]{2,1,0:T(2,128)S(1)} %get-tuple-element.11), channel_id=1, source_target_pairs={{0,1},{1,2},{2,3},{3,4},{4,5},{5,6},{6,7},{7,8},{8,9},{9,10},{10,1... | collective-permute-start | bytes 38024 | tf_op jit(solution)/shard_map/ppermute | solution.py:321
  425.7 1.9 collective-permute-start.17
  427.6 9.8 %collective-permute-done.17 = f32[12,2,132]{2,1,0:T(2,128)S(1)} collective-permute-done((f32[12,2,132]{2,1,0:T(2,128)S(1)}, f32[12,2,132]{2,1,0:T(2,128)S(1)}, u32[]{:S(2)}, u32[]{:S(2)}) %collective-permute-start.17) | collective-permute-done | bytes 12704 | tf_op jit(solution)/shard_map/ppermute | solution.py:324
  438.8 1.3 collective-permute-start.18
  440.1 1.3 collective-permute-start.19
  441.4 1.9 collective-permute-done.19
  443.5 3.1 collective-permute-start.20
  446.6 1.3 collective-permute-start.21
  448.5 5.7 %collective-permute-done.21 = f32[2,32,132]{2,1,0:T(8,128)S(1)} collective-permute-done((f32[2,32,132]{2,1,0:T(8,128)S(1)}, f32[2,32,132]{2,1,0:T(8,128)S(1)}, u32[]{:S(2)}, u32[]{:S(2)}) %collective-permute-start.21) | collective-permute-done | bytes 33824 | tf_op jit(solution)/shard_map/ppermute | solution.py:324
  454.3 1.9 collective-permute-start.22
  456.2 3.9 collective-permute-start.23
  460.1 7.9 %collective-permute-done.23 = f32[12,2,132]{2,1,0:T(2,128)S(1)} collective-permute-done((f32[12,2,132]{2,1,0:T(2,128)S(1)}, f32[12,2,132]{2,1,0:T(2,128)S(1)}, u32[]{:S(2)}, u32[]{:S(2)}) %collective-permute-start.23) | collective-permute-done | bytes 12704 | tf_op jit(solution)/shard_map/ppermute | solution.py:324
  469.5 1.3 collective-permute-start.24
  470.8 1.3 collective-permute-start.25
  472.1 1.9 collective-permute-done.25
  474.2 4.4 collective-permute-start.26
  478.6 1.3 collective-permute-start.27
  480.4 5.5 %collective-permute-done.27 = f32[2,32,132]{2,1,0:T(8,128)S(1)} collective-permute-done((f32[2,32,132]{2,1,0:T(8,128)S(1)}, f32[2,32,132]{2,1,0:T(8,128)S(1)}, u32[]{:S(2)}, u32[]{:S(2)}) %collective-permute-start.27) | collective-permute-done | bytes 33824 | tf_op jit(solution)/shard_map/ppermute | solution.py:324
  486.1 1.9 collective-permute-start.28
  488.0 3.9 collective-permute-start.29
  491.9 7.8 %collective-permute-done.29 = f32[12,2,132]{2,1,0:T(2,128)S(1)} collective-permute-done((f32[12,2,132]{2,1,0:T(2,128)S(1)}, f32[12,2,132]{2,1,0:T(2,128)S(1)}, u32[]{:S(2)}, u32[]{:S(2)}) %collective-permute-start.29) | collective-permute-done | bytes 12704 | tf_op jit(solution)/shard_map/ppermute | solution.py:324
  (120 shorter events, 21.1 us)
Async XLA Ops:
  7.2 12.1 %copy-start = (f32[32,16,512]{2,1,0:T(8,128)S(1)}, f32[32,16,512]{2,1,0:T(8,128)}, u32[]{:S(2)}) copy-start(f32[32,16,512]{2,1,0:T(8,128)} %x_ref.1) | copy-start | bytes 3145732
  7.2 392.3 %all-reduce.3.cloned.1.call-start = ((), (), s32[]{:S(2)}) async-start(), calls=%async_computation | async-start | bytes 1671168 | tf_op jit(solution)/shard_map/psum | solution.py:399
  8.4 118.1 %collective-permute-start = (f32[8,32,2]{2,1,0:T(8,128)S(1)}, f32[8,32,2]{2,1,0:T(8,128)S(1)}, u32[]{:S(2)}, u32[]{:S(2)}) collective-permute-start(f32[8,32,2]{2,1,0:T(8,128)S(1)} %get-tuple-element.35), channel_id=1, source_target_pairs={{0,256},{1,257},{2,258},{3,259},{4,260},{5,261},{6,262},{7,263},{8... | collective-permute-start | bytes 6152 | tf_op jit(solution)/shard_map/ppermute | solution.py:321
  10.1 116.4 %collective-permute-start.1 = (f32[8,32,2]{2,1,0:T(8,128)S(1)}, f32[8,32,2]{2,1,0:T(8,128)S(1)}, u32[]{:S(2)}, u32[]{:S(2)}) collective-permute-start(f32[8,32,2]{2,1,0:T(8,128)S(1)} %get-tuple-element.36), channel_id=1, source_target_pairs={{256,0},{257,1},{258,2},{259,3},{260,4},{261,5},{262,6},{263,7},{2... | collective-permute-start | bytes 6152 | tf_op jit(solution)/shard_map/ppermute | solution.py:324
  11.4 5.7 %copy-start.8 = (s32[3]{0:T(128)S(1)}, s32[3]{0:T(128)}, u32[]{:S(2)}) copy-start(s32[3]{0:T(128)} %param.15) | copy-start | bytes 40
  11.4 7.6 %copy-start.10 = (f32[2]{0:T(128)S(1)}, f32[2]{0:T(128)}, u32[]{:S(2)}) copy-start(f32[2]{0:T(128)} %constant.259) | copy-start | bytes 28
  11.4 7.6 %copy-start.11 = (f32[2]{0:T(128)S(1)}, f32[2]{0:T(128)}, u32[]{:S(2)}) copy-start(f32[2]{0:T(128)} %constant.260) | copy-start | bytes 28
  11.5 7.6 %copy-start.14 = (s32[2]{0:T(128)S(1)}, s32[2]{0:T(128)}, u32[]{:S(2)}) copy-start(s32[2]{0:T(128)} %constant.261) | copy-start | bytes 28
  12.6 6.7 %copy-start.3 = (f32[512,1]{1,0:T(8,128)S(1)}, f32[512,1]{1,0:T(8,128)}, u32[]{:S(2)}) copy-start(f32[512,1]{1,0:T(8,128)} %constant.229.clone.lamc_ref) | copy-start | bytes 6148
  12.6 118.2 %collective-permute-start.6 = (f32[8,32,1]{2,1,0:T(8,128)S(1)}, f32[8,32,1]{2,1,0:T(8,128)S(1)}, u32[]{:S(2)}, u32[]{:S(2)}) collective-permute-start(f32[8,32,1]{2,1,0:T(8,128)S(1)} %get-tuple-element.33), channel_id=1, source_target_pairs={{0,256},{1,257},{2,258},{3,259},{4,260},{5,261},{6,262},{7,263},{8... | collective-permute-start | bytes 3080 | tf_op jit(solution)/shard_map/ppermute | solution.py:321
  15.7 115.0 %collective-permute-start.7 = (f32[8,32,1]{2,1,0:T(8,128)S(1)}, f32[8,32,1]{2,1,0:T(8,128)S(1)}, u32[]{:S(2)}, u32[]{:S(2)}) collective-permute-start(f32[8,32,1]{2,1,0:T(8,128)S(1)} %get-tuple-element.34), channel_id=1, source_target_pairs={{256,0},{257,1},{258,2},{259,3},{260,4},{261,5},{262,6},{263,7},{2... | collective-permute-start | bytes 3080 | tf_op jit(solution)/shard_map/ppermute | solution.py:324
  19.1 0.7 copy-start.4
  19.1 0.7 copy-start.5
  19.8 1.0 copy-start.1
  20.8 1.0 copy-start.2
  116.6 1.2 copy-start.13
  120.3 0.7 copy-start.12
  125.0 1.6 copy-start.6
  126.5 4.3 copy-start.7
  126.7 10.1 %collective-permute-start.2 = (f32[2,32,132]{2,1,0:T(8,128)S(1)}, f32[2,32,132]{2,1,0:T(8,128)S(1)}, u32[]{:S(2)}, u32[]{:S(2)}) collective-permute-start(f32[2,32,132]{2,1,0:T(8,128)S(1)} %get-tuple-element.25), channel_id=1, source_target_pairs={{0,16},{16,32},{32,48},{48,64},{64,80},{80,96},{96,112},{112,128},... | collective-permute-start | bytes 101384 | tf_op jit(solution)/shard_map/ppermute | solution.py:321
  129.4 7.3 %collective-permute-start.3 = (f32[2,32,132]{2,1,0:T(8,128)S(1)}, f32[2,32,132]{2,1,0:T(8,128)S(1)}, u32[]{:S(2)}, u32[]{:S(2)}) collective-permute-start(f32[2,32,132]{2,1,0:T(8,128)S(1)} %get-tuple-element.26), channel_id=1, source_target_pairs={{16,0},{32,16},{48,32},{64,48},{80,64},{96,80},{112,96},{128,112},... | collective-permute-start | bytes 101384 | tf_op jit(solution)/shard_map/ppermute | solution.py:324
  130.9 15.2 %collective-permute-start.8 = (f32[1,32,130]{2,1,0:T(8,128)S(1)}, f32[1,32,130]{2,1,0:T(8,128)S(1)}, u32[]{:S(2)}, u32[]{:S(2)}) collective-permute-start(f32[1,32,130]{2,1,0:T(8,128)S(1)} %get-tuple-element.23), channel_id=1, source_target_pairs={{0,16},{16,32},{32,48},{48,64},{64,80},{80,96},{96,112},{112,128},... | collective-permute-start | bytes 49928 | tf_op jit(solution)/shard_map/ppermute | solution.py:321
  135.4 10.7 %collective-permute-start.9 = (f32[1,32,130]{2,1,0:T(8,128)S(1)}, f32[1,32,130]{2,1,0:T(8,128)S(1)}, u32[]{:S(2)}, u32[]{:S(2)}) collective-permute-start(f32[1,32,130]{2,1,0:T(8,128)S(1)} %get-tuple-element.24), channel_id=1, source_target_pairs={{16,0},{32,16},{48,32},{64,48},{80,64},{96,80},{112,96},{128,112},... | collective-permute-start | bytes 49928 | tf_op jit(solution)/shard_map/ppermute | solution.py:324
  136.9 21.4 %collective-permute-start.4 = (f32[12,2,132]{2,1,0:T(2,128)S(1)}, f32[12,2,132]{2,1,0:T(2,128)S(1)}, u32[]{:S(2)}, u32[]{:S(2)}) collective-permute-start(f32[12,2,132]{2,1,0:T(2,128)S(1)} %get-tuple-element.13), channel_id=1, source_target_pairs={{0,1},{1,2},{2,3},{3,4},{4,5},{5,6},{6,7},{7,8},{8,9},{9,10},{10,1... | collective-permute-start | bytes 38024 | tf_op jit(solution)/shard_map/ppermute | solution.py:321
  144.2 14.1 %collective-permute-start.5 = (f32[12,2,132]{2,1,0:T(2,128)S(1)}, f32[12,2,132]{2,1,0:T(2,128)S(1)}, u32[]{:S(2)}, u32[]{:S(2)}) collective-permute-start(f32[12,2,132]{2,1,0:T(2,128)S(1)} %get-tuple-element.14), channel_id=1, source_target_pairs={{1,0},{2,1},{3,2},{4,3},{5,4},{6,5},{7,6},{8,7},{9,8},{10,9},{11,1... | collective-permute-start | bytes 38024 | tf_op jit(solution)/shard_map/ppermute | solution.py:324
  146.2 258.0 %collective-permute-start.10 = (f32[10,1,130]{2,1,0:T(1,128)S(1)}, f32[10,1,130]{2,1,0:T(1,128)S(1)}, u32[]{:S(2)}, u32[]{:S(2)}) collective-permute-start(f32[10,1,130]{2,1,0:T(1,128)S(1)} %get-tuple-element.15), channel_id=1, source_target_pairs={{0,1},{1,2},{2,3},{3,4},{4,5},{5,6},{6,7},{7,8},{8,9},{9,10},{10,1... | collective-permute-start | bytes 15608 | tf_op jit(solution)/shard_map/ppermute | solution.py:321
  156.2 248.1 %collective-permute-start.11 = (f32[10,1,130]{2,1,0:T(1,128)S(1)}, f32[10,1,130]{2,1,0:T(1,128)S(1)}, u32[]{:S(2)}, u32[]{:S(2)}) collective-permute-start(f32[10,1,130]{2,1,0:T(1,128)S(1)} %get-tuple-element.16), channel_id=1, source_target_pairs={{1,0},{2,1},{3,2},{4,3},{5,4},{6,5},{7,6},{8,7},{9,8},{10,9},{11,1... | collective-permute-start | bytes 15608 | tf_op jit(solution)/shard_map/ppermute | solution.py:324
  402.9 0.9 copy-start.9
  405.8 2.6 collective-permute-start.12
  407.1 3.2 collective-permute-start.13
  410.5 3.5 collective-permute-start.14
  412.1 7.6 %collective-permute-start.15 = (f32[2,32,132]{2,1,0:T(8,128)S(1)}, f32[2,32,132]{2,1,0:T(8,128)S(1)}, u32[]{:S(2)}, u32[]{:S(2)}) collective-permute-start(f32[2,32,132]{2,1,0:T(8,128)S(1)} %get-tuple-element.22), channel_id=1, source_target_pairs={{16,0},{32,16},{48,32},{64,48},{80,64},{96,80},{112,96},{128,112},... | collective-permute-start | bytes 101384 | tf_op jit(solution)/shard_map/ppermute | solution.py:324
  419.8 7.8 %collective-permute-start.16 = (f32[12,2,132]{2,1,0:T(2,128)S(1)}, f32[12,2,132]{2,1,0:T(2,128)S(1)}, u32[]{:S(2)}, u32[]{:S(2)}) collective-permute-start(f32[12,2,132]{2,1,0:T(2,128)S(1)} %get-tuple-element.11), channel_id=1, source_target_pairs={{0,1},{1,2},{2,3},{3,4},{4,5},{5,6},{6,7},{7,8},{8,9},{9,10},{10,1... | collective-permute-start | bytes 38024 | tf_op jit(solution)/shard_map/ppermute | solution.py:321
  425.7 11.7 %collective-permute-start.17 = (f32[12,2,132]{2,1,0:T(2,128)S(1)}, f32[12,2,132]{2,1,0:T(2,128)S(1)}, u32[]{:S(2)}, u32[]{:S(2)}) collective-permute-start(f32[12,2,132]{2,1,0:T(2,128)S(1)} %get-tuple-element.12), channel_id=1, source_target_pairs={{1,0},{2,1},{3,2},{4,3},{5,4},{6,5},{7,6},{8,7},{9,8},{10,9},{11,1... | collective-permute-start | bytes 38024 | tf_op jit(solution)/shard_map/ppermute | solution.py:324
  438.8 2.6 collective-permute-start.18
  440.1 3.2 collective-permute-start.19
  443.5 5.0 collective-permute-start.20
  446.6 7.6 %collective-permute-start.21 = (f32[2,32,132]{2,1,0:T(8,128)S(1)}, f32[2,32,132]{2,1,0:T(8,128)S(1)}, u32[]{:S(2)}, u32[]{:S(2)}) collective-permute-start(f32[2,32,132]{2,1,0:T(8,128)S(1)} %get-tuple-element.20), channel_id=1, source_target_pairs={{16,0},{32,16},{48,32},{64,48},{80,64},{96,80},{112,96},{128,112},... | collective-permute-start | bytes 101384 | tf_op jit(solution)/shard_map/ppermute | solution.py:324
  454.3 5.9 %collective-permute-start.22 = (f32[12,2,132]{2,1,0:T(2,128)S(1)}, f32[12,2,132]{2,1,0:T(2,128)S(1)}, u32[]{:S(2)}, u32[]{:S(2)}) collective-permute-start(f32[12,2,132]{2,1,0:T(2,128)S(1)} %get-tuple-element.9), channel_id=1, source_target_pairs={{0,1},{1,2},{2,3},{3,4},{4,5},{5,6},{6,7},{7,8},{8,9},{9,10},{10,1... | collective-permute-start | bytes 38024 | tf_op jit(solution)/shard_map/ppermute | solution.py:321
  456.2 11.9 %collective-permute-start.23 = (f32[12,2,132]{2,1,0:T(2,128)S(1)}, f32[12,2,132]{2,1,0:T(2,128)S(1)}, u32[]{:S(2)}, u32[]{:S(2)}) collective-permute-start(f32[12,2,132]{2,1,0:T(2,128)S(1)} %get-tuple-element.10), channel_id=1, source_target_pairs={{1,0},{2,1},{3,2},{4,3},{5,4},{6,5},{7,6},{8,7},{9,8},{10,9},{11,1... | collective-permute-start | bytes 38024 | tf_op jit(solution)/shard_map/ppermute | solution.py:324
  469.5 2.6 collective-permute-start.24
  470.8 3.2 collective-permute-start.25
  474.2 6.3 %collective-permute-start.26 = (f32[2,32,132]{2,1,0:T(8,128)S(1)}, f32[2,32,132]{2,1,0:T(8,128)S(1)}, u32[]{:S(2)}, u32[]{:S(2)}) collective-permute-start(f32[2,32,132]{2,1,0:T(8,128)S(1)} %get-tuple-element.17), channel_id=1, source_target_pairs={{0,16},{16,32},{32,48},{48,64},{64,80},{80,96},{96,112},{112,128},... | collective-permute-start | bytes 101384 | tf_op jit(solution)/shard_map/ppermute | solution.py:321
  478.6 7.4 %collective-permute-start.27 = (f32[2,32,132]{2,1,0:T(8,128)S(1)}, f32[2,32,132]{2,1,0:T(8,128)S(1)}, u32[]{:S(2)}, u32[]{:S(2)}) collective-permute-start(f32[2,32,132]{2,1,0:T(8,128)S(1)} %get-tuple-element.18), channel_id=1, source_target_pairs={{16,0},{32,16},{48,32},{64,48},{80,64},{96,80},{112,96},{128,112},... | collective-permute-start | bytes 101384 | tf_op jit(solution)/shard_map/ppermute | solution.py:324
  486.1 5.9 %collective-permute-start.28 = (f32[12,2,132]{2,1,0:T(2,128)S(1)}, f32[12,2,132]{2,1,0:T(2,128)S(1)}, u32[]{:S(2)}, u32[]{:S(2)}) collective-permute-start(f32[12,2,132]{2,1,0:T(2,128)S(1)} %get-tuple-element.7), channel_id=1, source_target_pairs={{0,1},{1,2},{2,3},{3,4},{4,5},{5,6},{6,7},{7,8},{8,9},{9,10},{10,1... | collective-permute-start | bytes 38024 | tf_op jit(solution)/shard_map/ppermute | solution.py:321
  488.0 11.7 %collective-permute-start.29 = (f32[12,2,132]{2,1,0:T(2,128)S(1)}, f32[12,2,132]{2,1,0:T(2,128)S(1)}, u32[]{:S(2)}, u32[]{:S(2)}) collective-permute-start(f32[12,2,132]{2,1,0:T(2,128)S(1)} %get-tuple-element.8), channel_id=1, source_target_pairs={{1,0},{2,1},{3,2},{4,3},{5,4},{6,5},{7,6},{8,7},{9,8},{10,9},{11,1... | collective-permute-start | bytes 38024 | tf_op jit(solution)/shard_map/ppermute | solution.py:324
Sparse Core Ops, SparseCore 0:
  125.1 274.3 all-reduce.2

commit v2 on v1

v2 whole, which is shorter than its diff:
```python
import functools
import math

import jax
import jax.numpy as jnp
import numpy as np
from jax import lax
from jax.experimental import pallas as pl
from jax.experimental.pallas import tpu as pltpu
from jax.sharding import PartitionSpec as P

MESH = pl.DeviceIdType.MESH
NC = 512
F32 = jnp.float32
BF16 = jnp.bfloat16


def tables():
    index = np.arange(1, NC + 1, dtype=np.int64)
    angle = (index[:, None] * index[None, :]) % (2 * (NC + 1))
    sine = math.sqrt(2.0 / (NC + 1)) * np.sin(angle * (math.pi / (NC + 1)))
    sine = sine.astype(np.float32)
    high = sine.astype(jnp.bfloat16)
    low = (sine - high.astype(np.float32)).astype(jnp.bfloat16)
    lam = 4.0 * np.sin(index * (math.pi / (2 * (NC + 1)))) ** 2
    return high, low, lam.astype(np.float32)


def split(value):
    high = value.astype(BF16)
    low = (value - high.astype(F32)).astype(BF16)
    return high, low


def dot3(a, b, dims):
    ah, al = a
    bh, bl = b
    dd = functools.partial(
        lax.dot_general, dimension_numbers=(dims, ((), ())), preferred_element_type=F32
    )
    return dd(ah, bh) + (dd(al, bh) + dd(ah, bl))


def mm(a, b, dims):
    return lax.dot_general(a, b, (dims, ((), ())), preferred_element_type=F32)


def full(a, b, dims):
    return lax.dot_general(
        a, b, (dims, ((), ())), precision=lax.Precision.HIGHEST, preferred_element_type=F32
    )


NN = ((1,), (0,))
NT = ((1,), (1,))
TN = ((0,), (0,))


def exchange(v, lane):
    v = list(v)
    for bit in (1, 2, 4):
        upper = (lane & bit) != 0
        for i in range(8):
            if i & bit:
                continue
            a, c = v[i], v[i | bit]
            v[i] = jnp.where(upper, pltpu.roll(c, 16 * bit, 1), a)
            v[i | bit] = jnp.where(upper, c, pltpu.roll(a, 128 - 16 * bit, 1))
    return v


def swap_groups(source, target):
    lane = lax.broadcasted_iota(jnp.int32, (8, 128), 1) // 16

    def step(index, carry):
        at = index // 8
        bt = (index // 2) % 4
        row = pl.multiple_of((index % 2) * 8, 8)
        cols = pl.ds(pl.multiple_of(bt * 128, 128), 128)
        outs = pl.ds(pl.multiple_of(at * 128, 128), 128)
        v = [source[at * 8 + q, pl.ds(row, 8), cols] for q in range(8)]
        v = exchange(v, lane)
        for q in range(8):
            target[bt * 8 + q, pl.ds(row, 8), outs] = v[q]
        return carry

    lax.fori_loop(0, 32, step, 0)


def device(core, x, y, z):
    return (core, x * 4 + z % 4, (z // 4) * 8 + y)


ORDER = [
    (dy, side, core) for dy in (4, 3, 5, 2, 6, 1, 7, 0) for side in (0, 1) for core in (0, 1)
]


def shuffled():
    return list(ORDER[i] for i in np.random.RandomState(3).permutation(len(ORDER)))


def kernel(
    anchor, x_ref, fd_ref, fs_ref, sh_ref, sl_ref, lamr_ref, lamc_ref, lamq_ref, out_ref, fine_ref,
    za, zb, dd, u, dtab, m1, r1, m2, r2, dint, uh, ul, myh, myl, mz, mzth, mztl, wall, wys,
    mzx, rzx, my, ry, m5, r5, m6, r6, es, et, ed,
    s1, q1, s2, q2, s3, q3, s4, q4, sh1, qh1, sd, qd, sz, qz, sy, qy, s5, q5, s6, q6,
):
    core = lax.axis_index("grp")
    gx = lax.axis_index("gx")
    gy = lax.axis_index("gy")
    x, zl = gx // 4, gx % 4
    y, zh = gy % 8, gy // 8
    z = zh * 4 + zl
    me = core * 16 + gy
    zv = (z + 6) % 8
    lv, hv = zv % 4, zv // 4
    mid = core * 16 + hv * 8 + y
    pv = x * 4 + lv

    def to_mid(o):
        dy, side, oc = o
        ty = (y + dy) % 8
        tc = (core + oc) % 2
        return device(tc, x, ty, (zl + 4 * side + 2) % 8), tc * 16 + side * 8 + ty

    def to_real(o):
        dy, side, oc = o
        ty = (y + dy) % 8
        tc = (core + oc) % 2
        return device(tc, x, ty, lv + 4 * side), tc * 16 + side * 8 + ty

    def to_row(q):
        return device(core, q // 4, y, (q % 4 + 4 * hv + 2) % 8)

    def real_row(q):
        return device(core, q // 4, y, q % 4 + 4 * zh)

    here = (core, gx, gy)
    partner = (1 - core, gx, gy)
    own = pl.ds(pl.multiple_of(core * 128, 128), 128)
    sides = [(ox, oy) for ox in (-1, 0, 1) for oy in (-1, 0, 1) if (ox, oy) != (0, 0)]

    def beside(ox, oy):
        return (core, (gx + ox + 16) % 16, (gy + oy + 16) % 16)

    a0, a1, a2 = anchor[0], anchor[1], anchor[2]
    barrier = pltpu.get_barrier_semaphore()
    pl.semaphore_signal(barrier, inc=1, device_id=partner, device_id_type=MESH)
    for side in sides:
        pl.semaphore_signal(barrier, inc=1, device_id=beside(*side), device_id_type=MESH)
    for k in range(1, 16):
        pl.semaphore_signal(
            barrier, inc=1, device_id=real_row((gx + k) % 16), device_id_type=MESH
        )
    peers = shuffled()
    for o in peers:
        pl.semaphore_signal(barrier, inc=1, device_id=to_mid(o)[0], device_id_type=MESH)
    for k in range(1, 16):
        pl.semaphore_signal(barrier, inc=1, device_id=to_row((pv + k) % 16), device_id_type=MESH)

    s_pair = (sh_ref[...], sl_ref[...])
    value = x_ref[...].reshape(512, 512)
    za[...] = dot3(split(value), s_pair, NN).reshape(32, 16, 512)
    swap_groups(za, zb)

    pl.semaphore_wait(barrier, 71)

    t1 = []
    for i, o in enumerate(peers):
        target, block = to_mid(o)
        copy = pltpu.make_async_remote_copy(
            src_ref=zb.at[block], dst_ref=dd.at[me], send_sem=s1.at[i], recv_sem=q1.at[me],
            device_id=target, device_id_type=MESH,
        )
        copy.start()
        t1.append(copy)

    es[8:16, 8:40, own] = fs_ref[...]
    ed[8:16, 8:40, own] = fd_ref[...]
    halo = []
    for k, (ox, oy) in enumerate(sides):
        rows = {-1: pl.ds(0, 8), 0: pl.ds(0, 32), 1: pl.ds(24, 8)}[oy]
        to_rows = {-1: pl.ds(40, 8), 0: pl.ds(8, 32), 1: pl.ds(0, 8)}[oy]
        layers = {-1: pl.ds(16, 8), 0: pl.ds(8, 8), 1: pl.ds(0, 8)}[ox]
        for part, (src, dst) in enumerate(((fs_ref, es), (fd_ref, ed))):
            copy = pltpu.make_async_remote_copy(
                src_ref=src.at[:, rows, :], dst_ref=dst.at[layers, to_rows, own],
                send_sem=sh1.at[2 * k + part], recv_sem=qh1.at[2 * k + part],
                device_id=beside(ox, oy), device_id_type=MESH,
            )
            copy.start()
            halo.append(copy)

    def face_tables():
        def cells(rows, cols, first):
            grid = lax.broadcasted_iota(jnp.int32, (rows, cols), 0)
            return jnp.where(grid == first, 1.0, 0.0).astype(BF16)

        lane = lax.broadcasted_iota(jnp.int32, (512, 256), 1)
        pick = cells(512, 256, a1 - 3 + 8 * (lane // 16) + lane % 16)
        myh[...] = mm(sh_ref[...], pick, NN).astype(BF16)
        myl[...] = mm(sl_ref[...], pick, NN).astype(BF16)
        lane = lax.broadcasted_iota(jnp.int32, (512, 128), 1)
        pick = cells(512, 128, a2 - 1 + 30 * core + lane)
        mz[...] = (mm(sh_ref[...], pick, NN) + mm(sl_ref[...], pick, NN)).reshape(32, 16, 128)
        pick = cells(512, 128, a2 - 1 + 30 * (lane // 64) + lane % 64)
        mine = pl.ds(pl.multiple_of(mid * 16, 16), 16)
        high = mm(sh_ref[mine, :], pick, NN).astype(BF16)
        low = mm(sl_ref[mine, :], pick, NN).astype(BF16)
        mzth[...] = jnp.concatenate([high] * 32, axis=0)
        mztl[...] = jnp.concatenate([low] * 32, axis=0)

        def weights(cell, first, boxes, low_face, high_face):
            low_w = jnp.where(cell == first, 0.625, 0.0) + jnp.where(cell == first + 1, 0.375, 0.0)
            high_w = jnp.where(cell == first + boxes, 0.375, 0.0) + jnp.where(
                cell == first + boxes + 1, 0.625, 0.0
            )
            return jnp.where(low_face, low_w, 0.0) + jnp.where(high_face, high_w, 0.0)

        row = lax.broadcasted_iota(jnp.int32, (16, 512), 0)
        cell = lax.broadcasted_iota(jnp.int32, (16, 512), 1)
        wy = weights(cell, a1 - 1, 128, row == 0, row == 1).astype(BF16)
        wys[...] = mm(wy, sh_ref[...], NN) + mm(wy, sl_ref[...], NN)
        wz = weights(cell, a2 - 1, 64, row == 0, row == 1).astype(BF16)
        wz = mm(wz, sh_ref[...], NN) + mm(wz, sl_ref[...], NN)
        lane = lax.broadcasted_iota(jnp.int32, (512, 512), 1)
        pick = cells(512, 512, mid * 16 + lane % 16)
        wzh, wzl = split(wz)
        wz = mm(wzh, pick, NN) + mm(wzl, pick, NN)
        row = lax.broadcasted_iota(jnp.int32, (32, 512), 0)
        lane = lax.broadcasted_iota(jnp.int32, (32, 512), 1)
        for f in range(2):
            wall[32 * f : 32 * f + 32, :] = jnp.where(row == lane // 16, wz[f : f + 1, :], 0.0)
        wx = weights(32 * pv + lane // 16, a0 - 1, 32, row < 16, row >= 16)
        wall[64:96, :] = jnp.where(row % 16 == lane % 16, wx, 0.0)

    mu = lamr_ref[...] + lamc_ref[pl.ds(pl.multiple_of(mid * 16, 16), 16), :]

    def table(i, g):
        d = 1.0 / (1.0 + (mu + g))
        dtab[i] = d
        return (mu + g) * d

    lax.fori_loop(0, 31, table, jnp.ones((16, 512), F32))
    muq = lamq_ref[...] + lamc_ref[pl.ds(mid * 16 + pv, 1), :]
    c = 0.5 * muq
    c1 = c
    r32 = 2.0 * (1.0 + c)
    for _ in range(4):
        c = 2.0 * c * (c + 2.0)
        r32 = r32 * (2.0 * (1.0 + c))
    c = 2.0 * c * (c + 2.0)
    g = jnp.ones((4, 128), F32)
    for i in range(15):
        d = 1.0 / (1.0 + (2.0 * c + g))
        dint[i] = d
        g = (2.0 * c + g) * d
    dint[15] = 1.0 / (r32 * (1.0 + c1) + c + g)

    face_tables()
    for s in range(32):
        pltpu.make_async_remote_copy(
            src_ref=dd.at[s], dst_ref=dd.at[s], send_sem=s1.at[s], recv_sem=q1.at[s],
            device_id=(core, gx, gy), device_id_type=MESH,
        ).wait_recv()

    value = dd[...].reshape(512, 512)
    u[...] = dot3(split(value), s_pair, TN).reshape(32, 16, 512)

    first = -u[0]
    u[0] = first
    q0 = dtab[30]

    def forward(i, carry):
        yv, q, e = carry
        w = u[i]
        yv = dtab[i - 1] * yv - w
        u[i] = yv
        q = q * dtab[30 - i]
        return yv, q, e - q * w

    yv, _, e = lax.fori_loop(1, 31, forward, (first, q0, q0 * first))
    b = q0 * yv - u[31]
    for j in range(4):
        m1[pl.ds(j, 16, stride=8), :] = e[:, 128 * j : 128 * j + 128]
        m1[pl.ds(4 + j, 16, stride=8), :] = b[:, 128 * j : 128 * j + 128]
    t2 = []
    for k in range(1, 16):
        q = (pv + k) % 16
        copy = pltpu.make_async_remote_copy(
            src_ref=m1.at[pl.ds(pl.multiple_of(q * 8, 8), 8), :], dst_ref=r1.at[pv],
            send_sem=s2.at[k], recv_sem=q2.at[pv], device_id=to_row(q), device_id_type=MESH,
        )
        copy.start()
        t2.append(copy)
    for copy in halo:
        copy.wait_recv()
    pair = []
    for k, ref in enumerate((es, ed)):
        copy = pltpu.make_async_remote_copy(
            src_ref=ref.at[:, :, own], dst_ref=ref.at[:, :, own], send_sem=sd.at[k],
            recv_sem=qd.at[k], device_id=partner, device_id_type=MESH,
        )
        copy.start()
        pair.append(copy)
    r1[pv] = m1[pl.ds(pl.multiple_of(pv * 8, 8), 8), :]
    for k in range(1, 16):
        q = (pv + k) % 16
        pltpu.make_async_remote_copy(
            src_ref=r1.at[q], dst_ref=r1.at[q], send_sem=s2.at[k], recv_sem=q2.at[q],
            device_id=(core, gx, gy), device_id_type=MESH,
        ).wait_recv()
    ys = []
    prev = None
    for p in range(16):
        h = r1[p, 4:8, :]
        if p < 15:
            h = h + r1[p + 1, 0:4, :]
        h = r32 * h
        prev = h if p == 0 else h + dint[p - 1] * prev
        ys.append(prev)
    sol = [None] * 16
    sol[15] = dint[15] * ys[15]
    for p in range(14, -1, -1):
        sol[p] = dint[p] * (sol[p + 1] + ys[p])
    for p in range(16):
        m2[p, 0:4, :] = sol[p - 1] if p else jnp.zeros((4, 128), F32)
        m2[p, 4:8, :] = sol[p]
    t3 = []
    for k in range(1, 16):
        q = (pv + k) % 16
        copy = pltpu.make_async_remote_copy(
            src_ref=m2.at[q], dst_ref=r2.at[pl.ds(pl.multiple_of(pv * 8, 8), 8), :],
            send_sem=s3.at[k], recv_sem=q3.at[pv], device_id=to_row(q), device_id_type=MESH,
        )
        copy.start()
        t3.append(copy)
    r2[pl.ds(pl.multiple_of(pv * 8, 8), 8), :] = m2[pv]
    for k in range(1, 16):
        q = (pv + k) % 16
        view = r2.at[pl.ds(pl.multiple_of(q * 8, 8), 8), :]
        pltpu.make_async_remote_copy(
            src_ref=view, dst_ref=view, send_sem=s3.at[k], recv_sem=q3.at[q],
            device_id=(core, gx, gy), device_id_type=MESH,
        ).wait_recv()
    left = jnp.concatenate([r2[pl.ds(j, 16, stride=8), :] for j in range(4)], axis=1)
    right = jnp.concatenate([r2[pl.ds(4 + j, 16, stride=8), :] for j in range(4)], axis=1)

    def spread(i, t):
        u[i] = u[i] + t
        return dtab[i] * t

    lax.fori_loop(0, 31, spread, left)
    u[31] = right

    def backward(k, v):
        i = 30 - k
        v = dtab[i] * (v + u[i])
        u[i] = v
        return v

    lax.fori_loop(0, 31, backward, right)

    high, low = split(u[...].reshape(512, 512))
    uh[...] = high
    ul[...] = low
    u_pair = (uh[...], ul[...])
    rows = dot3(split(wall[...]), u_pair, NN)
    rows = dot3(split(rows), (myh[...], myl[...]), NN)
    lane = lax.broadcasted_iota(jnp.int32, (8, 128), 1) // 16
    for face in range(2):
        for t in range(2):
            cols = slice(128 * t, 128 * t + 128)
            v = [rows[32 * face + 8 * h : 32 * face + 8 * h + 8, cols] for h in range(4)]
            v += [rows[64 + 8 * h : 72 + 8 * h, cols] for h in range(4)]
            for q, w in enumerate(exchange(v, lane)):
                mzx[16 * face + 8 * t + q] = w
    ay = dot3(split(wys[...]), u_pair, NT)
    row = lax.broadcasted_iota(jnp.int32, (32, 512), 0)
    lanes = lax.broadcasted_iota(jnp.int32, (32, 512), 1)
    half = lax.broadcasted_iota(jnp.int32, (16, 128), 1) < 64
    for f in range(2):
        part = jnp.where(row == lanes // 16, ay[f : f + 1, :], 0.0)
        part = dot3(split(part), (mzth[...], mztl[...]), NN)
        top, bottom = part[:16], part[16:]
        my[f, 0] = jnp.where(half, top, pltpu.roll(bottom, 64, 1))
        my[f, 1] = jnp.where(half, pltpu.roll(top, 64, 1), bottom)
    tz = []
    for i, o in enumerate(peers):
        target, block = to_real(o)
        copy = pltpu.make_async_remote_copy(
            src_ref=mzx.at[block], dst_ref=rzx.at[mid], send_sem=sz.at[i], recv_sem=qz.at[mid],
            device_id=target, device_id_type=MESH,
        )
        copy.start()
        tz.append(copy)
    for f in range(2):
        for g in range(2):
            copy = pltpu.make_async_remote_copy(
                src_ref=my.at[f, g], dst_ref=ry.at[mid], send_sem=sy.at[2 * f + g],
                recv_sem=qy.at[mid], device_id=device(g, x, 7 * f, lv + 4 * f),
                device_id_type=MESH,
            )
            copy.start()
            tz.append(copy)

    for copy in t1:
        copy.wait_send()
    zb[...] = dot3(s_pair, u_pair, NT).reshape(32, 16, 512)
    t4 = []
    for i, o in enumerate(peers):
        target, block = to_real(o)
        copy = pltpu.make_async_remote_copy(
            src_ref=zb.at[block], dst_ref=za.at[mid], send_sem=s4.at[i], recv_sem=q4.at[mid],
            device_id=target, device_id_type=MESH,
        )
        copy.start()
        t4.append(copy)

    def arrived(ref, sem, index):
        pltpu.make_async_remote_copy(
            src_ref=ref.at[index], dst_ref=ref.at[index], send_sem=sem.at[index],
            recv_sem=sem.at[index], device_id=here, device_id_type=MESH,
        ).wait_recv()

    for s in range(32):
        arrived(rzx, qz, s)
    zsum = rzx[0]
    for s in range(1, 32):
        zsum = zsum + rzx[s]
    got = rzx[...].reshape(256, 128)
    parts = [full(got, mz[:, 8 * k : 8 * k + 8, :].reshape(256, 128), TN) for k in range(2)]
    for f in range(2):
        m6[f] = parts[0][64 + 32 * f : 80 + 32 * f] + parts[1][80 + 32 * f : 96 + 32 * f]
    row = lax.broadcasted_iota(jnp.int32, (128, 32), 0)
    col = lax.broadcasted_iota(jnp.int32, (128, 32), 1)
    pick = jnp.where(a0 - 3 + 2 * (row // 8) + row % 8 == 32 * gx + col, 1.0, 0.0)
    spread_z = jnp.concatenate([jnp.where(lane == h, zsum, 0.0) for h in range(4)], axis=0)
    m5[:, 0] = full(pick, spread_z, NN).reshape(16, 8, 128)
    m5[:, 1] = jnp.zeros((16, 8, 128), F32)
    at_y = (gy == 0) | (gy == 15)

    @pl.when(at_y)
    def _():
        for s in range(32):
            arrived(ry, qy, s)
        ysum = ry[0]
        for s in range(1, 32):
            ysum = ysum + ry[s]
        top = full(pick[:, :16], ysum, NN)
        bottom = full(pick[:, 16:], ysum, NN)
        left_half = lax.broadcasted_iota(jnp.int32, (128, 128), 1) < 64
        m5[:, 1] = jnp.where(left_half, top, bottom).reshape(16, 8, 128)

    t5 = []
    for k in range(1, 16):
        q = (gx + k) % 16
        copy = pltpu.make_async_remote_copy(
            src_ref=m5.at[q], dst_ref=r5.at[gx], send_sem=s5.at[k], recv_sem=q5.at[gx],
            device_id=real_row(q), device_id_type=MESH,
        )
        copy.start()
        t5.append(copy)
    r5[gx] = m5[gx]
    for f in range(2):
        end = 15 * f
        copy = pltpu.make_async_remote_copy(
            src_ref=m6.at[f], dst_ref=r6.at[gx], send_sem=s6.at[f], recv_sem=q6.at[gx],
            device_id=real_row(end), device_id_type=MESH,
        )

        @pl.when(gx != end)
        def _():
            copy.start()

        @pl.when(gx == end)
        def _():
            r6[gx] = m6[f]

    for k in range(1, 16):
        arrived(r5, q5, (gx + k) % 16)
    for copy in pair:
        copy.wait()

    def interpolate(rows, cols, fine, cell):
        scaled = 2 * fine + 5
        bottom = scaled // 8
        t = (scaled % 8).astype(F32) * 0.125
        return jnp.where(cell == bottom, 1.0 - t, 0.0) + jnp.where(cell == bottom + 1, t, 0.0)

    def grid(shape):
        return (lax.broadcasted_iota(jnp.int32, shape, 0), lax.broadcasted_iota(jnp.int32, shape, 1))

    row, col = grid((24, 8))
    int_x = interpolate(24, 8, row, col)
    row, col = grid((48, 128))
    int_y = jnp.where(col < 64, interpolate(48, 128, row, col % 16), 0.0)
    row, col = grid((128, 256))
    int_z = interpolate(128, 256, col, row % 64 + 30 * core)
    zb5 = r5[0, 0]
    yb5 = r5[0, 1]
    for s in range(1, 16):
        zb5 = zb5 + r5[s, 0]
        yb5 = yb5 + r5[s, 1]
    ghost_z = full(int_y, full(int_x, zb5, NN), NT)
    lane2 = lax.broadcasted_iota(jnp.int32, (48, 128), 1)
    edge = 127 * core
    for k in range(24):
        ed[k] = ed[k] * (-1.0 / 16.0)
        ed[k, :, own] = ed[k, :, own] + jnp.where(lane2 == edge, ghost_z[:, k : k + 1], 0.0)

    @pl.when(at_y)
    def _():
        ghost_y = full(full(int_x, yb5, NN), int_z, NN)
        for f in range(2):
            @pl.when(gy == 15 * f)
            def _():
                inner = 8 + 31 * f
                for k in range(24):
                    ed[k, inner : inner + 1, :] = ed[k, inner : inner + 1, :] + ghost_y[k : k + 1]

    for f in range(2):
        @pl.when(gx == 15 * f)
        def _():
            for k in range(16):
                if k != 15 * f:
                    arrived(r6, q6, k)
            xb6 = r6[0]
            for s in range(1, 16):
                xb6 = xb6 + r6[s]
            row, col = grid((48, 16))
            near_y = interpolate(48, 16, row, col)
            row, col = grid((128, 256))
            near_z = jnp.where(row < 64, interpolate(128, 256, col, row + 30 * core), 0.0)
            inner = 8 + 7 * f
            ed[inner] = ed[inner] + full(full(near_y, xb6, NN), near_z, NN)

    row = lax.broadcasted_iota(jnp.int32, (48, 256), 0)
    col = lax.broadcasted_iota(jnp.int32, (48, 256), 1)
    inside_y = (row + 32 * gy >= 8) & (row + 32 * gy < 520)

    def inside_x(k):
        return (k + 8 * gx >= 8) & (k + 8 * gx < 136)

    for k in range(24):
        es[k] = jnp.where(inside_y & inside_x(k), es[k], 0.0)

    def sweep(source, target, k):
        v = source[k]
        total = source[k - 1] + source[k + 1]
        total = total + (pltpu.roll(v, 1, 0) + pltpu.roll(v, 47, 0))
        total = total + jnp.where(col == 0, 0.0, pltpu.roll(v, 1, 1))
        total = total + jnp.where(col == 255, 0.0, pltpu.roll(v, 255, 1))
        factor = jnp.where(inside_y & inside_x(k), 1.0 / 6.0, 0.0)
        target[k] = (total + ed[k]) * factor

    def two(j, carry):
        def one(k, c):
            sweep(es, et, k)
            return c

        def other(k, c):
            sweep(et, es, k)
            return c

        lax.fori_loop(2 * j + 1, 23 - 2 * j, one, 0)
        lax.fori_loop(2 * j + 2, 22 - 2 * j, other, 0)
        return carry

    lax.fori_loop(0, 4, two, 0)
    fine_ref[...] = es[8:16, 8:40, own]

    for s in range(32):
        arrived(za, q4, s)
    swap_groups(za, dd)
    value = dd[...].reshape(512, 512)
    out_ref[...] = dot3(split(value), s_pair, NN).reshape(32, 16, 512)
    for copy in t2 + t3 + t4 + tz + t5 + halo:
        copy.wait_send()
    for f in range(2):
        @pl.when(gx != 15 * f)
        def _():
            pltpu.make_async_remote_copy(
                src_ref=m6.at[f], dst_ref=r6.at[gx], send_sem=s6.at[f], recv_sem=q6.at[gx],
                device_id=real_row(15 * f), device_id_type=MESH,
            ).wait_send()


def body(density, fine_density, fine_start, anchor):
    high, low, lam = tables()
    vm = pl.BlockSpec(memory_space=pltpu.VMEM)
    dma = pltpu.SemaphoreType.DMA

    def f32(*shape):
        return pltpu.VMEM(shape, F32)

    def b16(*shape):
        return pltpu.VMEM(shape, BF16)

    big = f32(32, 16, 512)
    return pl.pallas_call(
        kernel,
        out_shape=(
            jax.ShapeDtypeStruct((32, 16, 512), F32), jax.ShapeDtypeStruct((8, 32, 128), F32)
        ),
        in_specs=[pl.BlockSpec(memory_space=pltpu.SMEM)] + [vm] * 8,
        out_specs=(vm, vm),
        scratch_shapes=[
            big, big, big, big, f32(31, 16, 512),
            f32(128, 128), f32(16, 8, 128), f32(16, 8, 128), f32(128, 128), f32(16, 4, 128),
            b16(512, 512), b16(512, 512), b16(512, 256), b16(512, 256), f32(32, 16, 128),
            b16(512, 128), b16(512, 128), f32(96, 512), f32(16, 512),
            f32(32, 8, 128), f32(32, 8, 128), f32(2, 2, 16, 128), f32(32, 16, 128),
            f32(16, 2, 8, 128), f32(16, 2, 8, 128), f32(2, 16, 128), f32(16, 16, 128),
            f32(24, 48, 256), f32(24, 48, 256), f32(24, 48, 256),
            dma((32,)), dma((32,)), dma((16,)), dma((16,)), dma((16,)), dma((16,)),
            dma((32,)), dma((32,)), dma((16,)), dma((16,)), dma((2,)), dma((2,)),
            dma((32,)), dma((32,)), dma((4,)), dma((32,)), dma((16,)), dma((16,)),
            dma((2,)), dma((16,)),
        ],
        compiler_params=pltpu.CompilerParams(
            collective_id=0, has_side_effects=True, vmem_limit_bytes=56 << 20
        ),
    )(anchor, density, fine_density, fine_start, jnp.asarray(high), jnp.asarray(low),
      jnp.asarray(lam.reshape(1, 512)), jnp.asarray(lam.reshape(512, 1)),
      jnp.asarray(lam.reshape(4, 128)))


def solution(mesh):
    return jax.shard_map(
        body,
        mesh=mesh,
        in_specs=(P("gx", ("grp", "gy"), None), P("gx", "gy", "grp"), P("gx", "gy", "grp"), P()),
        out_specs=(P("gx", ("grp", "gy"), None), P("gx", "gy", "grp")),
        check_vma=False,
    )
```

time: 511 us -> 141 us (0.28)
  the two profiles are of different devices: /device:TPU:56 before, /device:TPU:1 now
where the time goes in v2:
time: 141 us
  Pallas kernels  137 us (97%)
  local copies, waits for them, and re-layouts  3 us (2%)
    pallas_call x1, Pallas kernels, body(): pl.pallas_call(kernel, out_shape=(jax.ShapeDtypeStruct((32, 16, 512), F32...  137 us
    unnamed x4, local copies, waits for them, and re-layouts  3 us

profile of v2, /device:TPU:1, one launch (start us, length us, event | category | flops | bytes accessed | tf_op | source)
XLA Modules:
  0.0 140.6 jit_solution(1065721009684918377)
XLA Ops:
  0.6 137.0 %shard_map.104 = (f32[32,16,512]{2,1,0:T(8,128)}, f32[8,32,128]{2,1,0:T(8,128)}) custom-call(s32[3]{0:T(128)} %anchor.1, f32[32,16,512]{2,1,0:T(8,128)} %x_ref.1, f32[8,32,128]{2,1,0:T(8,128)} %fd_ref.1, f32[8,32,128]{2,1,0:T(8,128)} %fs_ref.1, bf16[512,512]{1,0:T(8,128)(2,1)} %constant.10.clone.sh_ref, bf16[512,512]{1,0:T(8,128)(2,1)} %constant.11.clone.sl_ref, ...), custom_call_target="tpu_custom_call" | custom-call | tf_op jit(solution)/shard_map/pallas_call | solution.py:602
  137.6 0.0 copy-start
  137.6 2.3 %copy.13 = f32[32,16,512]{2,1,0:T(8,128)} copy(f32[32,16,512]{2,1,0:T(8,128)} %get-tuple-element.4) | data formatting | bytes 2097152
  139.9 0.0 copy-done
  139.9 0.7 copy.14
Async XLA Ops:
  137.6 2.4 %copy-start = (f32[8,32,128]{2,1,0:T(8,128)S(1)}, f32[8,32,128]{2,1,0:T(8,128)}, u32[]{:S(2)}) copy-start(f32[8,32,128]{2,1,0:T(8,128)} %get-tuple-element.5) | copy-start | bytes 393220

commit v3 on v2

--- a/solution.py
+++ b/solution.py
@@ -72,19 +72,16 @@
 def swap_groups(source, target):
     lane = lax.broadcasted_iota(jnp.int32, (8, 128), 1) // 16
 
-    def step(index, carry):
-        at = index // 8
-        bt = (index // 2) % 4
-        row = pl.multiple_of((index % 2) * 8, 8)
-        cols = pl.ds(pl.multiple_of(bt * 128, 128), 128)
+    def step(at, carry):
         outs = pl.ds(pl.multiple_of(at * 128, 128), 128)
-        v = [source[at * 8 + q, pl.ds(row, 8), cols] for q in range(8)]
-        v = exchange(v, lane)
-        for q in range(8):
-            target[bt * 8 + q, pl.ds(row, 8), outs] = v[q]
+        for bt in range(4):
+            for row in (0, 8):
+                v = [source[at * 8 + q, row : row + 8, 128 * bt : 128 * bt + 128] for q in range(8)]
+                for q, w in enumerate(exchange(v, lane)):
+                    target[bt * 8 + q, row : row + 8, outs] = w
         return carry
 
-    lax.fori_loop(0, 32, step, 0)
+    lax.fori_loop(0, 4, step, 0)
 
 
 def device(core, x, y, z):
@@ -101,10 +98,12 @@
 
 
 def kernel(
-    anchor, x_ref, fd_ref, fs_ref, sh_ref, sl_ref, lamr_ref, lamc_ref, lamq_ref, out_ref, fine_ref,
+    anchor, lamr_ref, lamc_ref, lamq_ref, x_hbm, fd_hbm, fs_hbm, sh_hbm, sl_hbm, out_ref, fine_ref,
+    x_ref, fd_ref, fs_ref, sh_ref, sl_ref,
     za, zb, dd, u, dtab, m1, r1, m2, r2, dint, uh, ul, myh, myl, mz, mzth, mztl, wall, wys,
-    mzx, rzx, my, ry, m5, r5, m6, r6, es, et, ed,
-    s1, q1, s2, q2, s3, q3, s4, q4, sh1, qh1, sd, qd, sz, qz, sy, qy, s5, q5, s6, q6,
+    mzx, rzx, my, ry, m5, r5, m6, r6, es, et, ed, fa, fb, fr, trace, tin,
+    s1, q1, s2, q2, s3, q3, s4, q4, sh1, qh1, sd, qd, sz, qz, sy, qy, s5, q5, s6, q6, sin,
+    st, qt, se, qe,
 ):
     core = lax.axis_index("grp")
     gx = lax.axis_index("gx")
@@ -139,7 +138,6 @@
     here = (core, gx, gy)
     partner = (1 - core, gx, gy)
     own = pl.ds(pl.multiple_of(core * 128, 128), 128)
-    sides = [(ox, oy) for ox in (-1, 0, 1) for oy in (-1, 0, 1) if (ox, oy) != (0, 0)]
 
     def beside(ox, oy):
         return (core, (gx + ox + 16) % 16, (gy + oy + 16) % 16)
@@ -147,8 +145,8 @@
     a0, a1, a2 = anchor[0], anchor[1], anchor[2]
     barrier = pltpu.get_barrier_semaphore()
     pl.semaphore_signal(barrier, inc=1, device_id=partner, device_id_type=MESH)
-    for side in sides:
-        pl.semaphore_signal(barrier, inc=1, device_id=beside(*side), device_id_type=MESH)
+    for oy in (-1, 1):
+        pl.semaphore_signal(barrier, inc=1, device_id=beside(0, oy), device_id_type=MESH)
     for k in range(1, 16):
         pl.semaphore_signal(
             barrier, inc=1, device_id=real_row((gx + k) % 16), device_id_type=MESH
@@ -159,13 +157,38 @@
     for k in range(1, 16):
         pl.semaphore_signal(barrier, inc=1, device_id=to_row((pv + k) % 16), device_id_type=MESH)
 
+    fetch = []
+    for k, (src, dst) in enumerate((
+        (x_hbm, x_ref), (sh_hbm, sh_ref), (sl_hbm, sl_ref), (fd_hbm, fd_ref), (fs_hbm, fs_ref)
+    )):
+        copy = pltpu.make_async_copy(src, dst, sin.at[k])
+        copy.start()
+        fetch.append(copy)
+    for copy in fetch[:3]:
+        copy.wait()
     s_pair = (sh_ref[...], sl_ref[...])
     value = x_ref[...].reshape(512, 512)
     za[...] = dot3(split(value), s_pair, NN).reshape(32, 16, 512)
     swap_groups(za, zb)
-
-    pl.semaphore_wait(barrier, 71)
-
+    fetch[3].wait()
+    fetch[4].wait()
+    fa[1:9, 8:40, own] = fs_ref[...]
+    fr[1:9, 8:40, own] = fd_ref[...]
+
+    pl.semaphore_wait(barrier, 65)
+
+    halo = []
+    for k, oy in enumerate((-1, 1)):
+        rows = pl.ds(0, 8) if oy < 0 else pl.ds(24, 8)
+        to_rows = pl.ds(40, 8) if oy < 0 else pl.ds(0, 8)
+        for part, (src, dst) in enumerate(((fs_ref, fa), (fd_ref, fr))):
+            copy = pltpu.make_async_remote_copy(
+                src_ref=src.at[:, rows, :], dst_ref=dst.at[pl.ds(1, 8), to_rows, own],
+                send_sem=sh1.at[2 * k + part], recv_sem=qh1.at[2 * k + part],
+                device_id=beside(0, oy), device_id_type=MESH,
+            )
+            copy.start()
+            halo.append(copy)
     t1 = []
     for i, o in enumerate(peers):
         target, block = to_mid(o)
@@ -175,22 +198,6 @@
         )
         copy.start()
         t1.append(copy)
-
-    es[8:16, 8:40, own] = fs_ref[...]
-    ed[8:16, 8:40, own] = fd_ref[...]
-    halo = []
-    for k, (ox, oy) in enumerate(sides):
-        rows = {-1: pl.ds(0, 8), 0: pl.ds(0, 32), 1: pl.ds(24, 8)}[oy]
-        to_rows = {-1: pl.ds(40, 8), 0: pl.ds(8, 32), 1: pl.ds(0, 8)}[oy]
-        layers = {-1: pl.ds(16, 8), 0: pl.ds(8, 8), 1: pl.ds(0, 8)}[ox]
-        for part, (src, dst) in enumerate(((fs_ref, es), (fd_ref, ed))):
-            copy = pltpu.make_async_remote_copy(
-                src_ref=src.at[:, rows, :], dst_ref=dst.at[layers, to_rows, own],
-                send_sem=sh1.at[2 * k + part], recv_sem=qh1.at[2 * k + part],
-                device_id=beside(ox, oy), device_id_type=MESH,
-            )
-            copy.start()
-            halo.append(copy)
 
     def face_tables():
         def cells(rows, cols, first):
@@ -259,6 +266,54 @@
     dint[15] = 1.0 / (r32 * (1.0 + c1) + c + g)
 
     face_tables()
+    for copy in halo:
+        copy.wait_recv()
+    pair = []
+    for k, ref in enumerate((fa, fr)):
+        view = ref.at[pl.ds(1, 8), :, own]
+        copy = pltpu.make_async_remote_copy(
+            src_ref=view, dst_ref=view, send_sem=sd.at[k], recv_sem=qd.at[k],
+            device_id=partner, device_id_type=MESH,
+        )
+        copy.start()
+        pair.append(copy)
+    for copy in pair:
+        copy.wait()
+    fine_row = lax.broadcasted_iota(jnp.int32, (48, 256), 0) + 32 * gy
+    fine_col = lax.broadcasted_iota(jnp.int32, (48, 256), 1)
+    inside_y = (fine_row >= 8) & (fine_row < 520)
+    sixth = jnp.where(inside_y, 1.0 / 6.0, 0.0)
+
+    def layer(source, extra, k):
+        v = source[k]
+        total = (source[k - 1] + source[k + 1]) + extra[k]
+        total = total + (pltpu.roll(v, 1, 0) + pltpu.roll(v, 47, 0))
+        total = total + jnp.where(fine_col == 0, 0.0, pltpu.roll(v, 1, 1))
+        return total + jnp.where(fine_col == 255, 0.0, pltpu.roll(v, 255, 1))
+
+    for k in (0, 9):
+        fa[k] = jnp.zeros((48, 256), F32)
+        fb[k] = jnp.zeros((48, 256), F32)
+    for k in range(1, 9):
+        fa[k] = jnp.where(inside_y, fa[k], 0.0)
+        fr[k] = fr[k] * (-1.0 / 16.0)
+        es[k + 7] = fa[k]
+
+    def alone(j, carry):
+        for part, (source, target) in enumerate(((fa, fb), (fb, fa))):
+            trace[0, 2 * j + part] = source[1]
+            trace[1, 2 * j + part] = source[8]
+
+            def four(k, c):
+                for m in range(4):
+                    index = 1 + 4 * k + m
+                    target[index] = layer(source, fr, index) * sixth
+                return c
+
+            lax.fori_loop(0, 2, four, 0)
+        return carry
+
+    lax.fori_loop(0, 4, alone, 0)
     for s in range(32):
         pltpu.make_async_remote_copy(
             src_ref=dd.at[s], dst_ref=dd.at[s], send_sem=s1.at[s], recv_sem=q1.at[s],
@@ -294,16 +349,15 @@
         )
         copy.start()
         t2.append(copy)
-    for copy in halo:
-        copy.wait_recv()
-    pair = []
-    for k, ref in enumerate((es, ed)):
-        copy = pltpu.make_async_remote_copy(
-            src_ref=ref.at[:, :, own], dst_ref=ref.at[:, :, own], send_sem=sd.at[k],
-            recv_sem=qd.at[k], device_id=partner, device_id_type=MESH,
-        )
-        copy.start()
-        pair.append(copy)
+    tt = []
+    for side, ox in enumerate((-1, 1)):
+        copy = pltpu.make_async_remote_copy(
+            src_ref=trace.at[side, :, :, own], dst_ref=tin.at[1 - side, :, :, own],
+            send_sem=st.at[side], recv_sem=qt.at[1 - side], device_id=beside(ox, 0),
+            device_id_type=MESH,
+        )
+        copy.start()
+        tt.append(copy)
     r1[pv] = m1[pl.ds(pl.multiple_of(pv * 8, 8), 8), :]
     for k in range(1, 16):
         q = (pv + k) % 16
@@ -418,6 +472,19 @@
         copy.start()
         t4.append(copy)
 
+    te = []
+    for side in range(2):
+        pltpu.make_async_remote_copy(
+            src_ref=trace.at[side, :, :, own], dst_ref=tin.at[side, :, :, own],
+            send_sem=st.at[side], recv_sem=qt.at[side], device_id=here, device_id_type=MESH,
+        ).wait_recv()
+        view = tin.at[side, :, :, own]
+        copy = pltpu.make_async_remote_copy(
+            src_ref=view, dst_ref=view, send_sem=se.at[side], recv_sem=qe.at[side],
+            device_id=partner, device_id_type=MESH,
+        )
+        copy.start()
+        te.append(copy)
     def arrived(ref, sem, index):
         pltpu.make_async_remote_copy(
             src_ref=ref.at[index], dst_ref=ref.at[index], send_sem=sem.at[index],
@@ -480,8 +547,6 @@
 
     for k in range(1, 16):
         arrived(r5, q5, (gx + k) % 16)
-    for copy in pair:
-        copy.wait()
 
     def interpolate(rows, cols, fine, cell):
         scaled = 2 * fine + 5
@@ -507,7 +572,7 @@
     lane2 = lax.broadcasted_iota(jnp.int32, (48, 128), 1)
     edge = 127 * core
     for k in range(24):
-        ed[k] = ed[k] * (-1.0 / 16.0)
+        ed[k] = fr[k - 7] if 8 <= k < 16 else jnp.zeros((48, 256), F32)
         ed[k, :, own] = ed[k, :, own] + jnp.where(lane2 == edge, ghost_z[:, k : k + 1], 0.0)
 
     @pl.when(at_y)
@@ -536,39 +601,27 @@
             inner = 8 + 7 * f
             ed[inner] = ed[inner] + full(full(near_y, xb6, NN), near_z, NN)
 
-    row = lax.broadcasted_iota(jnp.int32, (48, 256), 0)
-    col = lax.broadcasted_iota(jnp.int32, (48, 256), 1)
-    inside_y = (row + 32 * gy >= 8) & (row + 32 * gy < 520)
+    for copy in te:
+        copy.wait_recv()
 
     def inside_x(k):
         return (k + 8 * gx >= 8) & (k + 8 * gx < 136)
 
-    for k in range(24):
-        es[k] = jnp.where(inside_y & inside_x(k), es[k], 0.0)
-
-    def sweep(source, target, k):
-        v = source[k]
-        total = source[k - 1] + source[k + 1]
-        total = total + (pltpu.roll(v, 1, 0) + pltpu.roll(v, 47, 0))
-        total = total + jnp.where(col == 0, 0.0, pltpu.roll(v, 1, 1))
-        total = total + jnp.where(col == 255, 0.0, pltpu.roll(v, 255, 1))
-        factor = jnp.where(inside_y & inside_x(k), 1.0 / 6.0, 0.0)
-        target[k] = (total + ed[k]) * factor
-
-    def two(j, carry):
-        def one(k, c):
-            sweep(es, et, k)
+    for k in list(range(8)) + list(range(16, 24)):
+        es[k] = jnp.zeros((48, 256), F32)
+    ends = (jnp.where(gx == 0, 0.0, sixth), jnp.where(gx == 15, 0.0, sixth))
+    for j in range(8):
+        source, target = ((es, et), (et, es))[j % 2]
+
+        def two(k, c, source=source, target=target, j=j):
+            for m in range(2):
+                index = j + 1 + 2 * k + m
+                target[index] = layer(source, ed, index) * jnp.where(inside_x(index), sixth, 0.0)
             return c
 
-        def other(k, c):
-            sweep(et, es, k)
-            return c
-
-        lax.fori_loop(2 * j + 1, 23 - 2 * j, one, 0)
-        lax.fori_loop(2 * j + 2, 22 - 2 * j, other, 0)
-        return carry
-
-    lax.fori_loop(0, 4, two, 0)
+        lax.fori_loop(0, 11 - j, two, 0)
+        target[8] = target[8] + tin[0, j] * ends[0]
+        target[15] = target[15] + tin[1, j] * ends[1]
     fine_ref[...] = es[8:16, 8:40, own]
 
     for s in range(32):
@@ -576,7 +629,7 @@
     swap_groups(za, dd)
     value = dd[...].reshape(512, 512)
     out_ref[...] = dot3(split(value), s_pair, NN).reshape(32, 16, 512)
-    for copy in t2 + t3 + t4 + tz + t5 + halo:
+    for copy in t2 + t3 + t4 + tz + t5 + halo + tt + te:
         copy.wait_send()
     for f in range(2):
         @pl.when(gx != 15 * f)
@@ -604,9 +657,11 @@
         out_shape=(
             jax.ShapeDtypeStruct((32, 16, 512), F32), jax.ShapeDtypeStruct((8, 32, 128), F32)
         ),
-        in_specs=[pl.BlockSpec(memory_space=pltpu.SMEM)] + [vm] * 8,
+        in_specs=[pl.BlockSpec(memory_space=pltpu.SMEM)] + [vm] * 3
+        + [pl.BlockSpec(memory_space=pl.ANY)] * 5,
         out_specs=(vm, vm),
         scratch_shapes=[
+            big, f32(8, 32, 128), f32(8, 32, 128), b16(512, 512), b16(512, 512),
             big, big, big, big, f32(31, 16, 512),
             f32(128, 128), f32(16, 8, 128), f32(16, 8, 128), f32(128, 128), f32(16, 4, 128),
             b16(512, 512), b16(512, 512), b16(512, 256), b16(512, 256), f32(32, 16, 128),
@@ -614,17 +669,19 @@
             f32(32, 8, 128), f32(32, 8, 128), f32(2, 2, 16, 128), f32(32, 16, 128),
             f32(16, 2, 8, 128), f32(16, 2, 8, 128), f32(2, 16, 128), f32(16, 16, 128),
             f32(24, 48, 256), f32(24, 48, 256), f32(24, 48, 256),
+            f32(10, 48, 256), f32(10, 48, 256), f32(10, 48, 256),
+            f32(2, 8, 48, 256), f32(2, 8, 48, 256),
             dma((32,)), dma((32,)), dma((16,)), dma((16,)), dma((16,)), dma((16,)),
-            dma((32,)), dma((32,)), dma((16,)), dma((16,)), dma((2,)), dma((2,)),
+            dma((32,)), dma((32,)), dma((4,)), dma((4,)), dma((2,)), dma((2,)),
             dma((32,)), dma((32,)), dma((4,)), dma((32,)), dma((16,)), dma((16,)),
-            dma((2,)), dma((16,)),
+            dma((2,)), dma((16,)), dma((5,)), dma((2,)), dma((2,)), dma((2,)), dma((2,)),
         ],
         compiler_params=pltpu.CompilerParams(
             collective_id=0, has_side_effects=True, vmem_limit_bytes=56 << 20
         ),
-    )(anchor, density, fine_density, fine_start, jnp.asarray(high), jnp.asarray(low),
-      jnp.asarray(lam.reshape(1, 512)), jnp.asarray(lam.reshape(512, 1)),
-      jnp.asarray(lam.reshape(4, 128)))
+    )(anchor, jnp.asarray(lam.reshape(1, 512)), jnp.asarray(lam.reshape(512, 1)),
+      jnp.asarray(lam.reshape(4, 128)), density, fine_density, fine_start,
+      jnp.asarray(high), jnp.asarray(low))
 
 
 def solution(mesh):

time: 141 us -> 119 us (0.84)
  Pallas kernels: 137 us -> 115 us
    pallas_call x1, Pallas kernels: 137 us -> 115 us  [body(): pl.pallas_call(kernel, out_shape=(jax.ShapeDtypeStruct((32, 16, 512), F32...]
where the time goes in v3:
time: 119 us
  Pallas kernels  115 us (97%)
  local copies, waits for them, and re-layouts  3 us (3%)
    pallas_call x1, Pallas kernels, body(): pl.pallas_call(kernel, out_shape=(jax.ShapeDtypeStruct((32, 16, 512), F32...  115 us
    unnamed x4, local copies, waits for them, and re-layouts  3 us

profile of v3, /device:TPU:1, one launch (start us, length us, event | category | flops | bytes accessed | tf_op | source)
XLA Modules:
  0.0 118.8 jit_solution(15266616924718044505)
XLA Ops:
  0.6 115.1 %shard_map.104 = (f32[32,16,512]{2,1,0:T(8,128)}, f32[8,32,128]{2,1,0:T(8,128)}) custom-call(s32[3]{0:T(128)} %anchor.1, f32[1,512]{1,0:T(1,128)} %constant.10.clone.lamr_ref, f32[512,1]{1,0:T(8,128)} %constant.11.clone.lamc_ref, f32[4,128]{1,0:T(4,128)} %constant.12.clone.lamq_ref, f32[32,16,512]{2,1,0:T(8,128)} %x_hbm.1, f32[8,32,128]{2,1,0:T(8,128)} %fd_hbm.1, ...), custom_call_target="tpu_custom_call" | custom-call | tf_op jit(solution)/shard_map/pallas_call | solution.py:655
  115.8 0.0 copy-start
  115.8 2.3 %copy.13 = f32[32,16,512]{2,1,0:T(8,128)} copy(f32[32,16,512]{2,1,0:T(8,128)} %get-tuple-element.4) | data formatting | bytes 2097152
  118.1 0.0 copy-done
  118.1 0.7 copy.14
Async XLA Ops:
  115.8 2.4 %copy-start = (f32[8,32,128]{2,1,0:T(8,128)S(1)}, f32[8,32,128]{2,1,0:T(8,128)}, u32[]{:S(2)}) copy-start(f32[8,32,128]{2,1,0:T(8,128)} %get-tuple-element.5) | copy-start | bytes 393220

commit v4 on v3

v4 whole, which is shorter than its diff:
```python
import functools
import math

import jax
import jax.numpy as jnp
import numpy as np
from jax import lax
from jax.experimental import pallas as pl
from jax.experimental.pallas import tpu as pltpu
from jax.sharding import PartitionSpec as P

MESH = pl.DeviceIdType.MESH
NC = 512
F32 = jnp.float32
CUT1, CUT4A, CUT4B = 32, 16, 32
WIDE = 4
BF16 = jnp.bfloat16


def tables():
    index = np.arange(1, NC + 1, dtype=np.int64)
    angle = (index[:, None] * index[None, :]) % (2 * (NC + 1))
    sine = math.sqrt(2.0 / (NC + 1)) * np.sin(angle * (math.pi / (NC + 1)))
    sine = sine.astype(np.float32)
    high = sine.astype(jnp.bfloat16)
    low = (sine - high.astype(np.float32)).astype(jnp.bfloat16)
    lam = 4.0 * np.sin(index * (math.pi / (2 * (NC + 1)))) ** 2
    return high, low, lam.astype(np.float32)


def split(value):
    high = value.astype(BF16)
    low = (value - high.astype(F32)).astype(BF16)
    return high, low


def dot3(a, b, dims):
    ah, al = a
    bh, bl = b
    dd = functools.partial(
        lax.dot_general, dimension_numbers=(dims, ((), ())), preferred_element_type=F32
    )
    return dd(ah, bh) + (dd(al, bh) + dd(ah, bl))


def mm(a, b, dims):
    return lax.dot_general(a, b, (dims, ((), ())), preferred_element_type=F32)


def full(a, b, dims):
    return lax.dot_general(
        a, b, (dims, ((), ())), precision=lax.Precision.HIGHEST, preferred_element_type=F32
    )


NN = ((1,), (0,))
NT = ((1,), (1,))
TN = ((0,), (0,))


def exchange(v, lane):
    v = list(v)
    for bit in (1, 2, 4, 8):
        upper = (lane & bit) != 0
        for i in range(16):
            if i & bit:
                continue
            a, c = v[i], v[i | bit]
            v[i] = jnp.where(upper, pltpu.roll(c, 8 * bit, 1), a)
            v[i | bit] = jnp.where(upper, c, pltpu.roll(a, 128 - 8 * bit, 1))
    return v


def exchange8(v, lane):
    v = list(v)
    for bit in (1, 2, 4):
        upper = (lane & bit) != 0
        for i in range(8):
            if i & bit:
                continue
            a, c = v[i], v[i | bit]
            v[i] = jnp.where(upper, pltpu.roll(c, 16 * bit, 1), a)
            v[i | bit] = jnp.where(upper, c, pltpu.roll(a, 128 - 16 * bit, 1))
    return v


def swap_groups(source, target, first, out_first):
    lane = lax.broadcasted_iota(jnp.int32, (8, 128), 1) // 8
    for a in range(2):
        for b in range(2):
            cols = slice(first + 128 * b, first + 128 * b + 128)
            outs = slice(out_first + 128 * a, out_first + 128 * a + 128)
            for row in (0, 8):
                v = [source[16 * a + q, row : row + 8, cols] for q in range(16)]
                for q, w in enumerate(exchange(v, lane)):
                    target[16 * b + q, row : row + 8, outs] = w


def device(core, x, y, z):
    return (core, x * 4 + z % 4, (z // 4) * 8 + y)


ORDER = [
    (dy, side, core) for dy in (4, 3, 5, 2, 6, 1, 7, 0) for side in (0, 1) for core in (0, 1)
]
PEERS = [ORDER[i] for i in np.random.RandomState(3).permutation(32)]


def kernel(
    anchor_hbm, lamr_hbm, lamc_hbm, lamq_hbm, x_hbm, fd_hbm, fs_hbm, sh_hbm, sl_hbm, out_ref, fine_ref,
    anchor, lamr_ref, lamc_ref, lamq_ref, x_ref, fd_ref, fs_ref, sh_ref, sl_ref,
    za, zb, dd, gg, u, dtab, m1, r1, m2, r2, dint, rint, uh, ul, myh, myl, mz, mzy, mzt, wall, wys,
    mzx, rzx, my, ry, m5, r5, m6, r6, es, et, ed, fa, fb, fr, trace, tin, gz, ya, yb, yd,
    s1, q1, s2, q2, s3, q3, s4, q4, sh1, qh1, sd, qd, sz, qz, sy, qy, s5, q5, s6, q6, sin,
    st, qt, se, qe,
):
    core = lax.axis_index("grp")
    gx = lax.axis_index("gx")
    gy = lax.axis_index("gy")
    x, zl = gx // 4, gx % 4
    y, zh = gy % 8, gy // 8
    z = zh * 4 + zl
    me = core * 16 + gy
    zv = (z + 6) % 8
    lv, hv = zv % 4, zv // 4
    mid = core * 16 + hv * 8 + y
    pv = x * 4 + lv

    def to_mid(o):
        dy, side, oc = o
        ty = (y + dy + core * (8 - 2 * dy)) % 8
        tc = (core + oc) % 2
        return device(tc, x, ty, (zl + 4 * side + 2) % 8), tc * 16 + side * 8 + ty

    def to_real(o):
        dy, side, oc = o
        ty = (y + dy + core * (8 - 2 * dy)) % 8
        tc = (core + oc) % 2
        return device(tc, x, ty, lv + 4 * side), tc * 16 + side * 8 + ty

    def to_row(q):
        return device(core, q // 4, y, (q % 4 + 4 * hv + 2) % 8)

    def real_row(q):
        return device(core, q // 4, y, q % 4 + 4 * zh)

    here = (core, gx, gy)
    partner = (1 - core, gx, gy)
    own = pl.ds(pl.multiple_of(core * 128, 128), 128)

    def beside(ox, oy):
        return (core, (gx + ox + 16) % 16, (gy + oy + 16) % 16)

    fetch = []
    mine = [pl.ds(pl.multiple_of(256 * h + 8 * mid, 8), 8) for h in range(2)]
    for k, (src, dst) in enumerate((
        (x_hbm, x_ref), (sh_hbm, sh_ref), (sl_hbm, sl_ref), (fd_hbm, fd_ref), (fs_hbm, fs_ref),
        (lamr_hbm, lamr_ref), (lamq_hbm, lamq_ref), (lamc_hbm.at[mine[0], :], lamc_ref.at[0]),
        (lamc_hbm.at[mine[1], :], lamc_ref.at[1]), (anchor_hbm, anchor),
    )):
        copy = pltpu.make_async_copy(src, dst, sin.at[k])
        copy.start()
        fetch.append(copy)
    barrier = pltpu.get_barrier_semaphore()
    for o in PEERS:
        pl.semaphore_signal(barrier, inc=1, device_id=to_mid(o)[0], device_id_type=MESH)
    pl.semaphore_signal(barrier, inc=1, device_id=partner, device_id_type=MESH)
    for oy in (-1, 1):
        pl.semaphore_signal(barrier, inc=1, device_id=beside(0, oy), device_id_type=MESH)
    for k in range(1, 16):
        pl.semaphore_signal(barrier, inc=1, device_id=to_row((pv + k) % 16), device_id_type=MESH)
        pl.semaphore_signal(barrier, inc=1, device_id=real_row((gx + k) % 16), device_id_type=MESH)

    def arrived(ref, sem, index):
        pltpu.make_async_remote_copy(
            src_ref=ref.at[index], dst_ref=ref.at[index], send_sem=sem.at[index],
            recv_sem=sem.at[index], device_id=here, device_id_type=MESH,
        ).wait_recv()

    def send(src, dst, send_sem, recv_sem, target):
        copy = pltpu.make_async_remote_copy(
            src_ref=src, dst_ref=dst, send_sem=send_sem, recv_sem=recv_sem,
            device_id=target, device_id_type=MESH,
        )
        copy.start()
        return copy

    for copy in fetch[:3]:
        copy.wait()
    s_pair = (sh_ref[...], sl_ref[...])
    x_pair = split(x_ref[...].reshape(512, 512))
    halves = [slice(0, 256), slice(256, 512)]

    def forward_third(h):
        cols = tuple(part[:, halves[h]] for part in s_pair)
        za[:, :, halves[h]] = dot3(x_pair, cols, NN).reshape(32, 16, 256)
        swap_groups(za, zb.at[h], 256 * h, 0)

    t1 = [[], []]

    def send_first(h, lo, hi):
        for i in range(lo, hi):
            target, block = to_mid(PEERS[i])
            t1[h].append(
                send(zb.at[h, block], dd.at[h, me], s1.at[h, i], q1.at[h, me], target)
            )

    forward_third(0)
    for copy in fetch[3:]:
        copy.wait()
    a0, a1, a2 = anchor[0], anchor[1], anchor[2]
    fa[1:9, 8:40, own] = fs_ref[...]
    fr[1:9, 8:40, own] = fd_ref[...]
    pl.semaphore_wait(barrier, 65)
    halo = []
    for k, oy in enumerate((-1, 1)):
        rows = pl.ds(0, 8) if oy < 0 else pl.ds(24, 8)
        to_rows = pl.ds(40, 8) if oy < 0 else pl.ds(0, 8)
        for part, (src, dst) in enumerate(((fs_ref, fa), (fd_ref, fr))):
            halo.append(send(
                src.at[:, rows, :], dst.at[pl.ds(1, 8), to_rows, own],
                sh1.at[2 * k + part], qh1.at[2 * k + part], beside(0, oy),
            ))
    send_first(0, 0, 32)
    forward_third(1)
    send_first(1, 0, CUT1)
    for h in range(2):
        mu = lamr_ref[0:1, :] + jnp.concatenate([lamc_ref[h]] * 4, axis=1)

        def table(i, g, h=h, mu=mu):
            d = 1.0 / (1.0 + (mu + g))
            dtab[h, i] = d
            return (mu + g) * d

        lax.fori_loop(0, 31, table, jnp.ones((8, 512), F32))
        odd = pv % 2 == 1
        muq = jnp.where(odd, lamq_ref[2:4, :], lamq_ref[0:2, :]) + lamc_ref[h, pl.ds(pv // 2, 1), :]
        c = 0.5 * muq
        c1 = c
        r32 = 2.0 * (1.0 + c)
        for _ in range(4):
            c = 2.0 * c * (c + 2.0)
            r32 = r32 * (2.0 * (1.0 + c))
        c = 2.0 * c * (c + 2.0)
        rint[h] = r32
        g = jnp.ones((2, 128), F32)
        for i in range(15):
            d = 1.0 / (1.0 + (2.0 * c + g))
            dint[h, i] = d
            g = (2.0 * c + g) * d
        dint[h, 15] = 1.0 / (r32 * (1.0 + c1) + c + g)
    def cells(rows, cols, first):
        grid = lax.broadcasted_iota(jnp.int32, (rows, cols), 0)
        return jnp.where(grid == first, 1.0, 0.0).astype(BF16)

    lane = lax.broadcasted_iota(jnp.int32, (512, 256), 1)
    pick = cells(512, 256, a1 - 3 + 8 * (lane // 16) + lane % 16)
    myh[...] = mm(sh_ref[...], pick, NN).astype(BF16)
    myl[...] = mm(sl_ref[...], pick, NN).astype(BF16)
    lane = lax.broadcasted_iota(jnp.int32, (512, 128), 1)
    pick = cells(512, 128, a2 - 1 + 30 * core + lane)
    mz[...] = mm(sh_ref[...], pick, NN) + mm(sl_ref[...], pick, NN)
    pick = cells(512, 128, a2 - 1 + 30 * (lane // 64) + lane % 64)
    mzy[...] = mm(sh_ref[...], pick, NN) + mm(sl_ref[...], pick, NN)
    for h in range(2):
        high, low = split(jnp.concatenate([mzy[mine[h], :]] * 32, axis=0))
        mzt[h, 0] = high
        mzt[h, 1] = low

    def weights(cell, first, boxes, low_face, high_face):
        low_w = jnp.where(cell == first, 0.625, 0.0) + jnp.where(cell == first + 1, 0.375, 0.0)
        high_w = jnp.where(cell == first + boxes, 0.375, 0.0) + jnp.where(
            cell == first + boxes + 1, 0.625, 0.0
        )
        return jnp.where(low_face, low_w, 0.0) + jnp.where(high_face, high_w, 0.0)

    row = lax.broadcasted_iota(jnp.int32, (16, 512), 0)
    cell = lax.broadcasted_iota(jnp.int32, (16, 512), 1)
    wy = weights(cell, a1 - 1, 128, row == 0, row == 1).astype(BF16)
    wys[...] = mm(wy, sh_ref[...], NN) + mm(wy, sl_ref[...], NN)
    wz = weights(cell, a2 - 1, 64, row == 0, row == 1).astype(BF16)
    wz = mm(wz, sh_ref[...], NN) + mm(wz, sl_ref[...], NN)
    lane = lax.broadcasted_iota(jnp.int32, (512, 512), 1)
    pick = cells(512, 512, 256 * (lane // 256) + 8 * mid + lane % 8)
    wzh, wzl = split(wz)
    wz = mm(wzh, pick, NN) + mm(wzl, pick, NN)
    row = lax.broadcasted_iota(jnp.int32, (32, 256), 0)
    lane = lax.broadcasted_iota(jnp.int32, (32, 256), 1)
    row2 = lax.broadcasted_iota(jnp.int32, (16, 256), 0)
    lane2 = lax.broadcasted_iota(jnp.int32, (16, 256), 1)
    wx = weights(32 * pv + lane2 // 8, a0 - 1, 32, row2 < 8, row2 >= 8)
    wx = jnp.where(row2 % 8 == lane2 % 8, wx, 0.0)
    for h in range(2):
        for f in range(2):
            wall[h, 32 * f : 32 * f + 32, :] = jnp.where(
                row == lane // 8, wz[f : f + 1, halves[h]], 0.0
            )
        wall[h, 64:80, :] = wx
    for copy in halo:
        copy.wait_recv()
    pair = []
    for k, ref in enumerate((fa, fr)):
        view = ref.at[pl.ds(1, 8), :, own]
        copy = pltpu.make_async_remote_copy(
            src_ref=view, dst_ref=view, send_sem=sd.at[k], recv_sem=qd.at[k],
            device_id=partner, device_id_type=MESH,
        )
        copy.start()
        pair.append(copy)
    for copy in pair:
        copy.wait()
    fine_row = lax.broadcasted_iota(jnp.int32, (48, 256), 0) + 32 * gy
    fine_col = lax.broadcasted_iota(jnp.int32, (48, 256), 1)
    inside_y = (fine_row >= 8) & (fine_row < 520)
    sixth = jnp.where(inside_y, 1.0 / 6.0, 0.0)

    def layer(source, extra, k):
        v = source[k]
        total = (source[k - 1] + source[k + 1]) + extra[k]
        total = total + (pltpu.roll(v, 1, 0) + pltpu.roll(v, 47, 0))
        total = total + jnp.where(fine_col == 0, 0.0, pltpu.roll(v, 1, 1))
        return total + jnp.where(fine_col == 255, 0.0, pltpu.roll(v, 255, 1))

    for k in (0, 9):
        fa[k] = jnp.zeros((48, 256), F32)
        fb[k] = jnp.zeros((48, 256), F32)
    for k in range(1, 9):
        fa[k] = jnp.where(inside_y, fa[k], 0.0)
        fr[k] = fr[k] * (-1.0 / 16.0)
        es[k + 7] = fa[k]

    def alone(j, carry):
        for part, (source, target) in enumerate(((fa, fb), (fb, fa))):
            trace[0, 2 * j + part] = source[1]
            trace[1, 2 * j + part] = source[8]

            def four(k, c):
                for m in range(4):
                    index = 1 + 4 * k + m
                    target[index] = layer(source, fr, index) * sixth
                return c

            lax.fori_loop(0, 2, four, 0)
        return carry

    lax.fori_loop(0, 4, alone, 0)

    t2 = []
    t4 = [[], []]

    def second_and_eliminate(h):
        value = dd[h].reshape(512, 256)
        u[h] = dot3(split(value), s_pair, TN).reshape(32, 8, 512)
        first = -u[h, 0]
        u[h, 0] = first
        q0 = dtab[h, 30]

        def forward(i, carry):
            yv, q, e = carry
            w = u[h, i]
            yv = dtab[h, i - 1] * yv - w
            u[h, i] = yv
            q = q * dtab[h, 30 - i]
            return yv, q, e - q * w

        yv, _, e = lax.fori_loop(1, 31, forward, (first, q0, q0 * first))
        b = q0 * yv - u[h, 31]
        for j in range(4):
            start = 8 * (j // 2) + j % 2 + 4 * h
            m1[pl.ds(start, 8, stride=16), :] = e[:, 128 * j : 128 * j + 128]
            m1[pl.ds(start + 2, 8, stride=16), :] = b[:, 128 * j : 128 * j + 128]

    def send_ends():
        for k in range(1, 16):
            q = (pv + k) % 16
            t2.append(send(
                m1.at[pl.ds(pl.multiple_of(q * 8, 8), 8), :], r1.at[pv], s2.at[k], q2.at[pv],
                to_row(q),
            ))
        r1[pv] = m1[pl.ds(pl.multiple_of(pv * 8, 8), 8), :]

    def separators():
        for h in range(2):
            ys = []
            prev = None
            for p in range(16):
                end = r1[p, 4 * h + 2 : 4 * h + 4, :]
                if p < 15:
                    end = end + r1[p + 1, 4 * h : 4 * h + 2, :]
                end = rint[h] * end
                prev = end if p == 0 else end + dint[h, p - 1] * prev
                ys.append(prev)
            m2[0, 4 * h : 4 * h + 2, :] = jnp.zeros((2, 128), F32)
            sol = dint[h, 15] * ys[15]
            m2[15, 4 * h + 2 : 4 * h + 4, :] = sol
            for p in range(14, -1, -1):
                sol = dint[h, p] * (sol + ys[p])
                m2[p + 1, 4 * h : 4 * h + 2, :] = sol
                m2[p, 4 * h + 2 : 4 * h + 4, :] = sol
        for k in range(1, 16):
            q = (pv + k) % 16
            t2.append(send(
                m2.at[q], r2.at[pl.ds(pl.multiple_of(pv * 8, 8), 8), :], s3.at[k], q3.at[pv],
                to_row(q),
            ))
        r2[pl.ds(pl.multiple_of(pv * 8, 8), 8), :] = m2[pv]

    def wait_separators():
        for k in range(1, 16):
            q = (pv + k) % 16
            view = r2.at[pl.ds(pl.multiple_of(q * 8, 8), 8), :]
            pltpu.make_async_remote_copy(
                src_ref=view, dst_ref=view, send_sem=s3.at[k], recv_sem=q3.at[q],
                device_id=here, device_id_type=MESH,
            ).wait_recv()

    def substitute(h):
        starts = [8 * (j // 2) + j % 2 + 4 * h for j in range(4)]
        left = jnp.concatenate([r2[pl.ds(j, 8, stride=16), :] for j in starts], axis=1)
        right = jnp.concatenate([r2[pl.ds(j + 2, 8, stride=16), :] for j in starts], axis=1)

        def spread(i, t):
            u[h, i] = u[h, i] + t
            return dtab[h, i] * t

        lax.fori_loop(0, 31, spread, left)
        u[h, 31] = right

        def backward(k, v):
            i = 30 - k
            v = dtab[h, i] * (v + u[h, i])
            u[h, i] = v
            return v

        lax.fori_loop(0, 31, backward, right)
        high, low = split(u[h].reshape(256, 512))
        uh[h] = high
        ul[h] = low

    def inverse_second(h):
        for copy in t1[h]:
            copy.wait_send()
        zb[h] = dot3(s_pair, (uh[h], ul[h]), NT).reshape(32, 16, 256)

    def send_last(h, lo, hi):
        for i in range(lo, hi):
            target, block = to_real(PEERS[i])
            t4[h].append(
                send(zb.at[h, block], gg.at[h, mid], s4.at[h, i], q4.at[h, mid], target)
            )

    tt = []

    def send_traces(part):
        sweeps = pl.ds(4 * part, 4)
        for side, ox in enumerate((-1, 1)):
            tt.append(send(
                trace.at[side, sweeps, :, own], tin.at[1 - side, sweeps, :, own],
                st.at[side, part], qt.at[1 - side, part], beside(ox, 0),
            ))

    for s in range(32):
        arrived(dd.at[0], q1.at[0], s)
    second_and_eliminate(0)
    for s in range(32):
        arrived(dd.at[1], q1.at[1], s)
    second_and_eliminate(1)
    send_ends()
    send_traces(0)
    send_traces(1)
    for k in range(1, 16):
        arrived(r1, q2, (pv + k) % 16)
    separators()
    wait_separators()
    substitute(0)
    inverse_second(0)
    send_last(0, 0, CUT4A)
    substitute(1)
    face = []
    line = []
    cut_x = []
    row = lax.broadcasted_iota(jnp.int32, (32, 256), 0)
    lanes = lax.broadcasted_iota(jnp.int32, (32, 256), 1)

    def faces(h):
        pair_h = (uh[h], ul[h])
        rows = dot3(split(wall[h]), pair_h, NN)
        face.append(rows[:64])
        cut_x.append(rows[64:])
        ay = dot3(split(wys[...]), pair_h, NT)
        both = jnp.concatenate(
            [jnp.where(row == lanes // 8, ay[f : f + 1, :], 0.0) for f in range(2)], axis=0
        )
        line.append(dot3(split(both), (mzt[h, 0], mzt[h, 1]), NN))

    faces(0)
    faces(1)
    rows = jnp.concatenate([face[0] + face[1], cut_x[0], cut_x[1]], axis=0)
    rows = dot3(split(rows), (myh[...], myl[...]), NN)
    lane = lax.broadcasted_iota(jnp.int32, (8, 128), 1) // 16
    for f in range(2):
        for t in range(2):
            cols = slice(128 * t, 128 * t + 128)
            v = [rows[32 * f + 8 * k : 32 * f + 8 * k + 8, cols] for k in range(4)]
            for g in range(2):
                for h in range(2):
                    start = 64 + 16 * h + 8 * g
                    v.append(rows[start : start + 8, cols])
            for q, w in enumerate(exchange8(v, lane)):
                mzx[16 * f + 8 * t + q] = w
    line_sum = line[0] + line[1]
    half = lax.broadcasted_iota(jnp.int32, (16, 128), 1) < 64
    for f in range(2):
        top, bottom = line_sum[32 * f : 32 * f + 16], line_sum[32 * f + 16 : 32 * f + 32]
        my[f, 0] = jnp.where(half, top, pltpu.roll(bottom, 64, 1))
        my[f, 1] = jnp.where(half, pltpu.roll(top, 64, 1), bottom)
    tz = []
    for i, o in enumerate(PEERS):
        target, block = to_real(o)
        tz.append(send(mzx.at[block], rzx.at[mid], sz.at[i], qz.at[mid], target))
    for f in range(2):
        for g in range(2):
            tz.append(send(
                my.at[f, g], ry.at[mid], sy.at[2 * f + g], qy.at[mid],
                device(g, x, 7 * f, lv + 4 * f),
            ))
    send_last(0, CUT4A, 32)
    inverse_second(1)
    send_last(1, 0, CUT4B)
    te = []
    for part in range(2):
        sweeps = pl.ds(4 * part, 4)
        for side in range(2):
            view = tin.at[side, sweeps, :, own]
            pltpu.make_async_remote_copy(
                src_ref=view, dst_ref=view, send_sem=st.at[side, part],
                recv_sem=qt.at[side, part], device_id=here, device_id_type=MESH,
            ).wait_recv()
            te.append(send(view, view, se.at[side, part], qe.at[side, part], partner))
    for copy in te:
        copy.wait_recv()
    def factor(k):
        inside_x = (k + 8 * gx >= 8) & (k + 8 * gx < 136)
        return jnp.where(inside_x, sixth, 0.0)

    ends = (jnp.where(gx == 0, 0.0, sixth), jnp.where(gx == 15, 0.0, sixth))
    for k in (4, 5, 6, 7, 16, 17, 18, 19):
        es[k] = jnp.zeros((48, 256), F32)
        ed[k] = jnp.zeros((48, 256), F32)
    for k in (3, 4, 5, 6, 17, 18, 19, 20):
        et[k] = jnp.zeros((48, 256), F32)
    for k in range(8, 16):
        ed[k] = fr[k - 7]
    for j in range(8):
        source, target = ((es, et), (et, es))[j % 2]
        depth = min(j + 1, 7 - j)

        def some(k, c, source=source, target=target, first=8 - depth, step=WIDE):
            for m in range(step):
                index = first + step * k + m
                target[index] = layer(source, ed, index) * factor(index)
            return c

        layers = 8 + 2 * depth
        lax.fori_loop(0, layers // WIDE, some, 0)
        if layers % WIDE:
            some(0, 0, first=8 - depth + layers // WIDE * WIDE, step=layers % WIDE)
        target[8] = target[8] + tin[0, j] * ends[0]
        target[15] = target[15] + tin[1, j] * ends[1]
    for s in range(32):
        arrived(rzx, qz, s)
    zsum = rzx[0]
    for s in range(1, 32):
        zsum = zsum + rzx[s]
    got = rzx[...].reshape(256, 128)
    parts = [full(got, mz[256 * k : 256 * k + 256, :], TN) for k in range(2)]
    for f in range(2):
        m6[f] = parts[0][64 + 32 * f : 80 + 32 * f] + parts[1][80 + 32 * f : 96 + 32 * f]
    row = lax.broadcasted_iota(jnp.int32, (128, 32), 0)
    col = lax.broadcasted_iota(jnp.int32, (128, 32), 1)
    pick = jnp.where(a0 - 3 + 2 * (row // 8) + row % 8 == 32 * gx + col, 1.0, 0.0)
    spread_z = jnp.concatenate([jnp.where(lane == h, zsum, 0.0) for h in range(4)], axis=0)
    m5[:, 0] = full(pick, spread_z, NN).reshape(16, 8, 128)
    m5[:, 1] = jnp.zeros((16, 8, 128), F32)
    at_y = (gy == 0) | (gy == 15)

    @pl.when(at_y)
    def _():
        for s in range(32):
            arrived(ry, qy, s)
        ysum = ry[0]
        for s in range(1, 32):
            ysum = ysum + ry[s]
        top = full(pick[:, :16], ysum, NN)
        bottom = full(pick[:, 16:], ysum, NN)
        left_half = lax.broadcasted_iota(jnp.int32, (128, 128), 1) < 64
        m5[:, 1] = jnp.where(left_half, top, bottom).reshape(16, 8, 128)

    t5 = []
    for k in range(1, 16):
        q = (gx + k) % 16
        copy = pltpu.make_async_remote_copy(
            src_ref=m5.at[q], dst_ref=r5.at[gx], send_sem=s5.at[k], recv_sem=q5.at[gx],
            device_id=real_row(q), device_id_type=MESH,
        )
        copy.start()
        t5.append(copy)
    r5[gx] = m5[gx]
    for f in range(2):
        end = 15 * f
        copy = pltpu.make_async_remote_copy(
            src_ref=m6.at[f], dst_ref=r6.at[gx], send_sem=s6.at[f], recv_sem=q6.at[gx],
            device_id=real_row(end), device_id_type=MESH,
        )

        @pl.when(gx != end)
        def _():
            copy.start()

        @pl.when(gx == end)
        def _():
            r6[gx] = m6[f]


    send_last(1, CUT4B, 32)
    for s in range(32):
        arrived(gg.at[0], q4.at[0], s)
    def inverse_third(h):
        swap_groups(gg.at[h], za, 0, 256 * h)
        rows_h = tuple(part[halves[h], :] for part in s_pair)
        return dot3(split(za[:, :, halves[h]].reshape(512, 256)), rows_h, NN).reshape(32, 16, 512)

    out_ref[...] = inverse_third(0)
    for s in range(32):
        arrived(gg.at[1], q4.at[1], s)
    out_ref[...] = out_ref[...] + inverse_third(1)
    for k in range(1, 16):
        arrived(r5, q5, (gx + k) % 16)
    def interpolate(fine, cell):
        scaled = 2 * fine + 5
        bottom = scaled // 8
        t = (scaled % 8).astype(F32) * 0.125
        return jnp.where(cell == bottom, 1.0 - t, 0.0) + jnp.where(cell == bottom + 1, t, 0.0)

    def grid(shape):
        return (lax.broadcasted_iota(jnp.int32, shape, 0), lax.broadcasted_iota(jnp.int32, shape, 1))

    row, col = grid((24, 8))
    int_x = interpolate(row, col)
    row, col = grid((128, 128))
    int_y = jnp.where((col < 64) & (row < 48), interpolate(row, col % 16), 0.0)
    zb5 = r5[0, 0]
    yb5 = r5[0, 1]
    for s in range(1, 16):
        zb5 = zb5 + r5[s, 0]
        yb5 = yb5 + r5[s, 1]
    ghost_z = full(full(int_x, zb5, NN), int_y, NT)
    row, col = grid((24, 128))
    inside = (row + 8 * gx >= 8) & (row + 8 * gx < 136) & (col < 48)
    inside = inside & (col + 32 * gy >= 8) & (col + 32 * gy < 520)
    sixth_z = jnp.where(inside, 1.0 / 6.0, 0.0)
    plane = []
    for j in range(8):
        new = []
        for k in range(j + 1):
            total = ghost_z if k == 0 else plane[k - 1]
            if k + 1 < j:
                total = total + plane[k + 1]
            if k < j:
                v = plane[k]
                total = total + (pltpu.roll(v, 1, 0) + pltpu.roll(v, 23, 0))
                total = total + (pltpu.roll(v, 1, 1) + pltpu.roll(v, 127, 1))
            new.append(total * sixth_z)
        plane = new
    for k in range(8):
        gz[pl.ds(k, 24, stride=8), :] = plane[k]
    row, col = grid((8, 128))
    place = jnp.where(col == jnp.where(core == 0, row, 127 - row), 1.0, 0.0)
    for k in range(8):
        part = full(gz[8 * (k + 8) : 8 * (k + 8) + 8, :], place, TN)
        fine_ref[k] = es[k + 8, 8:40, own] + part[8:40]

    row, col = grid((128, 256))
    int_z = interpolate(col, row % 64 + 30 * core)

    row8 = lax.broadcasted_iota(jnp.int32, (8, 256), 0)
    col8 = lax.broadcasted_iota(jnp.int32, (8, 256), 1)
    for f in range(2):
        @pl.when(gy == 15 * f)
        def _():
            ghost_y = full(full(int_x, yb5, NN), int_z, NN)
            edge = 7 * f
            for k in range(24):
                yd[k] = jnp.where(row8 == edge, ghost_y[k : k + 1], 0.0)
            for j in range(8):
                source, target = ((ya, yb), (yb, ya))[j % 2]

                def one(k, c, source=source, target=target, j=j):
                    total = yd[k]
                    if j:
                        v = source[k]
                        total = total + source[k - 1] + source[k + 1]
                        total = total + jnp.where(row8 == 0, 0.0, pltpu.roll(v, 1, 0))
                        total = total + jnp.where(row8 == 7, 0.0, pltpu.roll(v, 7, 0))
                        total = total + jnp.where(col8 == 0, 0.0, pltpu.roll(v, 1, 1))
                        total = total + jnp.where(col8 == 255, 0.0, pltpu.roll(v, 255, 1))
                    inside_x = (k + 8 * gx >= 8) & (k + 8 * gx < 136)
                    target[k] = total * jnp.where(inside_x, 1.0 / 6.0, 0.0)
                    return c

                for k in range(j + 1, 23 - j):
                    one(k, 0)
            rows = pl.ds(24 * f, 8)
            for k in range(8):
                fine_ref[k, rows, :] = fine_ref[k, rows, :] + ya[k + 8, :, own]

    for f in range(2):
        @pl.when(gx == 15 * f)
        def _():
            for k in range(16):
                if k != 15 * f:
                    arrived(r6, q6, k)
            xb6 = r6[0]
            for s in range(1, 16):
                xb6 = xb6 + r6[s]
            row, col = grid((48, 16))
            near_y = interpolate(row, col)
            row, col = grid((128, 256))
            near_z = jnp.where(row < 64, int_z, 0.0)
            ghost_x = full(full(near_y, xb6, NN), near_z, NN)
            for k in range(1, 9):
                fr[k] = jnp.zeros((48, 256), F32)
                fa[k] = jnp.zeros((48, 256), F32)
                fb[k] = jnp.zeros((48, 256), F32)
            fr[1 + 7 * f] = ghost_x
            for j in range(8):
                source, target = ((fa, fb), (fb, fa))[j % 2]
                for k in range(j + 1):
                    index = 8 - k if f else 1 + k
                    target[index] = layer(source, fr, index) * sixth
            for k in range(8):
                fine_ref[k] = fine_ref[k] + fa[k + 1, 8:40, own]

    for copy in t2 + t4[0] + t4[1] + tz + t5 + halo + tt + te:
        copy.wait_send()
    for f in range(2):
        @pl.when(gx != 15 * f)
        def _():
            pltpu.make_async_remote_copy(
                src_ref=m6.at[f], dst_ref=r6.at[gx], send_sem=s6.at[f], recv_sem=q6.at[gx],
                device_id=real_row(15 * f), device_id_type=MESH,
            ).wait_send()


def body(density, fine_density, fine_start, anchor):
    high, low, lam = tables()
    vm = pl.BlockSpec(memory_space=pltpu.VMEM)
    dma = pltpu.SemaphoreType.DMA

    def f32(*shape):
        return pltpu.VMEM(shape, F32)

    def b16(*shape):
        return pltpu.VMEM(shape, BF16)

    big = f32(32, 16, 512)
    return pl.pallas_call(
        kernel,
        out_shape=(
            jax.ShapeDtypeStruct((32, 16, 512), F32), jax.ShapeDtypeStruct((8, 32, 128), F32)
        ),
        in_specs=[pl.BlockSpec(memory_space=pl.ANY)] * 9,
        out_specs=(vm, vm),
        scratch_shapes=[
            pltpu.SMEM((3,), jnp.int32), f32(8, 512), f32(2, 8, 128), f32(8, 128),
            big, f32(8, 32, 128), f32(8, 32, 128), b16(512, 512), b16(512, 512),
            big, f32(2, 32, 16, 256), f32(2, 32, 16, 256), f32(2, 32, 16, 256),
            f32(2, 32, 8, 512), f32(2, 31, 8, 512),
            f32(128, 128), f32(16, 8, 128), f32(16, 8, 128), f32(128, 128),
            f32(2, 16, 2, 128), f32(2, 2, 128),
            b16(2, 256, 512), b16(2, 256, 512), b16(512, 256), b16(512, 256),
            f32(512, 128), f32(512, 128), b16(2, 2, 256, 128), f32(2, 80, 256), f32(16, 512),
            f32(32, 8, 128), f32(32, 8, 128), f32(2, 2, 16, 128), f32(32, 16, 128),
            f32(16, 2, 8, 128), f32(16, 2, 8, 128), f32(2, 16, 128), f32(16, 16, 128),
            f32(24, 48, 256), f32(24, 48, 256), f32(24, 48, 256),
            f32(10, 48, 256), f32(10, 48, 256), f32(10, 48, 256),
            f32(2, 8, 48, 256), f32(2, 8, 48, 256), f32(192, 128),
            f32(24, 8, 256), f32(24, 8, 256), f32(24, 8, 256),
            dma((2, 32)), dma((2, 32)), dma((16,)), dma((16,)), dma((16,)), dma((16,)),
            dma((2, 32)), dma((2, 32)), dma((4,)), dma((4,)), dma((2,)), dma((2,)),
            dma((32,)), dma((32,)), dma((4,)), dma((32,)), dma((16,)), dma((16,)),
            dma((2,)), dma((16,)), dma((10,)), dma((2, 2)), dma((2, 2)), dma((2, 2)), dma((2, 2)),
        ],
        compiler_params=pltpu.CompilerParams(
            collective_id=0, has_side_effects=True, vmem_limit_bytes=56 << 20
        ),
    )(anchor, jnp.asarray(np.tile(lam.reshape(1, 512), (8, 1))),
      jnp.asarray(np.tile(lam.reshape(512, 1), (1, 128))),
      jnp.asarray(np.tile(lam.reshape(4, 128), (2, 1))), density, fine_density, fine_start,
      jnp.asarray(high), jnp.asarray(low))


def solution(mesh):
    return jax.shard_map(
        body,
        mesh=mesh,
        in_specs=(P("gx", ("grp", "gy"), None), P("gx", "gy", "grp"), P("gx", "gy", "grp"), P()),
        out_specs=(P("gx", ("grp", "gy"), None), P("gx", "gy", "grp")),
        check_vma=False,
    )
```

time: 119 us -> 112 us (0.941)
  Pallas kernels: 115 us -> 109 us
    pallas_call x1, Pallas kernels: 115 us -> 109 us  [body(): pl.pallas_call(kernel, out_shape=(jax.ShapeDtypeStruct((32, 16, 512), F32...]
where the time goes in v4:
time: 112 us
  Pallas kernels  109 us (97%)
  local copies, waits for them, and re-layouts  3 us (3%)
    pallas_call x1, Pallas kernels, body(): pl.pallas_call(kernel, out_shape=(jax.ShapeDtypeStruct((32, 16, 512), F32...  109 us
    unnamed x4, local copies, waits for them, and re-layouts  3 us

profile of v4, /device:TPU:1, one launch (start us, length us, event | category | flops | bytes accessed | tf_op | source)
XLA Modules:
  0.0 112.3 jit_solution(2479940480741789758)
XLA Ops:
  0.6 108.6 %shard_map.104 = (f32[32,16,512]{2,1,0:T(8,128)}, f32[8,32,128]{2,1,0:T(8,128)}) custom-call(s32[3]{0:T(128)} %anchor_hbm.1, f32[8,512]{1,0:T(8,128)} %constant.10.clone.lamr_hbm, f32[512,128]{1,0:T(8,128)} %constant.11.clone.lamc_hbm, f32[8,128]{1,0:T(8,128)} %constant.12.clone.lamq_hbm, f32[32,16,512]{2,1,0:T(8,128)} %x_hbm.1, f32[8,32,128]{2,1,0:T(8,128)} %fd_hbm.1, ...), custom_call_target="tpu_custom_call" | custom-call | tf_op jit(solution)/shard_map/pallas_call | solution.py:767
  109.3 0.0 copy-start
  109.3 2.3 %copy.13 = f32[32,16,512]{2,1,0:T(8,128)} copy(f32[32,16,512]{2,1,0:T(8,128)} %get-tuple-element.4) | data formatting | bytes 2097152
  111.6 0.0 copy-done
  111.6 0.7 copy.14
Async XLA Ops:
  109.3 2.4 %copy-start = (f32[8,32,128]{2,1,0:T(8,128)S(1)}, f32[8,32,128]{2,1,0:T(8,128)}, u32[]{:S(2)}) copy-start(f32[8,32,128]{2,1,0:T(8,128)} %get-tuple-element.5) | copy-start | bytes 393220

commit v5 on v4

--- a/solution.py
+++ b/solution.py
@@ -109,10 +109,10 @@
 def kernel(
     anchor_hbm, lamr_hbm, lamc_hbm, lamq_hbm, x_hbm, fd_hbm, fs_hbm, sh_hbm, sl_hbm, out_ref, fine_ref,
     anchor, lamr_ref, lamc_ref, lamq_ref, x_ref, fd_ref, fs_ref, sh_ref, sl_ref,
-    za, zb, dd, gg, u, dtab, m1, r1, m2, r2, dint, rint, uh, ul, myh, myl, mz, mzy, mzt, wall, wys,
+    za, zb, dd, gg, u, dtab, m1, r1, m2, r2, dint, rint, uh, ul, myh, myl, mz, wall, wys,
     mzx, rzx, my, ry, m5, r5, m6, r6, es, et, ed, fa, fb, fr, trace, tin, gz, ya, yb, yd,
     s1, q1, s2, q2, s3, q3, s4, q4, sh1, qh1, sd, qd, sz, qz, sy, qy, s5, q5, s6, q6, sin,
-    st, qt, se, qe,
+    st, qt, se, qe, sv, qv,
 ):
     core = lax.axis_index("grp")
     gx = lax.axis_index("gx")
@@ -177,11 +177,17 @@
             recv_sem=sem.at[index], device_id=here, device_id_type=MESH,
         ).wait_recv()
 
-    def send(src, dst, send_sem, recv_sem, target):
-        copy = pltpu.make_async_remote_copy(
+    has_y = (gy > 0, gy < 15)
+    has_x = (gx > 0, gx < 15)
+
+    def prepare(src, dst, send_sem, recv_sem, target):
+        return pltpu.make_async_remote_copy(
             src_ref=src, dst_ref=dst, send_sem=send_sem, recv_sem=recv_sem,
             device_id=target, device_id_type=MESH,
         )
+
+    def send(*args):
+        copy = prepare(*args)
         copy.start()
         return copy
 
@@ -217,10 +223,12 @@
         rows = pl.ds(0, 8) if oy < 0 else pl.ds(24, 8)
         to_rows = pl.ds(40, 8) if oy < 0 else pl.ds(0, 8)
         for part, (src, dst) in enumerate(((fs_ref, fa), (fd_ref, fr))):
-            halo.append(send(
+            copy = prepare(
                 src.at[:, rows, :], dst.at[pl.ds(1, 8), to_rows, own],
                 sh1.at[2 * k + part], qh1.at[2 * k + part], beside(0, oy),
-            ))
+            )
+            pl.when(has_y[k])(copy.start)
+            halo.append((copy, has_y[k], has_y[1 - k]))
     send_first(0, 0, 32)
     forward_third(1)
     send_first(1, 0, CUT1)
@@ -260,13 +268,6 @@
     lane = lax.broadcasted_iota(jnp.int32, (512, 128), 1)
     pick = cells(512, 128, a2 - 1 + 30 * core + lane)
     mz[...] = mm(sh_ref[...], pick, NN) + mm(sl_ref[...], pick, NN)
-    pick = cells(512, 128, a2 - 1 + 30 * (lane // 64) + lane % 64)
-    mzy[...] = mm(sh_ref[...], pick, NN) + mm(sl_ref[...], pick, NN)
-    for h in range(2):
-        high, low = split(jnp.concatenate([mzy[mine[h], :]] * 32, axis=0))
-        mzt[h, 0] = high
-        mzt[h, 1] = low
-
     def weights(cell, first, boxes, low_face, high_face):
         low_w = jnp.where(cell == first, 0.625, 0.0) + jnp.where(cell == first + 1, 0.375, 0.0)
         high_w = jnp.where(cell == first + boxes, 0.375, 0.0) + jnp.where(
@@ -296,8 +297,8 @@
                 row == lane // 8, wz[f : f + 1, halves[h]], 0.0
             )
         wall[h, 64:80, :] = wx
-    for copy in halo:
-        copy.wait_recv()
+    for copy, _, comes in halo:
+        pl.when(comes)(copy.wait_recv)
     pair = []
     for k, ref in enumerate((fa, fr)):
         view = ref.at[pl.ds(1, 8), :, own]
@@ -326,7 +327,7 @@
         fb[k] = jnp.zeros((48, 256), F32)
     for k in range(1, 9):
         fa[k] = jnp.where(inside_y, fa[k], 0.0)
-        fr[k] = fr[k] * (-1.0 / 16.0)
+        fr[k] = jnp.where(inside_y, fr[k], 0.0) * (-1.0 / 16.0)
         es[k + 7] = fa[k]
 
     def alone(j, carry):
@@ -454,10 +455,13 @@
     def send_traces(part):
         sweeps = pl.ds(4 * part, 4)
         for side, ox in enumerate((-1, 1)):
-            tt.append(send(
-                trace.at[side, sweeps, :, own], tin.at[1 - side, sweeps, :, own],
+            copy = prepare(
+                trace.at[side, sweeps, pl.ds(8, 32), own],
+                tin.at[1 - side, sweeps, pl.ds(8, 32), own],
                 st.at[side, part], qt.at[1 - side, part], beside(ox, 0),
-            ))
+            )
+            pl.when(has_x[side])(copy.start)
+            tt.append((copy, has_x[side]))
 
     for s in range(32):
         arrived(dd.at[0], q1.at[0], s)
@@ -475,23 +479,45 @@
     substitute(0)
     inverse_second(0)
     send_last(0, 0, CUT4A)
+    for part in range(2):
+        sweeps = pl.ds(4 * part, 4)
+        for side in range(2):
+            view = tin.at[side, sweeps, pl.ds(8, 32), own]
+            copy = pltpu.make_async_remote_copy(
+                src_ref=view, dst_ref=view, send_sem=st.at[side, part],
+                recv_sem=qt.at[side, part], device_id=here, device_id_type=MESH,
+            )
+            pl.when(has_x[side])(copy.wait_recv)
+    for side in range(2):
+        @pl.when(jnp.logical_not(has_x[side]))
+        def _():
+            tin[side, :, 8:40, own] = jnp.zeros((8, 32, 128), F32)
+
+        @pl.when(jnp.logical_not(has_y[side]))
+        def _():
+            tin[:, :, 40 * side : 40 * side + 8, own] = jnp.zeros((2, 8, 8, 128), F32)
+
+    for k, oy in enumerate((-1, 1)):
+        rows = pl.ds(8, 8) if oy < 0 else pl.ds(32, 8)
+        to_rows = pl.ds(40, 8) if oy < 0 else pl.ds(0, 8)
+        copy = prepare(
+            tin.at[:, :, rows, own], tin.at[:, :, to_rows, own], sv.at[k], qv.at[k], beside(0, oy)
+        )
+        pl.when(has_y[k])(copy.start)
+        tt.append((copy, has_y[k]))
     substitute(1)
     face = []
-    line = []
     cut_x = []
-    row = lax.broadcasted_iota(jnp.int32, (32, 256), 0)
-    lanes = lax.broadcasted_iota(jnp.int32, (32, 256), 1)
 
     def faces(h):
         pair_h = (uh[h], ul[h])
         rows = dot3(split(wall[h]), pair_h, NN)
         face.append(rows[:64])
         cut_x.append(rows[64:])
-        ay = dot3(split(wys[...]), pair_h, NT)
-        both = jnp.concatenate(
-            [jnp.where(row == lanes // 8, ay[f : f + 1, :], 0.0) for f in range(2)], axis=0
-        )
-        line.append(dot3(split(both), (mzt[h, 0], mzt[h, 1]), NN))
+        line = dot3(split(wys[...]), pair_h, NT)
+        for f in range(2):
+            for t in range(2):
+                my[f, 2 * h + t : 2 * h + t + 1, :] = line[f : f + 1, 128 * t : 128 * t + 128]
 
     faces(0)
     faces(1)
@@ -508,12 +534,6 @@
                     v.append(rows[start : start + 8, cols])
             for q, w in enumerate(exchange8(v, lane)):
                 mzx[16 * f + 8 * t + q] = w
-    line_sum = line[0] + line[1]
-    half = lax.broadcasted_iota(jnp.int32, (16, 128), 1) < 64
-    for f in range(2):
-        top, bottom = line_sum[32 * f : 32 * f + 16], line_sum[32 * f + 16 : 32 * f + 32]
-        my[f, 0] = jnp.where(half, top, pltpu.roll(bottom, 64, 1))
-        my[f, 1] = jnp.where(half, pltpu.roll(top, 64, 1), bottom)
     tz = []
     for i, o in enumerate(PEERS):
         target, block = to_real(o)
@@ -521,24 +541,22 @@
     for f in range(2):
         for g in range(2):
             tz.append(send(
-                my.at[f, g], ry.at[mid], sy.at[2 * f + g], qy.at[mid],
+                my.at[f], ry.at[mid], sy.at[2 * f + g], qy.at[mid],
                 device(g, x, 7 * f, lv + 4 * f),
             ))
     send_last(0, CUT4A, 32)
     inverse_second(1)
     send_last(1, 0, CUT4B)
-    te = []
-    for part in range(2):
-        sweeps = pl.ds(4 * part, 4)
-        for side in range(2):
-            view = tin.at[side, sweeps, :, own]
-            pltpu.make_async_remote_copy(
-                src_ref=view, dst_ref=view, send_sem=st.at[side, part],
-                recv_sem=qt.at[side, part], device_id=here, device_id_type=MESH,
-            ).wait_recv()
-            te.append(send(view, view, se.at[side, part], qe.at[side, part], partner))
-    for copy in te:
-        copy.wait_recv()
+    for k in range(2):
+        view = tin.at[:, :, pl.ds(40 - 40 * k, 8), own]
+        copy = pltpu.make_async_remote_copy(
+            src_ref=view, dst_ref=view, send_sem=sv.at[k], recv_sem=qv.at[k], device_id=here,
+            device_id_type=MESH,
+        )
+        pl.when(has_y[1 - k])(copy.wait_recv)
+    view = tin.at[:, :, :, own]
+    te = send(view, view, se.at[0], qe.at[0], partner)
+    te.wait_recv()
     def factor(k):
         inside_x = (k + 8 * gx >= 8) & (k + 8 * gx < 136)
         return jnp.where(inside_x, sixth, 0.0)
@@ -588,13 +606,23 @@
     def _():
         for s in range(32):
             arrived(ry, qy, s)
-        ysum = ry[0]
-        for s in range(1, 32):
-            ysum = ysum + ry[s]
-        top = full(pick[:, :16], ysum, NN)
-        bottom = full(pick[:, 16:], ysum, NN)
-        left_half = lax.broadcasted_iota(jnp.int32, (128, 128), 1) < 64
-        m5[:, 1] = jnp.where(left_half, top, bottom).reshape(16, 8, 128)
+        lane8 = lax.broadcasted_iota(jnp.int32, (32, 128), 1) % 8
+        group = lax.broadcasted_iota(jnp.int32, (16, 128), 0)
+        member = lax.broadcasted_iota(jnp.int32, (16, 128), 1) // 8
+        gather = jnp.where(group == member, 1.0, 0.0)
+        part = []
+        for t in range(2):
+            total = None
+            for h in range(2):
+                v = ry[:, 2 * h + t, :]
+                v = jnp.concatenate([jnp.where(lane8 == k, v, 0.0) for k in range(8)], axis=0)
+                modes = jnp.concatenate(
+                    [mz[pl.ds(256 * h + k, 32, stride=8), :] for k in range(8)], axis=0
+                )
+                w = full(v, modes, TN)
+                total = w if total is None else total + w
+            part.append(full(gather, total, NN))
+        m5[:, 1] = full(pick, jnp.concatenate(part, axis=0), NN).reshape(16, 8, 128)
 
     t5 = []
     for k in range(1, 16):
@@ -681,7 +709,7 @@
         fine_ref[k] = es[k + 8, 8:40, own] + part[8:40]
 
     row, col = grid((128, 256))
-    int_z = interpolate(col, row % 64 + 30 * core)
+    int_z = jnp.where(row < 64, interpolate(col, row + 30 * core), 0.0)
 
     row8 = lax.broadcasted_iota(jnp.int32, (8, 256), 0)
     col8 = lax.broadcasted_iota(jnp.int32, (8, 256), 1)
@@ -725,9 +753,7 @@
                 xb6 = xb6 + r6[s]
             row, col = grid((48, 16))
             near_y = interpolate(row, col)
-            row, col = grid((128, 256))
-            near_z = jnp.where(row < 64, int_z, 0.0)
-            ghost_x = full(full(near_y, xb6, NN), near_z, NN)
+            ghost_x = full(full(near_y, xb6, NN), int_z, NN)
             for k in range(1, 9):
                 fr[k] = jnp.zeros((48, 256), F32)
                 fa[k] = jnp.zeros((48, 256), F32)
@@ -741,8 +767,10 @@
             for k in range(8):
                 fine_ref[k] = fine_ref[k] + fa[k + 1, 8:40, own]
 
-    for copy in t2 + t4[0] + t4[1] + tz + t5 + halo + tt + te:
+    for copy in t2 + t4[0] + t4[1] + tz + t5 + [te]:
         copy.wait_send()
+    for copy, sent, *_ in halo + tt:
+        pl.when(sent)(copy.wait_send)
     for f in range(2):
         @pl.when(gx != 15 * f)
         def _():
@@ -779,8 +807,8 @@
             f32(128, 128), f32(16, 8, 128), f32(16, 8, 128), f32(128, 128),
             f32(2, 16, 2, 128), f32(2, 2, 128),
             b16(2, 256, 512), b16(2, 256, 512), b16(512, 256), b16(512, 256),
-            f32(512, 128), f32(512, 128), b16(2, 2, 256, 128), f32(2, 80, 256), f32(16, 512),
-            f32(32, 8, 128), f32(32, 8, 128), f32(2, 2, 16, 128), f32(32, 16, 128),
+            f32(512, 128), f32(2, 80, 256), f32(16, 512),
+            f32(32, 8, 128), f32(32, 8, 128), f32(2, 4, 128), f32(32, 4, 128),
             f32(16, 2, 8, 128), f32(16, 2, 8, 128), f32(2, 16, 128), f32(16, 16, 128),
             f32(24, 48, 256), f32(24, 48, 256), f32(24, 48, 256),
             f32(10, 48, 256), f32(10, 48, 256), f32(10, 48, 256),
@@ -789,7 +817,7 @@
             dma((2, 32)), dma((2, 32)), dma((16,)), dma((16,)), dma((16,)), dma((16,)),
             dma((2, 32)), dma((2, 32)), dma((4,)), dma((4,)), dma((2,)), dma((2,)),
             dma((32,)), dma((32,)), dma((4,)), dma((32,)), dma((16,)), dma((16,)),
-            dma((2,)), dma((16,)), dma((10,)), dma((2, 2)), dma((2, 2)), dma((2, 2)), dma((2, 2)),
+            dma((2,)), dma((16,)), dma((10,)), dma((2, 2)), dma((2, 2)), dma((1,)), dma((1,)), dma((2,)), dma((2,)),
         ],
         compiler_params=pltpu.CompilerParams(
             collective_id=0, has_side_effects=True, vmem_limit_bytes=56 << 20

time: 112 us -> 105 us (0.938)
  Pallas kernels: 109 us -> 102 us
    pallas_call x1, Pallas kernels: 109 us -> 102 us  [body(): pl.pallas_call(kernel, out_shape=(jax.ShapeDtypeStruct((32, 16, 512), F32...]
where the time goes in v5:
time: 105 us
  Pallas kernels  102 us (97%)
  local copies, waits for them, and re-layouts  3 us (3%)
    pallas_call x1, Pallas kernels, body(): pl.pallas_call(kernel, out_shape=(jax.ShapeDtypeStruct((32, 16, 512), F32...  102 us
    unnamed x4, local copies, waits for them, and re-layouts  3 us

profile of v5, /device:TPU:1, one launch (start us, length us, event | category | flops | bytes accessed | tf_op | source)
XLA Modules:
  0.0 105.2 jit_solution(3638135125920497986)
XLA Ops:
  0.6 101.5 %shard_map.104 = (f32[32,16,512]{2,1,0:T(8,128)}, f32[8,32,128]{2,1,0:T(8,128)}) custom-call(s32[3]{0:T(128)} %anchor_hbm.1, f32[8,512]{1,0:T(8,128)} %constant.10.clone.lamr_hbm, f32[512,128]{1,0:T(8,128)} %constant.11.clone.lamc_hbm, f32[8,128]{1,0:T(8,128)} %constant.12.clone.lamq_hbm, f32[32,16,512]{2,1,0:T(8,128)} %x_hbm.1, f32[8,32,128]{2,1,0:T(8,128)} %fd_hbm.1, ...), custom_call_target="tpu_custom_call" | custom-call | tf_op jit(solution)/shard_map/pallas_call | solution.py:795
  102.1 0.0 copy-start
  102.2 2.3 %copy.13 = f32[32,16,512]{2,1,0:T(8,128)} copy(f32[32,16,512]{2,1,0:T(8,128)} %get-tuple-element.4) | data formatting | bytes 2097152
  104.5 0.0 copy-done
  104.5 0.7 copy.14
Async XLA Ops:
  102.1 2.4 %copy-start = (f32[8,32,128]{2,1,0:T(8,128)S(1)}, f32[8,32,128]{2,1,0:T(8,128)}, u32[]{:S(2)}) copy-start(f32[8,32,128]{2,1,0:T(8,128)} %get-tuple-element.5) | copy-start | bytes 393220

commit v6 on v5

--- a/solution.py
+++ b/solution.py
@@ -110,9 +110,9 @@
     anchor_hbm, lamr_hbm, lamc_hbm, lamq_hbm, x_hbm, fd_hbm, fs_hbm, sh_hbm, sl_hbm, out_ref, fine_ref,
     anchor, lamr_ref, lamc_ref, lamq_ref, x_ref, fd_ref, fs_ref, sh_ref, sl_ref,
     za, zb, dd, gg, u, dtab, m1, r1, m2, r2, dint, rint, uh, ul, myh, myl, mz, wall, wys,
-    mzx, rzx, my, ry, m5, r5, m6, r6, es, et, ed, fa, fb, fr, trace, tin, gz, ya, yb, yd,
+    mzx, rzx, my, ry, m5, r5, m6, r6, m7, r7, es, et, ed, fa, fb, fr, trace, tin, gz, ya, yb, yd,
     s1, q1, s2, q2, s3, q3, s4, q4, sh1, qh1, sd, qd, sz, qz, sy, qy, s5, q5, s6, q6, sin,
-    st, qt, se, qe, sv, qv,
+    st, qt, se, qe, sv, qv, sx, qx, s7, q7,
 ):
     core = lax.axis_index("grp")
     gx = lax.axis_index("gx")
@@ -179,6 +179,9 @@
 
     has_y = (gy > 0, gy < 15)
     has_x = (gx > 0, gx < 15)
+    middle = (gy == 7) | (gy == 8)
+    turns = ((gy > 0) & (gy != 8), (gy < 15) & (gy != 7))
+    corner = pl.ds(pl.multiple_of((8 - gy) % 8 * 40, 8), 8)
 
     def prepare(src, dst, send_sem, recv_sem, target):
         return pltpu.make_async_remote_copy(
@@ -463,6 +466,16 @@
             pl.when(has_x[side])(copy.start)
             tt.append((copy, has_x[side]))
 
+    def send_corners():
+        for side, ox in enumerate((-1, 1)):
+            copy = prepare(
+                trace.at[side, :, corner, own], tin.at[1 - side, :, corner, own], sx.at[side],
+                qx.at[1 - side], beside(ox, 0),
+            )
+            sent = has_x[side] & middle
+            pl.when(sent)(copy.start)
+            tt.append((copy, sent))
+
     for s in range(32):
         arrived(dd.at[0], q1.at[0], s)
     second_and_eliminate(0)
@@ -472,6 +485,7 @@
     send_ends()
     send_traces(0)
     send_traces(1)
+    send_corners()
     for k in range(1, 16):
         arrived(r1, q2, (pv + k) % 16)
     separators()
@@ -489,9 +503,19 @@
             )
             pl.when(has_x[side])(copy.wait_recv)
     for side in range(2):
+        copy = prepare(
+            tin.at[side, :, corner, own], tin.at[side, :, corner, own], sx.at[side], qx.at[side],
+            here,
+        )
+        pl.when(has_x[side] & middle)(copy.wait_recv)
+
         @pl.when(jnp.logical_not(has_x[side]))
         def _():
             tin[side, :, 8:40, own] = jnp.zeros((8, 32, 128), F32)
+
+        @pl.when(jnp.logical_not(has_x[side]) & middle)
+        def _():
+            tin[side, :, corner, own] = jnp.zeros((8, 8, 128), F32)
 
         @pl.when(jnp.logical_not(has_y[side]))
         def _():
@@ -503,8 +527,8 @@
         copy = prepare(
             tin.at[:, :, rows, own], tin.at[:, :, to_rows, own], sv.at[k], qv.at[k], beside(0, oy)
         )
-        pl.when(has_y[k])(copy.start)
-        tt.append((copy, has_y[k]))
+        pl.when(turns[k])(copy.start)
+        tt.append((copy, turns[k]))
     substitute(1)
     face = []
     cut_x = []
@@ -553,7 +577,7 @@
             src_ref=view, dst_ref=view, send_sem=sv.at[k], recv_sem=qv.at[k], device_id=here,
             device_id_type=MESH,
         )
-        pl.when(has_y[1 - k])(copy.wait_recv)
+        pl.when(turns[1 - k])(copy.wait_recv)
     view = tin.at[:, :, :, own]
     te = send(view, view, se.at[0], qe.at[0], partner)
     te.wait_recv()
@@ -590,16 +614,41 @@
     zsum = rzx[0]
     for s in range(1, 32):
         zsum = zsum + rzx[s]
+    row = lax.broadcasted_iota(jnp.int32, (128, 512), 0)
+    col = lax.broadcasted_iota(jnp.int32, (128, 512), 1)
+    tile = jnp.where(row == col // 128 * 16 + col % 16, 1.0, 0.0)
+    spread_z = full(zsum, tile, NN)
+    spread_z = jnp.concatenate([spread_z[:, 128 * h : 128 * h + 128] for h in range(4)], axis=0)
+    lane32 = lax.broadcasted_iota(jnp.int32, (32, 128), 1) // 16
+    spread_z = jnp.concatenate(
+        [jnp.where(lane32 == k, spread_z, 0.0) for k in range(8)], axis=0
+    )
+    row = lax.broadcasted_iota(jnp.int32, (16, 256), 0)
+    col = lax.broadcasted_iota(jnp.int32, (16, 256), 1)
+    pick = jnp.where(a0 - 3 + 2 * row + col // 32 == 32 * gx + col % 32, 1.0, 0.0)
+    rows = full(pick, spread_z, NN)
+    for q in range(16):
+        m5[q] = rows[q : q + 1]
+    t5 = []
+    for k in range(1, 16):
+        q = (gx + k) % 16
+        t5.append(send(m5.at[q], r5.at[gx], s5.at[k], q5.at[gx], real_row(q)))
+    r5[gx] = m5[gx]
     got = rzx[...].reshape(256, 128)
     parts = [full(got, mz[256 * k : 256 * k + 256, :], TN) for k in range(2)]
+    left_half = lax.broadcasted_iota(jnp.int32, (8, 128), 1) < 64
     for f in range(2):
-        m6[f] = parts[0][64 + 32 * f : 80 + 32 * f] + parts[1][80 + 32 * f : 96 + 32 * f]
-    row = lax.broadcasted_iota(jnp.int32, (128, 32), 0)
-    col = lax.broadcasted_iota(jnp.int32, (128, 32), 1)
-    pick = jnp.where(a0 - 3 + 2 * (row // 8) + row % 8 == 32 * gx + col, 1.0, 0.0)
-    spread_z = jnp.concatenate([jnp.where(lane == h, zsum, 0.0) for h in range(4)], axis=0)
-    m5[:, 0] = full(pick, spread_z, NN).reshape(16, 8, 128)
-    m5[:, 1] = jnp.zeros((16, 8, 128), F32)
+        cells_x = parts[0][64 + 32 * f : 80 + 32 * f] + parts[1][80 + 32 * f : 96 + 32 * f]
+        m6[f] = jnp.where(left_half, cells_x[:8], pltpu.roll(cells_x[8:], 64, 1))
+    for f in range(2):
+        end = 15 * f
+        copy = prepare(m6.at[f], r6.at[gx], s6.at[f], q6.at[gx], real_row(end))
+        pl.when(gx != end)(copy.start)
+
+        @pl.when(gx == end)
+        def _():
+            r6[gx] = m6[f]
+
     at_y = (gy == 0) | (gy == 15)
 
     @pl.when(at_y)
@@ -622,33 +671,14 @@
                 w = full(v, modes, TN)
                 total = w if total is None else total + w
             part.append(full(gather, total, NN))
-        m5[:, 1] = full(pick, jnp.concatenate(part, axis=0), NN).reshape(16, 8, 128)
-
-    t5 = []
-    for k in range(1, 16):
-        q = (gx + k) % 16
-        copy = pltpu.make_async_remote_copy(
-            src_ref=m5.at[q], dst_ref=r5.at[gx], send_sem=s5.at[k], recv_sem=q5.at[gx],
-            device_id=real_row(q), device_id_type=MESH,
-        )
-        copy.start()
-        t5.append(copy)
-    r5[gx] = m5[gx]
-    for f in range(2):
-        end = 15 * f
-        copy = pltpu.make_async_remote_copy(
-            src_ref=m6.at[f], dst_ref=r6.at[gx], send_sem=s6.at[f], recv_sem=q6.at[gx],
-            device_id=real_row(end), device_id_type=MESH,
-        )
-
-        @pl.when(gx != end)
-        def _():
-            copy.start()
-
-        @pl.when(gx == end)
-        def _():
-            r6[gx] = m6[f]
-
+        row = lax.broadcasted_iota(jnp.int32, (128, 32), 0)
+        col = lax.broadcasted_iota(jnp.int32, (128, 32), 1)
+        pick = jnp.where(a0 - 3 + 2 * (row // 8) + row % 8 == 32 * gx + col, 1.0, 0.0)
+        m7[...] = full(pick, jnp.concatenate(part, axis=0), NN).reshape(16, 8, 128)
+        for k in range(1, 16):
+            q = (gx + k) % 16
+            send(m7.at[q], r7.at[gx], s7.at[k], q7.at[gx], real_row(q))
+        r7[gx] = m7[gx]
 
     send_last(1, CUT4B, 32)
     for s in range(32):
@@ -659,9 +689,6 @@
         return dot3(split(za[:, :, halves[h]].reshape(512, 256)), rows_h, NN).reshape(32, 16, 512)
 
     out_ref[...] = inverse_third(0)
-    for s in range(32):
-        arrived(gg.at[1], q4.at[1], s)
-    out_ref[...] = out_ref[...] + inverse_third(1)
     for k in range(1, 16):
         arrived(r5, q5, (gx + k) % 16)
     def interpolate(fine, cell):
@@ -676,12 +703,12 @@
     row, col = grid((24, 8))
     int_x = interpolate(row, col)
     row, col = grid((128, 128))
-    int_y = jnp.where((col < 64) & (row < 48), interpolate(row, col % 16), 0.0)
-    zb5 = r5[0, 0]
-    yb5 = r5[0, 1]
+    int_y = jnp.where(row < 48, interpolate(row, col % 16), 0.0)
+    zb5 = r5[0]
     for s in range(1, 16):
-        zb5 = zb5 + r5[s, 0]
-        yb5 = yb5 + r5[s, 1]
+        zb5 = zb5 + r5[s]
+    row, col = grid((8, 128))
+    zb5 = jnp.where(row == col // 16, jnp.broadcast_to(zb5, (8, 128)), 0.0)
     ghost_z = full(full(int_x, zb5, NN), int_y, NT)
     row, col = grid((24, 128))
     inside = (row + 8 * gx >= 8) & (row + 8 * gx < 136) & (col < 48)
@@ -711,12 +738,20 @@
     row, col = grid((128, 256))
     int_z = jnp.where(row < 64, interpolate(col, row + 30 * core), 0.0)
 
+    for s in range(32):
+        arrived(gg.at[1], q4.at[1], s)
+    out_ref[...] = out_ref[...] + inverse_third(1)
     row8 = lax.broadcasted_iota(jnp.int32, (8, 256), 0)
     col8 = lax.broadcasted_iota(jnp.int32, (8, 256), 1)
     for f in range(2):
         @pl.when(gy == 15 * f)
         def _():
-            ghost_y = full(full(int_x, yb5, NN), int_z, NN)
+            for k in range(1, 16):
+                arrived(r7, q7, (gx + k) % 16)
+            yb7 = r7[0]
+            for k in range(1, 16):
+                yb7 = yb7 + r7[k]
+            ghost_y = full(full(int_x, yb7, NN), int_z, NN)
             edge = 7 * f
             for k in range(24):
                 yd[k] = jnp.where(row8 == edge, ghost_y[k : k + 1], 0.0)
@@ -751,9 +786,11 @@
             xb6 = r6[0]
             for s in range(1, 16):
                 xb6 = xb6 + r6[s]
-            row, col = grid((48, 16))
-            near_y = interpolate(row, col)
-            ghost_x = full(full(near_y, xb6, NN), int_z, NN)
+            row, col = grid((48, 8))
+            near_y = full(interpolate(row, col), xb6, NN)
+            far_y = full(interpolate(row, col + 8), xb6, NN)
+            row, col = grid((48, 128))
+            ghost_x = full(jnp.where(col < 64, near_y + pltpu.roll(far_y, 64, 1), 0.0), int_z, NN)
             for k in range(1, 9):
                 fr[k] = jnp.zeros((48, 256), F32)
                 fa[k] = jnp.zeros((48, 256), F32)
@@ -771,6 +808,11 @@
         copy.wait_send()
     for copy, sent, *_ in halo + tt:
         pl.when(sent)(copy.wait_send)
+    @pl.when(at_y)
+    def _():
+        for k in range(1, 16):
+            prepare(m7.at[k], r7.at[gx], s7.at[k], q7.at[gx], here).wait_send()
+
     for f in range(2):
         @pl.when(gx != 15 * f)
         def _():
@@ -809,7 +851,8 @@
             b16(2, 256, 512), b16(2, 256, 512), b16(512, 256), b16(512, 256),
             f32(512, 128), f32(2, 80, 256), f32(16, 512),
             f32(32, 8, 128), f32(32, 8, 128), f32(2, 4, 128), f32(32, 4, 128),
-            f32(16, 2, 8, 128), f32(16, 2, 8, 128), f32(2, 16, 128), f32(16, 16, 128),
+            f32(16, 1, 128), f32(16, 1, 128), f32(2, 8, 128), f32(16, 8, 128),
+            f32(16, 8, 128), f32(16, 8, 128),
             f32(24, 48, 256), f32(24, 48, 256), f32(24, 48, 256),
             f32(10, 48, 256), f32(10, 48, 256), f32(10, 48, 256),
             f32(2, 8, 48, 256), f32(2, 8, 48, 256), f32(192, 128),
@@ -818,6 +861,7 @@
             dma((2, 32)), dma((2, 32)), dma((4,)), dma((4,)), dma((2,)), dma((2,)),
             dma((32,)), dma((32,)), dma((4,)), dma((32,)), dma((16,)), dma((16,)),
             dma((2,)), dma((16,)), dma((10,)), dma((2, 2)), dma((2, 2)), dma((1,)), dma((1,)), dma((2,)), dma((2,)),
+            dma((2,)), dma((2,)), dma((16,)), dma((16,)),
         ],
         compiler_params=pltpu.CompilerParams(
             collective_id=0, has_side_effects=True, vmem_limit_bytes=56 << 20

time: 105 us -> 101 us (0.962)
  Pallas kernels: 102 us -> 97.7 us
    pallas_call x1, Pallas kernels: 102 us -> 97.7 us  [body(): pl.pallas_call(kernel, out_shape=(jax.ShapeDtypeStruct((32, 16, 512), F32...]
where the time goes in v6:
time: 101 us
  Pallas kernels  97.7 us (97%)
  local copies, waits for them, and re-layouts  3 us (3%)
    pallas_call x1, Pallas kernels, body(): pl.pallas_call(kernel, out_shape=(jax.ShapeDtypeStruct((32, 16, 512), F32...  97.7 us
    unnamed x4, local copies, waits for them, and re-layouts  3 us

profile of v6, /device:TPU:1, one launch (start us, length us, event | category | flops | bytes accessed | tf_op | source)
XLA Modules:
  0.0 101.3 jit_solution(17605189458458137228)
XLA Ops:
  0.6 97.7 %shard_map.104 = (f32[32,16,512]{2,1,0:T(8,128)}, f32[8,32,128]{2,1,0:T(8,128)}) custom-call(s32[3]{0:T(128)} %anchor_hbm.1, f32[8,512]{1,0:T(8,128)} %constant.10.clone.lamr_hbm, f32[512,128]{1,0:T(8,128)} %constant.11.clone.lamc_hbm, f32[8,128]{1,0:T(8,128)} %constant.12.clone.lamq_hbm, f32[32,16,512]{2,1,0:T(8,128)} %x_hbm.1, f32[8,32,128]{2,1,0:T(8,128)} %fd_hbm.1, ...), custom_call_target="tpu_custom_call" | custom-call | tf_op jit(solution)/shard_map/pallas_call | solution.py:837
  98.3 0.0 copy-start
  98.3 2.3 %copy.13 = f32[32,16,512]{2,1,0:T(8,128)} copy(f32[32,16,512]{2,1,0:T(8,128)} %get-tuple-element.4) | data formatting | bytes 2097152
  100.6 0.0 copy-done
  100.6 0.7 copy.14
Async XLA Ops:
  98.3 2.4 %copy-start = (f32[8,32,128]{2,1,0:T(8,128)S(1)}, f32[8,32,128]{2,1,0:T(8,128)}, u32[]{:S(2)}) copy-start(f32[8,32,128]{2,1,0:T(8,128)} %get-tuple-element.5) | copy-start | bytes 393220

commit v7 on v6

--- a/solution.py
+++ b/solution.py
@@ -104,6 +104,8 @@
     (dy, side, core) for dy in (4, 3, 5, 2, 6, 1, 7, 0) for side in (0, 1) for core in (0, 1)
 ]
 PEERS = [ORDER[i] for i in np.random.RandomState(3).permutation(32)]
+SIDES = [[o for o in PEERS if o[1] == side] for side in (0, 1)]
+PEERS = [o for both in zip(*SIDES) for o in both]
 
 
 def kernel(
@@ -837,7 +839,7 @@
     return pl.pallas_call(
         kernel,
         out_shape=(
-            jax.ShapeDtypeStruct((32, 16, 512), F32), jax.ShapeDtypeStruct((8, 32, 128), F32)
+            pltpu.VMEM((32, 16, 512), F32), pltpu.VMEM((8, 32, 128), F32)
         ),
         in_specs=[pl.BlockSpec(memory_space=pl.ANY)] * 9,
         out_specs=(vm, vm),

time: 101 us -> 99.5 us (0.985)
  local copies, waits for them, and re-layouts: 3 us -> 1.63 us
    unnamed x4 -> x2, local copies, waits for them, and re-layouts: 3 us -> 1.63 us
where the time goes in v7:
time: 99.5 us; the launch traced here: 99.4 us
  Pallas kernels  97.1 us (98%)
  local copies, waits for them, and re-layouts  1.63 us (2%)
    pallas_call x1, Pallas kernels, body(): pl.pallas_call(kernel, out_shape=(pltpu.VMEM((32, 16, 512), F32), pltpu.V...  97.1 us

profile of v7, /device:TPU:1, one launch (start us, length us, event | category | flops | bytes accessed | tf_op | source)
XLA Modules:
  0.0 99.4 jit_solution(2899376712644158168)
XLA Ops:
  0.6 97.1 %shard_map.104 = (f32[32,16,512]{2,1,0:T(8,128)S(1)}, f32[8,32,128]{2,1,0:T(8,128)S(1)}) custom-call(s32[3]{0:T(128)} %anchor_hbm.1, f32[8,512]{1,0:T(8,128)} %constant.10.clone.lamr_hbm, f32[512,128]{1,0:T(8,128)} %constant.11.clone.lamc_hbm, f32[8,128]{1,0:T(8,128)} %constant.12.clone.lamq_hbm, f32[32,16,512]{2,1,0:T(8,128)} %x_hbm.1, ...), custom_call_target="tpu_custom_call" | custom-call | tf_op jit(solution)/shard_map/pallas_call | solution.py:839
  97.7 1.0 copy.13
  98.7 0.7 copy.14

commit v8 on v7

--- a/solution.py
+++ b/solution.py
@@ -183,7 +183,7 @@
     has_x = (gx > 0, gx < 15)
     middle = (gy == 7) | (gy == 8)
     turns = ((gy > 0) & (gy != 8), (gy < 15) & (gy != 7))
-    corner = pl.ds(pl.multiple_of((8 - gy) % 8 * 40, 8), 8)
+    corner = pl.ds(pl.multiple_of((15 - gy) // 8 * 40, 8), 8)
 
     def prepare(src, dst, send_sem, recv_sem, target):
         return pltpu.make_async_remote_copy(
@@ -492,9 +492,6 @@
         arrived(r1, q2, (pv + k) % 16)
     separators()
     wait_separators()
-    substitute(0)
-    inverse_second(0)
-    send_last(0, 0, CUT4A)
     for part in range(2):
         sweeps = pl.ds(4 * part, 4)
         for side in range(2):
@@ -531,6 +528,9 @@
         )
         pl.when(turns[k])(copy.start)
         tt.append((copy, turns[k]))
+    substitute(0)
+    inverse_second(0)
+    send_last(0, 0, CUT4A)
     substitute(1)
     face = []
     cut_x = []
@@ -740,6 +740,23 @@
     row, col = grid((128, 256))
     int_z = jnp.where(row < 64, interpolate(col, row + 30 * core), 0.0)
 
+    for copy in t2 + t4[0] + t4[1] + tz + t5 + [te]:
+        copy.wait_send()
+    for copy, sent, *_ in halo + tt:
+        pl.when(sent)(copy.wait_send)
+    @pl.when(at_y)
+    def _():
+        for k in range(1, 16):
+            prepare(m7.at[k], r7.at[gx], s7.at[k], q7.at[gx], here).wait_send()
+
+    for f in range(2):
+        @pl.when(gx != 15 * f)
+        def _():
+            pltpu.make_async_remote_copy(
+                src_ref=m6.at[f], dst_ref=r6.at[gx], send_sem=s6.at[f], recv_sem=q6.at[gx],
+                device_id=real_row(15 * f), device_id_type=MESH,
+            ).wait_send()
+
     for s in range(32):
         arrived(gg.at[1], q4.at[1], s)
     out_ref[...] = out_ref[...] + inverse_third(1)
@@ -805,23 +822,6 @@
                     target[index] = layer(source, fr, index) * sixth
             for k in range(8):
                 fine_ref[k] = fine_ref[k] + fa[k + 1, 8:40, own]
-
-    for copy in t2 + t4[0] + t4[1] + tz + t5 + [te]:
-        copy.wait_send()
-    for copy, sent, *_ in halo + tt:
-        pl.when(sent)(copy.wait_send)
-    @pl.when(at_y)
-    def _():
-        for k in range(1, 16):
-            prepare(m7.at[k], r7.at[gx], s7.at[k], q7.at[gx], here).wait_send()
-
-    for f in range(2):
-        @pl.when(gx != 15 * f)
-        def _():
-            pltpu.make_async_remote_copy(
-                src_ref=m6.at[f], dst_ref=r6.at[gx], send_sem=s6.at[f], recv_sem=q6.at[gx],
-                device_id=real_row(15 * f), device_id_type=MESH,
-            ).wait_send()
 
 
 def body(density, fine_density, fine_start, anchor):

time: 99.5 us -> 98.7 us (level)
  no operation moved by 1% of the time
where the time goes in v8:
time: 98.7 us; the launch traced here: 98.5 us
  Pallas kernels  96.3 us (98%)
  local copies, waits for them, and re-layouts  1.63 us (2%)
    pallas_call x1, Pallas kernels, body(): pl.pallas_call(kernel, out_shape=(pltpu.VMEM((32, 16, 512), F32), pltpu.V...  96.3 us

profile of v8, /device:TPU:1, one launch (start us, length us, event | category | flops | bytes accessed | tf_op | source)
XLA Modules:
  0.0 98.5 jit_solution(1717888771453438069)
XLA Ops:
  0.6 96.3 %shard_map.104 = (f32[32,16,512]{2,1,0:T(8,128)S(1)}, f32[8,32,128]{2,1,0:T(8,128)S(1)}) custom-call(s32[3]{0:T(128)} %anchor_hbm.1, f32[8,512]{1,0:T(8,128)} %constant.10.clone.lamr_hbm, f32[512,128]{1,0:T(8,128)} %constant.11.clone.lamc_hbm, f32[8,128]{1,0:T(8,128)} %constant.12.clone.lamq_hbm, f32[32,16,512]{2,1,0:T(8,128)} %x_hbm.1, ...), custom_call_target="tpu_custom_call" | custom-call | tf_op jit(solution)/shard_map/pallas_call | solution.py:839
  96.9 1.0 copy.13
  97.9 0.7 copy.14

commit v9 on v8

--- a/solution.py
+++ b/solution.py
@@ -824,6 +824,17 @@
                 fine_ref[k] = fine_ref[k] + fa[k + 1, 8:40, own]
 
 
+def store(potential, fine, potential_out, fine_out, sem):
+    copies = [
+        pltpu.make_async_copy(potential, potential_out, sem.at[0]),
+        pltpu.make_async_copy(fine, fine_out, sem.at[1]),
+    ]
+    for copy in copies:
+        copy.start()
+    for copy in copies:
+        copy.wait()
+
+
 def body(density, fine_density, fine_start, anchor):
     high, low, lam = tables()
     vm = pl.BlockSpec(memory_space=pltpu.VMEM)
@@ -836,7 +847,7 @@
         return pltpu.VMEM(shape, BF16)
 
     big = f32(32, 16, 512)
-    return pl.pallas_call(
+    results = pl.pallas_call(
         kernel,
         out_shape=(
             pltpu.VMEM((32, 16, 512), F32), pltpu.VMEM((8, 32, 128), F32)
@@ -872,6 +883,16 @@
       jnp.asarray(np.tile(lam.reshape(512, 1), (1, 128))),
       jnp.asarray(np.tile(lam.reshape(4, 128), (2, 1))), density, fine_density, fine_start,
       jnp.asarray(high), jnp.asarray(low))
+    return pl.pallas_call(
+        store,
+        out_shape=(
+            jax.ShapeDtypeStruct((32, 16, 512), F32), jax.ShapeDtypeStruct((8, 32, 128), F32)
+        ),
+        in_specs=[vm] * 2,
+        out_specs=(pl.BlockSpec(memory_space=pl.ANY),) * 2,
+        scratch_shapes=[dma((2,))],
+        compiler_params=pltpu.CompilerParams(vmem_limit_bytes=4 << 20),
+    )(*results)
 
 
 def solution(mesh):

time: 98.7 us -> 98.2 us (level)
  local copies, waits for them, and re-layouts: 1.63 us -> 0 us
  Pallas kernels: 96.3 us -> 97.3 us
    unnamed x2 -> x0, local copies, waits for them, and re-layouts: 1.63 us -> none
    pallas_call x0 -> x1, Pallas kernels: none -> 1.02 us  [body(): pl.pallas_call(store, out_shape=(jax.ShapeDtypeStruct((32, 16, 512), F32)...]
where the time goes in v9:
time: 98.2 us; the launch traced here: 98.1 us
  Pallas kernels  97.3 us (99%)
    pallas_call x1, Pallas kernels, body(): pl.pallas_call(kernel, out_shape=(pltpu.VMEM((32, 16, 512), F32), pltpu.V...  96.3 us

profile of v9, /device:TPU:1, one launch (start us, length us, event | category | flops | bytes accessed | tf_op | source)
XLA Modules:
  0.0 98.1 jit_solution(17993788620671461494)
XLA Ops:
  0.6 96.3 %shard_map.104 = (f32[32,16,512]{2,1,0:T(8,128)S(1)}, f32[8,32,128]{2,1,0:T(8,128)S(1)}) custom-call(s32[3]{0:T(128)} %anchor_hbm.1, f32[8,512]{1,0:T(8,128)} %constant.10.clone.lamr_hbm, f32[512,128]{1,0:T(8,128)} %constant.11.clone.lamc_hbm, f32[8,128]{1,0:T(8,128)} %constant.12.clone.lamq_hbm, f32[32,16,512]{2,1,0:T(8,128)} %x_hbm.1, ...), custom_call_target="tpu_custom_call" | custom-call | tf_op jit(solution)/shard_map/pallas_call | solution.py:850
  96.9 1.0 %shard_map.105 = (f32[32,16,512]{2,1,0:T(8,128)}, f32[8,32,128]{2,1,0:T(8,128)}) custom-call(f32[32,16,512]{2,1,0:T(8,128)S(1)} %get-tuple-element.4.potential, f32[8,32,128]{2,1,0:T(8,128)S(1)} %get-tuple-element.5.fine), custom_call_target="tpu_custom_call" | custom-call | tf_op jit(solution)/shard_map/pallas_call | solution.py:886
